TPU v7x, 256 devices: a whole 4x4x8 slice. The times are simulated.
256 devices in a mesh: rows: 8 (over y_hi, x), cols: 32 (over y_lo, z, core).
Axes of the slice: x: 4, y: 4 (y_hi: 2, y_lo: 2; y = y_hi * 2 + y_lo), z: 8, core: 2. Of those that a mesh axis runs over, the one named last changes fastest.
Arguments:
- embeddings: bfloat16 [65536, 768], P(('rows', 'cols')), may hold values from -6 to 6
- document_cluster_index: int32 [65536], P(('rows', 'cols')), may hold values from 0 to 127, as said below
Outputs:
- max_similarity: float32 [65536], P(('rows', 'cols'))
- histogram: float32 [128], replicated
Inputs may be any that keep to these rules, and one draw needn't show every extreme that they name: `document_cluster_index`: cluster r * 16 to (r + 1) * 16 - 1 form row group r. Each device's block of 256 documents names at most 64 documents of any one row group, and exactly 64 of one. The documents that the devices with one index along cols name for one row group hold at most 64 documents of any one cluster, and in every draw some such set holds exactly 64 of one cluster.
All inputs are finite; a program needn't handle non-finite values.
Results may differ from a plain program's by a relative error of at most 0.0014.
Values may be sent and summed in bfloat16 or wider, within the bound.
No kernel may reach another device: no remote copies, remote signals or barrier semaphores. Data moves between devices by JAX's collectives and lax.ppermute only.
A program may use at most 64 MiB of HBM per device.

v0:
```python
import jax
import jax.numpy as jnp
from jax import lax
from jax.sharding import Mesh
from jax.sharding import PartitionSpec as P

CAP = 64
GROUP_CLUSTERS = 16
BINS = 128
ROWS = ("rows_0", "rows_1")
COLS = ("cols_0", "cols_1", "cols_2")
ROWS_COLS = ("rows_0", "rows_1", "cols_0", "cols_1", "cols_2")


def in_one_piece(arrays, axis, split_dim, concat_dim, along):
    columns = [a.reshape(*a.shape[:along], -1) for a in arrays]
    both = jnp.concatenate(columns, axis=along)
    result, at, finished = (
        lax.all_to_all(both, axis, split_axis=split_dim, concat_axis=concat_dim, tiled=True),
        0,
        [],
    )
    for a, column in zip(arrays, columns):
        piece = result[..., at : at + column.shape[along]]
        finished.append(piece.reshape(*piece.shape[:along], *a.shape[along:]))
        at += column.shape[along]
    return tuple(finished)


def from_partner(value, axis, bit):
    mask = 2**bit
    pairs = [(source, source ^ mask) for source in range(lax.axis_size(axis))]
    return lax.ppermute(value, axis, pairs)


def one_axis_at_a_time(x, axes):
    for axis in axes:
        x = lax.psum(x, axis)
    return x


def shards(embeddings, document_cluster_index):
    row_count = lax.axis_size(ROWS)
    col_count = lax.axis_size(COLS)
    doc_count = embeddings.shape[0]
    width = embeddings.shape[1]
    slot_count = CAP * row_count
    values = embeddings.astype(jnp.float32)
    normed = (values * lax.rsqrt(jnp.sum(values * values, axis=1, keepdims=True) + 1e-06)).astype(
        jnp.bfloat16
    )
    owner_devices = document_cluster_index // GROUP_CLUSTERS
    within_cluster = (document_cluster_index % GROUP_CLUSTERS).astype(jnp.float32)
    onehot_rows = (
        owner_devices[:, None] == jnp.arange(row_count, dtype=jnp.int32)[None, :]
    ).astype(jnp.int32)
    slot_ranks = jnp.sum((jnp.cumsum(onehot_rows, axis=0) - 1) * onehot_rows, axis=1)
    places = owner_devices * CAP + slot_ranks
    outgoing = jnp.zeros((slot_count, width), jnp.bfloat16).at[places].set(normed)
    out_labels = (
        jnp.full((slot_count,), -1.0, jnp.float32)
        .at[places]
        .set(within_cluster)
        .astype(jnp.bfloat16)
    )
    resident, res_labels = (
        lax.all_to_all(outgoing, ROWS, split_axis=0, concat_axis=0, tiled=True),
        lax.all_to_all(out_labels, ROWS, split_axis=0, concat_axis=0, tiled=True),
    )
    home_labels = res_labels.astype(jnp.float32)
    partner_count = max(1, col_count // GROUP_CLUSTERS)
    owned_count = max(1, GROUP_CLUSTERS // col_count)
    slot_quota = 2 * slot_count // GROUP_CLUSTERS // partner_count
    send_total = col_count * owned_count * slot_quota
    local_cluster = res_labels.astype(jnp.int32)
    occupied = local_cluster >= 0
    onehot_clusters = (
        local_cluster[:, None] == jnp.arange(GROUP_CLUSTERS, dtype=jnp.int32)[None, :]
    ).astype(jnp.int32)
    cluster_rank = jnp.sum((jnp.cumsum(onehot_clusters, axis=0) - 1) * onehot_clusters, axis=1)
    member_slot = cluster_rank % partner_count
    cluster_depth = cluster_rank // partner_count
    destination = local_cluster // owned_count * partner_count + member_slot
    send_place = (
        destination * (owned_count * slot_quota)
        + local_cluster % owned_count * slot_quota
        + cluster_depth
    )
    send_place = jnp.where(occupied, send_place, send_total)
    send_rows = (
        jnp.zeros((send_total, width), jnp.bfloat16).at[send_place].set(resident, mode="drop")
    )
    send_labels = (
        jnp.full((send_total,), -1.0, jnp.float32)
        .at[send_place]
        .set(home_labels, mode="drop")
        .astype(jnp.bfloat16)
    )
    got_rows, got_labels = in_one_piece((send_rows, send_labels), COLS, 0, 0, 1)
    member_index = lax.axis_index(COLS) % partner_count
    gathered_rows, gathered_labels = (got_rows, got_labels)
    other_rows, other_labels = from_partner((gathered_rows, gathered_labels), COLS, 0)
    upper = member_index // 2**0 % 2 == 1
    gathered_rows = jnp.where(
        upper,
        jnp.concatenate([other_rows, gathered_rows], axis=0),
        jnp.concatenate([gathered_rows, other_rows], axis=0),
    )
    gathered_labels = jnp.where(
        upper,
        jnp.concatenate([other_labels, gathered_labels], axis=0),
        jnp.concatenate([gathered_labels, other_labels], axis=0),
    )
    similarity_scores = lax.dot_general(
        got_rows, gathered_rows, (((1,), (1,)), ((), ())), preferred_element_type=jnp.float32
    )
    own_labels = got_labels.astype(jnp.float32)
    all_labels = gathered_labels.astype(jnp.float32)
    column_index = jnp.arange(gathered_rows.shape[0], dtype=jnp.int32)
    own_index = member_index * send_total + jnp.arange(send_total, dtype=jnp.int32)
    same_cluster = (own_labels[:, None] == all_labels[None, :]) & (own_labels[:, None] >= 0.0)
    same_cluster = same_cluster & (own_index[:, None] != column_index[None, :])
    best_owned = jnp.max(jnp.where(same_cluster, similarity_scores, -1.0), axis=1)
    came_back = lax.all_to_all(best_owned, COLS, split_axis=0, concat_axis=0, tiled=True)
    row_best = jnp.where(occupied, came_back[jnp.minimum(send_place, send_total - 1)], -1.0)
    answers = lax.all_to_all(row_best, ROWS, split_axis=0, concat_axis=0, tiled=True)
    max_similarity = answers[places]
    bin_width = 2.0 / (BINS - 1)
    centers = -1.0 + jnp.arange(BINS, dtype=jnp.float32) * bin_width
    bin_weights = jax.nn.relu(1.0 - jnp.abs(max_similarity[:, None] - centers[None, :]) / bin_width)
    bin_totals = one_axis_at_a_time(jnp.sum(bin_weights, axis=0), ROWS_COLS)
    return (max_similarity, bin_totals / (doc_count * row_count * col_count))


def solution(mesh):
    torus = Mesh(
        mesh.devices.reshape(2, 4, 2, 8, 2), ("rows_0", "rows_1", "cols_0", "cols_1", "cols_2")
    )
    in_specs = (P(ROWS_COLS, None), P(ROWS_COLS))
    out_specs = (P(ROWS_COLS), P())
    return jax.shard_map(
        shards, mesh=torus, in_specs=in_specs, out_specs=out_specs, check_vma=False
    )
```

profile of v0, /device:TPU:1, one launch (start us, length us, event | category | flops | bytes accessed | tf_op | source)
XLA Modules:
  0.0 174.9 jit_solution(9868133892344737554)
XLA Ops:
  0.6 0.7 fusion.25
  1.3 0.6 reduce-window.14
  2.3 1.4 scatter_custom_fusion
  3.7 0.7 all_to_all.46
  4.4 7.5 %all-to-all-start = ((bf16[8,64,1]{1,2,0:T(2,128)(2,1)}), bf16[8,64,1]{1,2,0:T(2,128)(2,1)S(1)}, u32[]{:S(2)}, u32[]{:S(2)}) async-start(bf16[8,64,1]{1,2,0:T(2,128)(2,1)} %all_to_all.46), calls=%async_computation | async-start | bytes 8192 | tf_op jit(solution)/shard_map/all_to_all | solution.py:68
  11.8 1.2 fusion.7
  13.0 3.1 %scatter_custom_fusion.1 = bf16[512,768]{1,0:T(8,128)(2,1)} fusion(s32[256]{0:T(256)S(1)} %compare_select_fusion.6, bf16[256,768]{1,0:T(8,128)(2,1)} %param.2, f32[256]{0:T(256)S(1)} %add_rsqrt_fusion, bf16[]{:T(256)} %constant.140.clone.1), kind=kCustom, calls=%fused_computation.26 | custom fusion | flops 589824 | bytes 1180674 | tf_op jit(solution)/shard_map/scatter | solution.py:59
  16.1 2.3 %all-to-all-done = bf16[8,64,1]{1,2,0:T(2,128)(2,1)S(1)} async-done(((bf16[8,64,1]{1,2,0:T(2,128)(2,1)}), bf16[8,64,1]{1,2,0:T(2,128)(2,1)S(1)}, u32[]{:S(2)}, u32[]{:S(2)}) %all-to-all-start) | async-done | bytes 1056 | tf_op jit(solution)/shard_map/all_to_all | solution.py:68
  18.4 4.4 %all-to-all-start.1 = ((bf16[8,64,768]{2,1,0:T(8,128)(2,1)}), bf16[8,64,768]{2,1,0:T(8,128)(2,1)S(1)}, u32[]{:S(2)}, u32[]{:S(2)}) async-start(bf16[8,64,768]{2,1,0:T(8,128)(2,1)} %bitcast.6), calls=%async_computation.1 | async-start | bytes 1572864 | tf_op jit(solution)/shard_map/all_to_all | solution.py:67
  22.9 1.1 reduce-window.16
  24.8 2.4 %scatter_custom_fusion.3 = f32[1024]{0:T(1024)S(1)} fusion(s32[512]{0:T(512)S(1)} %bitcast.44, f32[512]{0:T(512)S(1)} %reshape.299, f32[]{:T(128)} %constant.131.clone.1), kind=kCustom, calls=%fused_computation.63 | custom fusion | bytes 4100 | tf_op jit(solution)/shard_map/scatter | solution.py:96
  27.7 9.6 %all-to-all-done.1 = bf16[8,64,768]{2,1,0:T(8,128)(2,1)S(1)} async-done(((bf16[8,64,768]{2,1,0:T(8,128)(2,1)}), bf16[8,64,768]{2,1,0:T(8,128)(2,1)S(1)}, u32[]{:S(2)}, u32[]{:S(2)}) %all-to-all-start.1) | async-done | bytes 786464 | tf_op jit(solution)/shard_map/all_to_all | solution.py:67
  37.3 3.0 %scatter_custom_fusion.2 = bf16[1024,768]{1,0:T(8,128)(2,1)S(1)} fusion(s32[512]{0:T(512)S(1)} %bitcast.45, bf16[512,768]{1,0:T(8,128)(2,1)S(1)} %bitcast.39, bf16[]{:T(256)} %constant.140.clone.1), kind=kCustom, calls=%fused_computation.21 | custom fusion | bytes 1572866 | tf_op jit(solution)/shard_map/scatter | solution.py:91
  40.5 52.9 %all_to_all.52 = bf16[32,32,769]{2,1,0:T(8,128)(2,1)S(1)} all-to-all(bf16[32,32,769]{2,1,0:T(8,128)(2,1)S(1)} %pad_maximum_fusion), channel_id=1, replica_groups=mesh['rows_0'=2,'rows_1'=4,'cols_0'=2,'cols_1'=8,'cols_2'=2] {'cols_0','..., dimensions={0} | all-to-all | bytes 3149824 | tf_op jit(solution)/shard_map/all_to_all | solution.py:19
  93.5 2.7 %collective-permute-start.1 = (bf16[1024,768]{1,0:T(8,128)(2,1)S(1)}, bf16[1024,768]{1,0:T(8,128)(2,1)}, u32[]{:S(2)}, u32[]{:S(2)}) collective-permute-start(bf16[1024,768]{1,0:T(8,128)(2,1)S(1)} %slice.31), channel_id=1, source_target_pairs={{0,1},{1,0},{2,3},{3,2},{4,5},{5,4},{6,7},{7,6},{8,9},{9,8},{10,11... | collective-permute-start | bytes 4718600 | tf_op jit(solution)/shard_map/ppermute | solution.py:33
  97.0 2.3 %collective-permute-done = bf16[1024]{0:T(1024)(128)(2,1)S(1)} collective-permute-done((bf16[1024]{0:T(1024)(128)(2,1)S(1)}, bf16[1024]{0:T(1024)(128)(2,1)S(1)}, u32[]{:S(2)}, u32[]{:S(2)}) %collective-permute-start) | collective-permute-done | bytes 2080 | tf_op jit(solution)/shard_map/ppermute | solution.py:33
  99.3 6.5 %select_reduce_fusion = f32[1024]{0:T(1024)S(1)} fusion(s32[1024]{0:T(1024)S(1)} %iota_add_fusion, f32[2048]{0:T(1024)S(1)} %fusion.21, f32[1024]{0:T(1024)S(1)} %convert_reduce_fusion, pred[1024]{0:T(1024)(128)(4,1)S(1)} %fusion.11, bf16[1024,768]{1,0:T(8,128)(2,1)S(1)} %slice.31, bf16[1024,768]{1,0:T(8,128)(2,1)} %collective-permute-done.1, pred[]{:T(512)S(6)} %eq.85), kind=kOutput, calls=%fused_computation.6 | convolution fusion | flops 3247963136 | bytes 3167233 | tf_op jit(solution)/shard_map/dot_general | solution.py:114
  105.9 0.7 all_to_all.41
  106.6 3.9 %all-to-all-start.3 = ((f32[32,32,1]{1,2,0:T(1,128)}), f32[32,32,1]{1,2,0:T(1,128)S(1)}, u32[]{:S(2)}, u32[]{:S(2)}) async-start(f32[32,32,1]{1,2,0:T(1,128)} %bitcast.10), calls=%async_computation.3 | async-start | bytes 32768 | tf_op jit(solution)/shard_map/all_to_all | solution.py:124
  110.4 8.0 %all-to-all-done.3 = f32[32,32,1]{1,2,0:T(1,128)S(1)} async-done(((f32[32,32,1]{1,2,0:T(1,128)}), f32[32,32,1]{1,2,0:T(1,128)S(1)}, u32[]{:S(2)}, u32[]{:S(2)}) %all-to-all-start.3) | async-done | bytes 4128 | tf_op jit(solution)/shard_map/all_to_all | solution.py:124
  118.9 0.7 reduce.32
  119.7 2.3 %gather_fusion = f32[512]{0:T(512)S(1)} fusion(f32[1024]{0:T(1024)S(1)} %all_to_all.43, s32[1024]{0:T(1024)S(1)} %pad_clamp_fusion.1), kind=kCustom, calls=%fused_computation | custom fusion | bytes 6144 | tf_op jit(solution)/shard_map/gather | solution.py:125
  122.1 0.6 compare_select_fusion.2
  122.7 3.3 %all-to-all-start.4 = ((f32[8,64,1]{1,2,0:T(1,128)}), f32[8,64,1]{1,2,0:T(1,128)S(1)}, u32[]{:S(2)}, u32[]{:S(2)}) async-start(f32[8,64,1]{1,2,0:T(1,128)} %compare_select_fusion.2), calls=%async_computation.4 | async-start | bytes 8192 | tf_op jit(solution)/shard_map/all_to_all | solution.py:126
  126.0 6.5 %all-to-all-done.4 = f32[8,64,1]{1,2,0:T(1,128)S(1)} async-done(((f32[8,64,1]{1,2,0:T(1,128)}), f32[8,64,1]{1,2,0:T(1,128)S(1)}, u32[]{:S(2)}, u32[]{:S(2)}) %all-to-all-start.4) | async-done | bytes 2080 | tf_op jit(solution)/shard_map/all_to_all | solution.py:126
  132.5 0.7 reduce.33
  133.2 1.9 %gather_fusion.1 = f32[256]{0:T(256)S(1)} fusion(f32[512]{0:T(512)S(1)} %all_to_all.45, s32[1024]{0:T(1024)S(1)} %pad_clamp_fusion), kind=kCustom, calls=%fused_computation.1 | custom fusion | bytes 3072 | tf_op jit(solution)/shard_map/gather | solution.py:127
  135.3 5.3 %psum.35 = f32[128]{0:T(128)S(1)} all-reduce(f32[128]{0:T(128)S(1)} %maximum_reduce_fusion), channel_id=1, replica_groups=mesh['rows_0'=2,'rows_1'=4,'cols_0'=2,'cols_1'=8,'cols_2'=2] {'rows_0'}, use_global_device_ids=true, to_apply=%region_13.14 | all-reduce | flops 128 | bytes 1024 | tf_op jit(solution)/shard_map/psum | solution.py:38
  140.6 6.8 %psum.36 = f32[128]{0:T(128)S(1)} all-reduce(f32[128]{0:T(128)S(1)} %psum.35), channel_id=1, replica_groups=mesh['rows_0'=2,'rows_1'=4,'cols_0'=2,'cols_1'=8,'cols_2'=2] {'rows_1'}, use_global_device_ids=true, to_apply=%region_14.15 | all-reduce | flops 128 | bytes 1024 | tf_op jit(solution)/shard_map/psum | solution.py:38
  147.4 3.8 %psum.37 = f32[128]{0:T(128)S(1)} all-reduce(f32[128]{0:T(128)S(1)} %psum.36), channel_id=1, replica_groups=mesh['rows_0'=2,'rows_1'=4,'cols_0'=2,'cols_1'=8,'cols_2'=2] {'cols_0'}, use_global_device_ids=true, to_apply=%region_15.16 | all-reduce | flops 128 | bytes 1024 | tf_op jit(solution)/shard_map/psum | solution.py:38
  151.2 11.3 %psum.38 = f32[128]{0:T(128)S(1)} all-reduce(f32[128]{0:T(128)S(1)} %psum.37), channel_id=1, replica_groups=mesh['rows_0'=2,'rows_1'=4,'cols_0'=2,'cols_1'=8,'cols_2'=2] {'cols_1'}, use_global_device_ids=true, to_apply=%region_16.17 | all-reduce | flops 128 | bytes 1024 | tf_op jit(solution)/shard_map/psum | solution.py:38
  162.5 11.9 %psum.39 = f32[128]{0:T(128)S(1)} all-reduce(f32[128]{0:T(128)S(1)} %psum.38), channel_id=1, replica_groups=mesh['rows_0'=2,'rows_1'=4,'cols_0'=2,'cols_1'=8,'cols_2'=2] {'cols_2'}, use_global_device_ids=true, to_apply=%region_17.18 | all-reduce | flops 128 | bytes 1024 | tf_op jit(solution)/shard_map/psum | solution.py:38
  (46 shorter events, 4.2 us)
Async XLA Ops:
  4.4 14.0 %all-to-all-start = ((bf16[8,64,1]{1,2,0:T(2,128)(2,1)}), bf16[8,64,1]{1,2,0:T(2,128)(2,1)S(1)}, u32[]{:S(2)}, u32[]{:S(2)}) async-start(bf16[8,64,1]{1,2,0:T(2,128)(2,1)} %all_to_all.46), calls=%async_computation | async-start | bytes 8192 | tf_op jit(solution)/shard_map/all_to_all | solution.py:68
  18.4 19.0 %all-to-all-start.1 = ((bf16[8,64,768]{2,1,0:T(8,128)(2,1)}), bf16[8,64,768]{2,1,0:T(8,128)(2,1)S(1)}, u32[]{:S(2)}, u32[]{:S(2)}) async-start(bf16[8,64,768]{2,1,0:T(8,128)(2,1)} %bitcast.6), calls=%async_computation.1 | async-start | bytes 1572864 | tf_op jit(solution)/shard_map/all_to_all | solution.py:67
  93.5 5.9 %collective-permute-start.1 = (bf16[1024,768]{1,0:T(8,128)(2,1)S(1)}, bf16[1024,768]{1,0:T(8,128)(2,1)}, u32[]{:S(2)}, u32[]{:S(2)}) collective-permute-start(bf16[1024,768]{1,0:T(8,128)(2,1)S(1)} %slice.31), channel_id=1, source_target_pairs={{0,1},{1,0},{2,3},{3,2},{4,5},{5,4},{6,7},{7,6},{8,9},{9,8},{10,11... | collective-permute-start | bytes 4718600 | tf_op jit(solution)/shard_map/ppermute | solution.py:33
  96.3 3.0 %collective-permute-start = (bf16[1024]{0:T(1024)(128)(2,1)S(1)}, bf16[1024]{0:T(1024)(128)(2,1)S(1)}, u32[]{:S(2)}, u32[]{:S(2)}) collective-permute-start(bf16[1024]{0:T(1024)(128)(2,1)S(1)} %slice_reduce_fusion), channel_id=1, source_target_pairs={{0,1},{1,0},{2,3},{3,2},{4,5},{5,4},{6,7},{7,6},{8,9},{9,8},{10,11... | collective-permute-start | bytes 6152 | tf_op jit(solution)/shard_map/ppermute | solution.py:33
  106.6 11.9 %all-to-all-start.3 = ((f32[32,32,1]{1,2,0:T(1,128)}), f32[32,32,1]{1,2,0:T(1,128)S(1)}, u32[]{:S(2)}, u32[]{:S(2)}) async-start(f32[32,32,1]{1,2,0:T(1,128)} %bitcast.10), calls=%async_computation.3 | async-start | bytes 32768 | tf_op jit(solution)/shard_map/all_to_all | solution.py:124
  122.7 9.8 %all-to-all-start.4 = ((f32[8,64,1]{1,2,0:T(1,128)}), f32[8,64,1]{1,2,0:T(1,128)S(1)}, u32[]{:S(2)}, u32[]{:S(2)}) async-start(f32[8,64,1]{1,2,0:T(1,128)} %compare_select_fusion.2), calls=%async_computation.4 | async-start | bytes 8192 | tf_op jit(solution)/shard_map/all_to_all | solution.py:126
  135.2 39.7 %copy-start = (f32[256]{0:T(256)}, f32[256]{0:T(256)S(1)}, u32[]{:S(2)}) copy-start(f32[256]{0:T(256)S(1)} %gather_fusion.1) | copy-start | bytes 3076
where the time goes:
time: 175 us
  blocking collectives  92 us (53%)
  waiting for transfers between devices  28.6 us (16%)
  starting transfers between devices  22.1 us (13%)
  local copies, waits for them, and re-layouts  14.7 us (8%)
  other arithmetic  10.2 us (6%)
  matrix products  6.54 us (4%)
    all_to_all x1, blocking collectives, in_one_piece(): lax.all_to_all(both, axis, split_axis=split_dim, concat_axis=concat_dim,...  52.9 us
    psum x5, blocking collectives, one_axis_at_a_time(): x = lax.psum(x, axis)  39.1 us
    all_to_all x1, waiting for transfers between devices, shards(): lax.all_to_all(outgoing, ROWS, split_axis=0, concat_axis=0, tiled=True)  9.61 us
    all_to_all x1, waiting for transfers between devices, shards(): lax.all_to_all(best_owned, COLS, split_axis=0, concat_axis=0, tiled=True)  7.97 us
    all_to_all x1, starting transfers between devices, shards(): lax.all_to_all(out_labels, ROWS, split_axis=0, concat_axis=0, tiled=True)  7.47 us
    dot_general x1, matrix products, shards(): lax.dot_general(got_rows, gathered_rows, (((1,), (1,)), ((), ())), prefer...  6.54 us
    all_to_all x1, waiting for transfers between devices, shards(): lax.all_to_all(row_best, ROWS, split_axis=0, concat_axis=0, tiled=True)  6.45 us
    all_to_all x1, starting transfers between devices, shards(): lax.all_to_all(outgoing, ROWS, split_axis=0, concat_axis=0, tiled=True)  4.39 us
  transfers between devices with their start and end apart: 6, of which 5 were waited for; matrix products, arithmetic and copies ran while one was open for 6% of the time, Pallas kernels for 0%

commit v1 on v0

v1 whole, which is shorter than its diff:
```python
import jax
import jax.numpy as jnp
from jax import lax
from jax.experimental import pallas as pl
from jax.experimental.pallas import tpu as pltpu
from jax.sharding import Mesh
from jax.sharding import PartitionSpec as P

CAP = 64
GROUP_CLUSTERS = 16
BINS = 128
ROWS = ("rows_0", "rows_1")
COLS = ("cols_0", "cols_1", "cols_2")
ALL = ROWS + COLS
META = 8
EMPTY = 2.0
F32 = jnp.float32
BF16 = jnp.bfloat16


def iota(shape, dim):
    return lax.broadcasted_iota(jnp.int32, shape, dim)


def dot(a, b):
    return lax.dot_general(a, b, (((1,), (0,)), ((), ())), preferred_element_type=F32)


def dot_t(a, b):
    return lax.dot_general(a, b, (((1,), (1,)), ((), ())), preferred_element_type=F32)


def ones_where(mask):
    return jnp.where(mask, 1.0, 0.0).astype(BF16)


def before(n):
    return ones_where(iota((n, n), 0) < iota((n, n), 1))


def rank_of(onehot, n):
    earlier = dot(onehot, before(n))
    return jnp.sum(onehot.astype(F32) * earlier, axis=0, keepdims=True)


def normalise_and_slot(labels_ref, embeddings_ref, out_ref, rank_ref):
    docs, width = embeddings_ref.shape
    groups = out_ref.shape[0]
    clusters = groups * GROUP_CLUSTERS
    labels = labels_ref[...]
    group = lax.shift_right_logical(labels, 4)
    onehot = ones_where(iota((groups, docs), 0) == group)
    slot = group * CAP + rank_of(onehot, docs).astype(jnp.int32)
    places = ones_where(iota((groups * CAP, docs), 0) == slot)
    values = embeddings_ref[...].astype(F32)
    total = jnp.sum(values * values, axis=1, keepdims=True)
    normed = (values * lax.rsqrt(total + 1e-06)).astype(BF16)
    rows = dot(places, normed).astype(BF16)
    out_ref[:, 0:CAP, :] = rows.reshape(groups, CAP, width)
    shifted = jnp.broadcast_to((labels + 1).astype(F32), (META, docs)).astype(BF16)
    slot_labels = dot_t(shifted, places)
    of_cluster = ones_where(iota((clusters, docs), 0) == labels)
    counts = dot_t(jnp.ones((META, docs), BF16), of_cluster)
    blank = jnp.zeros((META, width - groups * CAP - clusters), F32)
    meta = jnp.concatenate([slot_labels, counts, blank], axis=1).astype(BF16)
    for g in range(groups):
        out_ref[g, CAP:, :] = meta
    rank_ref[...] = rank_of(of_cluster, docs)


def meta_rows(got_ref):
    groups = got_ref.shape[0]
    meta = got_ref[0, CAP:, :].astype(F32)
    row = iota(meta.shape, 0)
    for g in range(1, groups):
        meta = jnp.where(row == g, got_ref[g, CAP:, :].astype(F32), meta)
    return meta


def reslot(where_ref, got_ref, out_ref):
    groups, _, width = got_ref.shape
    slots = groups * CAP
    me = where_ref[0]
    labels = meta_rows(got_ref)[:, 0:slots].astype(BF16)
    lane, at = iota((slots, slots), 0), iota((slots, slots), 1)
    mine = ones_where(lane == me * CAP + lax.bitwise_and(at, CAP - 1))
    picked = dot(labels, mine)
    own = iota((groups, slots), 0) == lax.shift_right_logical(iota((groups, slots), 1), 6)
    label = jnp.sum(jnp.where(own, picked, 0.0), axis=0, keepdims=True).astype(jnp.int32)
    cluster = label - 1 - me * GROUP_CLUSTERS
    onehot = ones_where(iota((GROUP_CLUSTERS, slots), 0) == cluster)
    place = cluster * CAP + rank_of(onehot, slots).astype(jnp.int32)
    place = jnp.where(label > 0, place, -1)
    total = GROUP_CLUSTERS * CAP
    step = total // 4
    rows = got_ref[:, 0:CAP, :].reshape(slots, width)
    for s in range(0, total, step):
        places = jnp.where(iota((step, slots), 0) + s == place, 1.0, 0.0)
        filled = jnp.sum(places, axis=1, keepdims=True) > 0.5
        moved = dot(places.astype(BF16), rows)
        out_ref[s : s + step, :] = moved.astype(BF16)
        first = moved[:, 0:128]
        first = jnp.where((iota(first.shape, 1) == 0) & ~filled, EMPTY, first)
        out_ref[s : s + step, 0:128] = first.astype(BF16)


def return_index(where_ref, labels_ref, rank_ref, got_ref, out_ref):
    groups = got_ref.shape[0]
    docs = labels_ref.shape[1]
    clusters = groups * GROUP_CLUSTERS
    me = where_ref[0]
    counts = meta_rows(got_ref)[:, groups * CAP : groups * CAP + clusters]
    counts = jnp.where(iota(counts.shape, 0) < me, counts, 0.0).astype(BF16)
    labels = labels_ref[...]
    of_cluster = ones_where(iota((clusters, docs), 0) == labels)
    earlier = jnp.sum(dot(counts, of_cluster), axis=0, keepdims=True)
    out_ref[...] = labels * CAP + (rank_ref[...] + earlier).astype(jnp.int32)


def best_against(own_ref, other_ref, same):
    total = own_ref.shape[0]
    block = 256
    out = []
    for j in range(0, total, block):
        mine = own_ref[j : j + block, :]
        best = jnp.full((8, block), -1.0, F32)
        for i in range(0, total, block):
            theirs = other_ref[i : i + block, :]
            scores = dot_t(theirs, mine)
            keep = theirs[:, 0:1].astype(F32) < 1.5
            if same and i == j:
                keep = keep & (iota((block, block), 0) != iota((block, block), 1))
            scores = jnp.where(keep, scores, -1.0)
            best = jnp.maximum(best, jnp.max(scores.reshape(block // 8, 8, block), axis=0))
        out.append(jnp.max(best, axis=0, keepdims=True))
    return jnp.concatenate(out, axis=1)


def best_own(own_ref, out_ref):
    out_ref[...] = best_against(own_ref, own_ref, True)


def best_all(own_ref, other_ref, first_ref, out_ref):
    total = own_ref.shape[0]
    best = jnp.maximum(best_against(own_ref, other_ref, False), first_ref[...])
    pick = ones_where(iota((8, 256), 1) == 0)
    flag = dot_t(pick, own_ref[:, 0:256])[0:1, :]
    width = 2.0 / (BINS - 1)
    centers = -1.0 + iota((BINS, 1), 0).astype(F32) * width
    weights = jnp.maximum(1.0 - jnp.abs(best - centers) / width, 0.0)
    weights = jnp.where(flag < 1.5, weights, 0.0)
    folded = weights[:, 0:128]
    for s in range(128, total, 128):
        folded = folded + weights[:, s : s + 128]
    hist = jnp.sum(folded.T, axis=0, keepdims=True)
    rows = out_ref.shape[0]
    hists = jnp.broadcast_to(hist, (rows, BINS))
    out_ref[:, 128:256] = hists
    pieces = jnp.concatenate(
        [jnp.broadcast_to(best[:, s : s + 128], (4, 128)) for s in range(0, total, 128)], axis=0
    )
    for s in range(0, rows, 32):
        out_ref[s : s + 32, 0:128] = pieces


def pick_results(where_ref, index_ref, got_ref, best_ref, hist_ref):
    owners = got_ref.shape[0]
    docs = index_ref.shape[1]
    quarter = where_ref[1]
    index = index_ref[...]
    owner = lax.shift_right_logical(index, 5)
    lane = quarter * 32 + lax.bitwise_and(index, 31)
    onehot = ones_where(iota((owners, docs), 0) == owner)
    values = got_ref[:, 0:128].T
    high = values.astype(BF16)
    rest = values - high.astype(F32)
    middle = rest.astype(BF16)
    low = (rest - middle.astype(F32)).astype(BF16)
    picked = dot(high, onehot) + dot(middle, onehot) + dot(low, onehot)
    picked = jnp.where(iota((128, docs), 0) == lane, picked, 0.0)
    best_ref[...] = jnp.sum(picked, axis=0, keepdims=True)
    hist = jnp.sum(got_ref[:, 128:256], axis=0, keepdims=True)
    hist_ref[...] = hist * (1.0 / (owners * docs))


VMEM = pl.BlockSpec(memory_space=pltpu.VMEM)
SMEM = pl.BlockSpec(memory_space=pltpu.SMEM)


def call(kernel, outs, specs, flops):
    many = isinstance(outs, tuple)
    return pl.pallas_call(
        kernel,
        out_shape=outs,
        in_specs=specs,
        out_specs=tuple(VMEM for _ in outs) if many else VMEM,
        cost_estimate=pl.CostEstimate(flops=flops, bytes_accessed=4000000, transcendentals=0),
    )


def shape(dims, dtype):
    return jax.ShapeDtypeStruct(dims, dtype)


def exchange(x, axes):
    return lax.all_to_all(x, axes, split_axis=0, concat_axis=0, tiled=True)


def shards(embeddings, document_cluster_index):
    row_count = lax.axis_size(ROWS)
    col_count = lax.axis_size(COLS)
    docs, width = embeddings.shape
    labels = document_cluster_index.reshape(1, docs)
    col = lax.axis_index(COLS)
    where = jnp.stack([lax.axis_index(ROWS), col % 4]).astype(jnp.int32)
    block = CAP + META
    sends, rank = call(
        normalise_and_slot,
        (shape((row_count, block, width), BF16), shape((1, docs), F32)),
        [VMEM, VMEM],
        2 * row_count * CAP * docs * width,
    )(labels, embeddings)
    got = exchange(sends, ROWS)
    total = GROUP_CLUSTERS * CAP
    sends = call(
        reslot, shape((total, width), BF16), [SMEM, VMEM], 2 * total * row_count * CAP * width
    )(where, got)
    index = call(return_index, shape((1, docs), jnp.int32), [SMEM, VMEM, VMEM, VMEM], 2**26)(
        where, labels, rank, got
    )
    own = exchange(sends.reshape(col_count, total // col_count, width), COLS)
    own = own.reshape(total, width)
    other = lax.ppermute(own, COLS, [(i, i ^ 1) for i in range(col_count)])
    flops = 2 * total * total * width
    first = call(best_own, shape((1, total), F32), [VMEM], flops)(own)
    results = call(
        best_all, shape((row_count * col_count, 256), F32), [VMEM, VMEM, VMEM], flops
    )(own, other, first)
    results = exchange(results, ALL)
    best, hist = call(
        pick_results, (shape((1, docs), F32), shape((1, BINS), F32)), [SMEM, VMEM, VMEM], 2**26
    )(where, index, results)
    return (best.reshape(docs), hist.reshape(BINS))


def solution(mesh):
    torus = Mesh(
        mesh.devices.reshape(2, 4, 2, 8, 2), ("rows_0", "rows_1", "cols_0", "cols_1", "cols_2")
    )
    in_specs = (P(ALL, None), P(ALL))
    out_specs = (P(ALL), P())
    return jax.shard_map(
        shards, mesh=torus, in_specs=in_specs, out_specs=out_specs, check_vma=False
    )
```

time: 175 us -> 117 us (0.67)
  blocking collectives: 92 us -> 48.4 us
  Pallas kernels: 0 us -> 18.4 us
  local copies, waits for them, and re-layouts: 14.7 us -> 3.55 us
  other arithmetic: 10.2 us -> 0.59 us
  matrix products: 6.54 us -> 0 us
  starting transfers between devices: 22.1 us -> 16.1 us
    psum x5 -> x0, blocking collectives: 39.1 us -> none  [one_axis_at_a_time(): x = lax.psum(x, axis)]
    pallas_call x0 -> x6, Pallas kernels: none -> 18.4 us  [the longest x1 4.6 us: shards(): call(best_all, shape((row_count * col_count, 256), F32), [VMEM, VMEM, VME...]
    scatter x3 -> x0, local copies, waits for them, and re-layouts: 6.82 us -> none  [the longest x1 2.98 us: shards(): jnp.zeros((send_total, width), jnp.bfloat16).at[send_place]]
    dot_general x1 -> x0, matrix products: 6.54 us -> none  [shards(): lax.dot_general(got_rows, gathered_rows, (((1,), (1,)), ((), ())), prefer...]
    all_to_all x4 -> x2, starting transfers between devices: 19.1 us -> 13.6 us  [exchange(): return lax.all_to_all(x, axes, split_axis=0, concat_axis=0, tiled=True)]
    all_to_all x1, blocking collectives: 52.9 us -> 48.4 us  [exchange(): return lax.all_to_all(x, axes, split_axis=0, concat_axis=0, tiled=True)]
    gather x3 -> x0, local copies, waits for them, and re-layouts: 4.31 us -> none  [the longest x2 2.36 us: shards(): came_back[jnp.minimum(send_place, send_total - 1)]]
    scatter x1 -> x0, other arithmetic: 3.11 us -> none  [shards(): jnp.zeros((slot_count, width), jnp.bfloat16).at[places].set(normed)]
  transfers between devices with their start and end apart: 6 -> 3, of which waited for: 5 -> 2; matrix products, arithmetic and copies ran while one was open for 6% -> 1% of each run, Pallas kernels for 0% -> 5%
where the time goes in v1:
time: 117 us; the launch traced here: 116 us
  blocking collectives  48.4 us (41%)
  waiting for transfers between devices  28.8 us (25%)
  Pallas kernels  18.4 us (16%)
  starting transfers between devices  16.1 us (14%)
  local copies, waits for them, and re-layouts  3.55 us (3%)
    all_to_all x1, blocking collectives, exchange(): return lax.all_to_all(x, axes, split_axis=0, concat_axis=0, tiled=True)  48.4 us
    all_to_all x2, waiting for transfers between devices, exchange(): return lax.all_to_all(x, axes, split_axis=0, concat_axis=0, tiled=True)  28.8 us
    all_to_all x2, starting transfers between devices, exchange(): return lax.all_to_all(x, axes, split_axis=0, concat_axis=0, tiled=True)  13.6 us
    pallas_call x1, Pallas kernels, shards(): call(best_all, shape((row_count * col_count, 256), F32), [VMEM, VMEM, VME...  4.6 us
    pallas_call x1, Pallas kernels, shards(): first = call(best_own, shape((1, total), F32), [VMEM], flops)(own)  3.84 us
    pallas_call x1, Pallas kernels, shards(): call(reslot, shape((total, width), BF16), [SMEM, VMEM], 2 * total * row_c...  3.74 us
    pallas_call x1, Pallas kernels, shards(): call(normalise_and_slot, (shape((row_count, block, width), BF16), shape((...  2.57 us
    ppermute x1, starting transfers between devices, shards(): other = lax.ppermute(own, COLS, [(i, i ^ 1) for i in range(col_count)])  2.43 us
  transfers between devices with their start and end apart: 3, of which 2 were waited for; matrix products, arithmetic and copies ran while one was open for 1% of the time, Pallas kernels for 5%

profile of v1, /device:TPU:1, one launch (start us, length us, event | category | flops | bytes accessed | tf_op | source)
XLA Modules:
  0.0 116.5 jit_solution(17714774573792960862)
XLA Ops:
  0.6 2.6 %shard_map.41 = (bf16[8,72,768]{2,1,0:T(8,128)(2,1)}, f32[1,256]{1,0:T(1,128)}) custom-call(s32[1,256]{1,0:T(1,128)} %bitcast.17, bf16[256,768]{1,0:T(8,128)(2,1)} %embeddings_ref.1), custom_call_target="tpu_custom_call" | custom-call | flops 201326592 | bytes 4000000 | tf_op jit(solution)/shard_map/pallas_call | solution.py:217
  3.2 7.5 %all-to-all-start = ((bf16[8,72,768]{2,1,0:T(8,128)(2,1)}), bf16[8,72,768]{2,1,0:T(8,128)(2,1)S(1)}, u32[]{:S(2)}, u32[]{:S(2)}) async-start(bf16[8,72,768]{2,1,0:T(8,128)(2,1)} %get-tuple-element.7), calls=%async_computation | async-start | bytes 1769472 | tf_op jit(solution)/shard_map/all_to_all | solution.py:206
  10.7 0.6 pad_add_fusion.where_ref
  11.3 15.0 %all-to-all-done.got_ref = bf16[8,72,768]{2,1,0:T(8,128)(2,1)S(1)} async-done(((bf16[8,72,768]{2,1,0:T(8,128)(2,1)}), bf16[8,72,768]{2,1,0:T(8,128)(2,1)S(1)}, u32[]{:S(2)}, u32[]{:S(2)}) %all-to-all-start) | async-done | bytes 884768 | tf_op jit(solution)/shard_map/all_to_all | solution.py:206
  26.3 0.0 copy-start
  26.3 0.9 copy-done
  27.2 3.7 %shard_map.43 = bf16[1024,768]{1,0:T(8,128)(2,1)} custom-call(s32[2]{0:T(128)} %pad_add_fusion.where_ref, bf16[8,72,768]{2,1,0:T(8,128)(2,1)} %copy-done), custom_call_target="tpu_custom_call" | custom-call | flops 805306368 | bytes 4000000 | tf_op jit(solution)/shard_map/pallas_call | solution.py:225
  31.0 48.4 %all_to_all.21 = bf16[32,32,768]{2,1,0:T(8,128)(2,1)S(1)} all-to-all(bf16[32,32,768]{2,1,0:T(8,128)(2,1)} %bitcast.14), channel_id=1, replica_groups=mesh['rows_0'=2,'rows_1'=4,'cols_0'=2,'cols_1'=8,'cols_2'=2] {'cols_0','..., dimensions={0} | all-to-all | bytes 3145728 | tf_op jit(solution)/shard_map/all_to_all | solution.py:206
  79.3 0.0 copy-start.1
  79.3 2.4 %collective-permute-start = (bf16[1024,768]{1,0:T(8,128)(2,1)S(1)}, bf16[1024,768]{1,0:T(8,128)(2,1)}, u32[]{:S(2)}, u32[]{:S(2)}) collective-permute-start(bf16[1024,768]{1,0:T(8,128)(2,1)S(1)} %bitcast.11), channel_id=1, source_target_pairs={{0,1},{1,0},{2,3},{3,2},{4,5},{5,4},{6,7},{7,6},{8,9},{9,8},{10,11... | collective-permute-start | bytes 4718600 | tf_op jit(solution)/shard_map/ppermute | solution.py:233
  81.8 0.0 copy-done.1
  81.8 3.8 %shard_map.44.first_ref = f32[1,1024]{1,0:T(1,128)} custom-call(bf16[1024,768]{1,0:T(8,128)(2,1)} %bitcast.12), custom_call_target="tpu_custom_call" | custom-call | flops 1610612736 | bytes 4000000 | tf_op jit(solution)/shard_map/pallas_call | solution.py:235
  85.6 0.0 collective-permute-done.other_ref
  85.6 4.6 %shard_map.45 = f32[256,256]{1,0:T(8,128)} custom-call(bf16[1024,768]{1,0:T(8,128)(2,1)} %bitcast.13, bf16[1024,768]{1,0:T(8,128)(2,1)} %collective-permute-done.other_ref, f32[1,1024]{1,0:T(1,128)} %shard_map.44.first_ref), custom_call_target="tpu_custom_call" | custom-call | flops 1610612736 | bytes 4000000 | tf_op jit(solution)/shard_map/pallas_call | solution.py:236
  90.2 1.9 %copy.4 = f32[256,1,256]{2,1,0:T(1,128)} copy(f32[256,1,256]{2,0,1:T(8,128)} %bitcast.16) | data formatting | bytes 524288 | tf_op jit(solution)/shard_map/all_to_all | solution.py:206
  92.1 6.1 %all-to-all-start.2 = ((f32[256,1,256]{2,1,0:T(1,128)}), f32[256,1,256]{2,1,0:T(1,128)S(1)}, u32[]{:S(2)}, u32[]{:S(2)}) async-start(f32[256,1,256]{2,1,0:T(1,128)} %copy.4), calls=%async_computation.2 | async-start | bytes 524288 | tf_op jit(solution)/shard_map/all_to_all | solution.py:206
  98.3 1.9 %shard_map.42.index_ref = s32[1,256]{1,0:T(1,128)} custom-call(s32[2]{0:T(128)} %pad_add_fusion.where_ref, s32[1,256]{1,0:T(1,128)} %bitcast.18, f32[1,256]{1,0:T(1,128)} %get-tuple-element.6.rank_ref, bf16[8,72,768]{2,1,0:T(8,128)(2,1)} %copy-done), custom_call_target="tpu_custom_call" | custom-call | flops 67108864 | bytes 4000000 | tf_op jit(solution)/shard_map/pallas_call | solution.py:228
  100.2 13.8 %all-to-all-done.2 = f32[256,1,256]{2,1,0:T(1,128)S(1)} async-done(((f32[256,1,256]{2,1,0:T(1,128)}), f32[256,1,256]{2,1,0:T(1,128)S(1)}, u32[]{:S(2)}, u32[]{:S(2)}) %all-to-all-start.2) | async-done | bytes 262176 | tf_op jit(solution)/shard_map/all_to_all | solution.py:206
  114.0 0.7 copy.7
  114.7 1.8 %shard_map.46 = (f32[1,256]{1,0:T(1,128)}, f32[1,128]{1,0:T(1,128)}) custom-call(s32[2]{0:T(128)} %pad_add_fusion.where_ref, s32[1,256]{1,0:T(1,128)} %shard_map.42.index_ref, f32[256,256]{1,0:T(8,128)} %bitcast.15), custom_call_target="tpu_custom_call" | custom-call | flops 67108864 | bytes 4000000 | tf_op jit(solution)/shard_map/pallas_call | solution.py:240
Async XLA Ops:
  3.2 23.1 %all-to-all-start = ((bf16[8,72,768]{2,1,0:T(8,128)(2,1)}), bf16[8,72,768]{2,1,0:T(8,128)(2,1)S(1)}, u32[]{:S(2)}, u32[]{:S(2)}) async-start(bf16[8,72,768]{2,1,0:T(8,128)(2,1)} %get-tuple-element.7), calls=%async_computation | async-start | bytes 1769472 | tf_op jit(solution)/shard_map/all_to_all | solution.py:206
  26.3 0.9 copy-start
  79.3 2.4 %copy-start.1 = (bf16[32,32,768]{2,1,0:T(8,128)(2,1)}, bf16[32,32,768]{2,1,0:T(8,128)(2,1)S(1)}, u32[]{:S(2)}) copy-start(bf16[32,32,768]{2,1,0:T(8,128)(2,1)S(1)} %all_to_all.21) | copy-start | bytes 4718596
  79.3 6.3 %collective-permute-start = (bf16[1024,768]{1,0:T(8,128)(2,1)S(1)}, bf16[1024,768]{1,0:T(8,128)(2,1)}, u32[]{:S(2)}, u32[]{:S(2)}) collective-permute-start(bf16[1024,768]{1,0:T(8,128)(2,1)S(1)} %bitcast.11), channel_id=1, source_target_pairs={{0,1},{1,0},{2,3},{3,2},{4,5},{5,4},{6,7},{7,6},{8,9},{9,8},{10,11... | collective-permute-start | bytes 4718600 | tf_op jit(solution)/shard_map/ppermute | solution.py:233
  92.1 21.9 %all-to-all-start.2 = ((f32[256,1,256]{2,1,0:T(1,128)}), f32[256,1,256]{2,1,0:T(1,128)S(1)}, u32[]{:S(2)}, u32[]{:S(2)}) async-start(f32[256,1,256]{2,1,0:T(1,128)} %copy.4), calls=%async_computation.2 | async-start | bytes 524288 | tf_op jit(solution)/shard_map/all_to_all | solution.py:206

commit v2 on v1

--- a/solution.py
+++ b/solution.py
@@ -153,25 +153,22 @@
     for s in range(128, total, 128):
         folded = folded + weights[:, s : s + 128]
     hist = jnp.sum(folded.T, axis=0, keepdims=True)
-    rows = out_ref.shape[0]
-    hists = jnp.broadcast_to(hist, (rows, BINS))
-    out_ref[:, 128:256] = hists
-    pieces = jnp.concatenate(
-        [jnp.broadcast_to(best[:, s : s + 128], (4, 128)) for s in range(0, total, 128)], axis=0
-    )
-    for s in range(0, rows, 32):
-        out_ref[s : s + 32, 0:128] = pieces
+    even = lax.bitwise_and(iota((8, 128), 0), 1) == 0
+    for s in range(0, total, 128):
+        pair = jnp.where(even, best[:, s : s + 128], hist)
+        for at in range(s // 16, out_ref.shape[0], total // 16):
+            out_ref[at : at + 8, :] = pair
 
 
 def pick_results(where_ref, index_ref, got_ref, best_ref, hist_ref):
-    owners = got_ref.shape[0]
+    owners = got_ref.shape[0] // 2
     docs = index_ref.shape[1]
     quarter = where_ref[1]
     index = index_ref[...]
     owner = lax.shift_right_logical(index, 5)
     lane = quarter * 32 + lax.bitwise_and(index, 31)
     onehot = ones_where(iota((owners, docs), 0) == owner)
-    values = got_ref[:, 0:128].T
+    values = got_ref[pl.ds(0, owners, stride=2), :].T
     high = values.astype(BF16)
     rest = values - high.astype(F32)
     middle = rest.astype(BF16)
@@ -179,7 +176,7 @@
     picked = dot(high, onehot) + dot(middle, onehot) + dot(low, onehot)
     picked = jnp.where(iota((128, docs), 0) == lane, picked, 0.0)
     best_ref[...] = jnp.sum(picked, axis=0, keepdims=True)
-    hist = jnp.sum(got_ref[:, 128:256], axis=0, keepdims=True)
+    hist = jnp.sum(got_ref[pl.ds(1, owners, stride=2), :], axis=0, keepdims=True)
     hist_ref[...] = hist * (1.0 / (owners * docs))
 
 
@@ -194,6 +191,7 @@
         out_shape=outs,
         in_specs=specs,
         out_specs=tuple(VMEM for _ in outs) if many else VMEM,
+        compiler_params=pltpu.CompilerParams(vmem_limit_bytes=24 * 2**20),
         cost_estimate=pl.CostEstimate(flops=flops, bytes_accessed=4000000, transcendentals=0),
     )
 
@@ -234,9 +232,10 @@
     flops = 2 * total * total * width
     first = call(best_own, shape((1, total), F32), [VMEM], flops)(own)
     results = call(
-        best_all, shape((row_count * col_count, 256), F32), [VMEM, VMEM, VMEM], flops
+        best_all, shape((row_count * col_count * 2, 128), F32), [VMEM, VMEM, VMEM], flops
     )(own, other, first)
-    results = exchange(results, ALL)
+    results = exchange(results.reshape(row_count * col_count, 2, 128), ALL)
+    results = results.reshape(row_count * col_count * 2, 128)
     best, hist = call(
         pick_results, (shape((1, docs), F32), shape((1, BINS), F32)), [SMEM, VMEM, VMEM], 2**26
     )(where, index, results)

time: 117 us -> 108 us (0.923)
  Pallas kernels: 18.4 us -> 10.2 us
  waiting for transfers between devices: 28.8 us -> 31.7 us
  local copies, waits for them, and re-layouts: 3.55 us -> 1.68 us
    pallas_call x1, Pallas kernels: 3.84 us -> 1.92 us  [shards(): first = call(best_own, shape((1, total), F32), [VMEM], flops)(own)]
    all_to_all x1 -> x0, local copies, waits for them, and re-layouts: 1.91 us -> none  [exchange(): return lax.all_to_all(x, axes, split_axis=0, concat_axis=0, tiled=True)]
    pallas_call x1, Pallas kernels: 4.6 us -> 2.77 us  [shards(): call(best_all, shape((row_count * col_count * 2, 128), F32), [VMEM, VMEM,...]
    pallas_call x1, Pallas kernels: 3.74 us -> 1.95 us  [shards(): call(reslot, shape((total, width), BF16), [SMEM, VMEM], 2 * total * row_c...]
    all_to_all x2, waiting for transfers between devices: 28.8 us -> 30.6 us  [exchange(): return lax.all_to_all(x, axes, split_axis=0, concat_axis=0, tiled=True)]
    pallas_call x1, Pallas kernels: 1.9 us -> 0.69 us  [shards(): call(return_index, shape((1, docs), jnp.int32), [SMEM, VMEM, VMEM, VMEM],...]
  transfers between devices with their start and end apart: 3 -> 3, of which waited for: 2 -> 3; matrix products, arithmetic and copies ran while one was open for 1% -> 0% of each run, Pallas kernels for 5% -> 2%
where the time goes in v2:
time: 108 us
  blocking collectives  48.2 us (45%)
  waiting for transfers between devices  31.7 us (29%)
  starting transfers between devices  15.3 us (14%)
  Pallas kernels  10.2 us (9%)
  local copies, waits for them, and re-layouts  1.68 us (2%)
    all_to_all x1, blocking collectives, exchange(): return lax.all_to_all(x, axes, split_axis=0, concat_axis=0, tiled=True)  48.2 us
    all_to_all x2, waiting for transfers between devices, exchange(): return lax.all_to_all(x, axes, split_axis=0, concat_axis=0, tiled=True)  30.6 us
    all_to_all x2, starting transfers between devices, exchange(): return lax.all_to_all(x, axes, split_axis=0, concat_axis=0, tiled=True)  12.9 us
    pallas_call x1, Pallas kernels, shards(): call(best_all, shape((row_count * col_count * 2, 128), F32), [VMEM, VMEM,...  2.77 us
    ppermute x1, starting transfers between devices, shards(): other = lax.ppermute(own, COLS, [(i, i ^ 1) for i in range(col_count)])  2.43 us
  transfers between devices with their start and end apart: 3, of which 3 were waited for; matrix products, arithmetic and copies ran while one was open for 0% of the time, Pallas kernels for 2%

profile of v2, /device:TPU:1, one launch (start us, length us, event | category | flops | bytes accessed | tf_op | source)
XLA Modules:
  0.0 107.8 jit_solution(9649472110431788540)
XLA Ops:
  0.6 0.0 copy-start
  0.6 0.7 copy-done
  1.3 0.0 copy-start.2
  1.3 1.0 copy-done.2
  2.3 1.5 %shard_map.41 = (bf16[8,72,768]{2,1,0:T(8,128)(2,1)}, f32[1,256]{1,0:T(1,128)S(1)}) custom-call(s32[1,256]{1,0:T(1,128)S(1)} %bitcast.14, bf16[256,768]{1,0:T(8,128)(2,1)S(1)} %copy-done.2), custom_call_target="tpu_custom_call" | custom-call | flops 201326592 | bytes 4000000 | tf_op jit(solution)/shard_map/pallas_call | solution.py:215
  3.9 7.5 %all-to-all-start = ((bf16[8,72,768]{2,1,0:T(8,128)(2,1)}), bf16[8,72,768]{2,1,0:T(8,128)(2,1)S(1)}, u32[]{:S(2)}, u32[]{:S(2)}) async-start(bf16[8,72,768]{2,1,0:T(8,128)(2,1)} %get-tuple-element.7), calls=%async_computation | async-start | bytes 1769472 | tf_op jit(solution)/shard_map/all_to_all | solution.py:204
  11.3 0.1 pad_add_fusion.where_ref
  11.4 15.5 %all-to-all-done.got_ref = bf16[8,72,768]{2,1,0:T(8,128)(2,1)S(1)} async-done(((bf16[8,72,768]{2,1,0:T(8,128)(2,1)}), bf16[8,72,768]{2,1,0:T(8,128)(2,1)S(1)}, u32[]{:S(2)}, u32[]{:S(2)}) %all-to-all-start) | async-done | bytes 884768 | tf_op jit(solution)/shard_map/all_to_all | solution.py:204
  26.9 1.9 %shard_map.43 = bf16[1024,768]{1,0:T(8,128)(2,1)S(1)} custom-call(s32[2]{0:T(128)S(1)} %pad_add_fusion.where_ref, bf16[8,72,768]{2,1,0:T(8,128)(2,1)S(1)} %all-to-all-done.got_ref), custom_call_target="tpu_custom_call" | custom-call | flops 805306368 | bytes 4000000 | tf_op jit(solution)/shard_map/pallas_call | solution.py:223
  28.9 48.2 %all_to_all.15 = bf16[32,32,768]{2,1,0:T(8,128)(2,1)S(1)} all-to-all(bf16[32,32,768]{2,1,0:T(8,128)(2,1)S(1)} %bitcast.12), channel_id=1, replica_groups=mesh['rows_0'=2,'rows_1'=4,'cols_0'=2,'cols_1'=8,'cols_2'=2] {'cols_0','..., dimensions={0} | all-to-all | bytes 3145728 | tf_op jit(solution)/shard_map/all_to_all | solution.py:204
  77.1 2.4 %collective-permute-start = (bf16[1024,768]{1,0:T(8,128)(2,1)S(1)}, bf16[1024,768]{1,0:T(8,128)(2,1)S(1)}, u32[]{:S(2)}, u32[]{:S(2)}) collective-permute-start(bf16[1024,768]{1,0:T(8,128)(2,1)S(1)} %bitcast.9), channel_id=1, source_target_pairs={{0,1},{1,0},{2,3},{3,2},{4,5},{5,4},{6,7},{7,6},{8,9},{9,8},{10,11... | collective-permute-start | bytes 4718600 | tf_op jit(solution)/shard_map/ppermute | solution.py:231
  79.5 1.9 %shard_map.44.first_ref = f32[1,1024]{1,0:T(1,128)S(1)} custom-call(bf16[1024,768]{1,0:T(8,128)(2,1)S(1)} %bitcast.10), custom_call_target="tpu_custom_call" | custom-call | flops 1610612736 | bytes 4000000 | tf_op jit(solution)/shard_map/pallas_call | solution.py:233
  81.4 0.0 copy-start.1
  81.4 1.1 %collective-permute-done.other_ref = bf16[1024,768]{1,0:T(8,128)(2,1)S(1)} collective-permute-done((bf16[1024,768]{1,0:T(8,128)(2,1)S(1)}, bf16[1024,768]{1,0:T(8,128)(2,1)S(1)}, u32[]{:S(2)}, u32[]{:S(2)}) %collective-permute-start) | collective-permute-done | bytes 1572896 | tf_op jit(solution)/shard_map/ppermute | solution.py:231
  82.5 2.8 %shard_map.45 = f32[512,128]{1,0:T(8,128)} custom-call(bf16[1024,768]{1,0:T(8,128)(2,1)S(1)} %bitcast.11, bf16[1024,768]{1,0:T(8,128)(2,1)S(1)} %collective-permute-done.other_ref, f32[1,1024]{1,0:T(1,128)S(1)} %shard_map.44.first_ref), custom_call_target="tpu_custom_call" | custom-call | flops 1610612736 | bytes 4000000 | tf_op jit(solution)/shard_map/pallas_call | solution.py:234
  85.3 5.4 %all-to-all-start.2 = ((f32[256,2,128]{2,1,0:T(2,128)}), f32[256,2,128]{2,1,0:T(2,128)S(1)}, u32[]{:S(2)}, u32[]{:S(2)}) async-start(f32[256,2,128]{2,1,0:T(2,128)} %bitcast.5), calls=%async_computation.2 | async-start | bytes 524288 | tf_op jit(solution)/shard_map/all_to_all | solution.py:204
  90.7 0.0 copy-done.1
  90.7 0.7 shard_map.42.index_ref
  91.4 15.0 %all-to-all-done.2 = f32[256,2,128]{2,1,0:T(2,128)S(1)} async-done(((f32[256,2,128]{2,1,0:T(2,128)}), f32[256,2,128]{2,1,0:T(2,128)S(1)}, u32[]{:S(2)}, u32[]{:S(2)}) %all-to-all-start.2) | async-done | bytes 262176 | tf_op jit(solution)/shard_map/all_to_all | solution.py:204
  106.4 1.4 %shard_map.46 = (f32[1,256]{1,0:T(1,128)}, f32[1,128]{1,0:T(1,128)}) custom-call(s32[2]{0:T(128)S(1)} %pad_add_fusion.where_ref, s32[1,256]{1,0:T(1,128)S(1)} %shard_map.42.index_ref, f32[512,128]{1,0:T(8,128)S(1)} %bitcast.13), custom_call_target="tpu_custom_call" | custom-call | flops 67108864 | bytes 4000000 | tf_op jit(solution)/shard_map/pallas_call | solution.py:239
Async XLA Ops:
  0.6 0.7 copy-start
  1.3 1.0 copy-start.2
  3.9 23.1 %all-to-all-start = ((bf16[8,72,768]{2,1,0:T(8,128)(2,1)}), bf16[8,72,768]{2,1,0:T(8,128)(2,1)S(1)}, u32[]{:S(2)}, u32[]{:S(2)}) async-start(bf16[8,72,768]{2,1,0:T(8,128)(2,1)} %get-tuple-element.7), calls=%async_computation | async-start | bytes 1769472 | tf_op jit(solution)/shard_map/all_to_all | solution.py:204
  77.1 5.5 %collective-permute-start = (bf16[1024,768]{1,0:T(8,128)(2,1)S(1)}, bf16[1024,768]{1,0:T(8,128)(2,1)S(1)}, u32[]{:S(2)}, u32[]{:S(2)}) collective-permute-start(bf16[1024,768]{1,0:T(8,128)(2,1)S(1)} %bitcast.9), channel_id=1, source_target_pairs={{0,1},{1,0},{2,3},{3,2},{4,5},{5,4},{6,7},{7,6},{8,9},{9,8},{10,11... | collective-permute-start | bytes 4718600 | tf_op jit(solution)/shard_map/ppermute | solution.py:231
  81.4 9.3 %copy-start.1 = (s32[256]{0:T(256)S(1)}, s32[256]{0:T(256)}, u32[]{:S(2)}) copy-start(s32[256]{0:T(256)} %param.3) | copy-start | bytes 3076
  85.3 21.1 %all-to-all-start.2 = ((f32[256,2,128]{2,1,0:T(2,128)}), f32[256,2,128]{2,1,0:T(2,128)S(1)}, u32[]{:S(2)}, u32[]{:S(2)}) async-start(f32[256,2,128]{2,1,0:T(2,128)} %bitcast.5), calls=%async_computation.2 | async-start | bytes 524288 | tf_op jit(solution)/shard_map/all_to_all | solution.py:204

commit v3 on v2

v3 whole, which is shorter than its diff:
```python
import jax
import jax.numpy as jnp
from jax import lax
from jax.experimental import pallas as pl
from jax.experimental.pallas import tpu as pltpu
from jax.sharding import Mesh
from jax.sharding import PartitionSpec as P

CAP = 64
GROUP_CLUSTERS = 16
BINS = 128
ROWS = ("rows_0", "rows_1")
COLS = ("cols_0", "cols_1", "cols_2")
ALL = ROWS + COLS
LANES = 128
EMPTY = 2.0
F32 = jnp.float32
BF16 = jnp.bfloat16


def iota(shape, dim):
    return lax.broadcasted_iota(jnp.int32, shape, dim)


def dot(a, b):
    return lax.dot_general(a, b, (((1,), (0,)), ((), ())), preferred_element_type=F32)


def dot_t(a, b):
    return lax.dot_general(a, b, (((1,), (1,)), ((), ())), preferred_element_type=F32)


def ones_where(mask):
    return jnp.where(mask, 1.0, 0.0).astype(BF16)


def before(n):
    return ones_where(iota((n, n), 0) < iota((n, n), 1))


def rank_of(onehot, n):
    earlier = dot(onehot, before(n))
    return jnp.sum(onehot.astype(F32) * earlier, axis=0, keepdims=True)


def normalise_and_slot(labels_hbm, embeddings_hbm, out_ref, rank_ref, labels_ref, embeddings_ref, sems):
    labels_copy = pltpu.make_async_copy(labels_hbm, labels_ref, sems.at[0])
    embeddings_copy = pltpu.make_async_copy(embeddings_hbm, embeddings_ref, sems.at[1])
    labels_copy.start()
    embeddings_copy.start()
    docs, width = embeddings_ref.shape
    groups = out_ref.shape[0]
    clusters = groups * GROUP_CLUSTERS
    labels_copy.wait()
    labels = labels_ref[...]
    group = lax.shift_right_logical(labels, 4)
    onehot = ones_where(iota((groups, docs), 0) == group)
    slot = group * CAP + rank_of(onehot, docs).astype(jnp.int32)
    places = ones_where(iota((groups * CAP, docs), 0) == slot)
    shifted = jnp.broadcast_to((labels + 1).astype(F32), (8, docs)).astype(BF16)
    slot_labels = dot_t(shifted, places)
    of_cluster = ones_where(iota((clusters, docs), 0) == labels)
    counts = dot_t(jnp.ones((8, docs), BF16), of_cluster)
    row = iota((8, LANES), 0)
    meta = jnp.where(row == groups * CAP // LANES, counts, 0.0)
    for s in range(groups * CAP // LANES):
        meta = jnp.where(row == s, slot_labels[:, s * LANES : (s + 1) * LANES], meta)
    meta = meta.astype(BF16)
    rank_ref[...] = rank_of(of_cluster, docs)
    embeddings_copy.wait()
    values = embeddings_ref[...].astype(F32)
    total = jnp.sum(values * values, axis=1, keepdims=True)
    normed = (values * lax.rsqrt(total + 1e-06)).astype(BF16)
    rows = dot(places, normed).astype(BF16)
    pieces = width // LANES
    for g in range(groups):
        for f in range(pieces):
            block = rows[g * CAP : (g + 1) * CAP, f * LANES : (f + 1) * LANES]
            out_ref[g, f * CAP : (f + 1) * CAP, :] = block
        out_ref[g, pieces * CAP :, :] = meta


def slot_labels_of(got_ref, me):
    groups = got_ref.shape[0]
    slots = groups * CAP
    at = got_ref.shape[1] - 8
    source = lax.shift_right_logical(iota((8, slots), 1), 6)
    row = iota((8, LANES), 0)
    per_row = LANES // CAP
    picked = []
    for g in range(groups):
        meta = got_ref[g, at:, :].astype(F32)
        line = jnp.where(row == lax.shift_right_logical(me, 1), meta, 0.0)
        picked.append(jnp.sum(line, axis=0, keepdims=True))
    lines = jnp.concatenate(picked, axis=0).astype(BF16)
    lane, to = iota((LANES, slots), 0), iota((LANES, slots), 1)
    start = lax.bitwise_and(me, per_row - 1) * CAP
    move = ones_where(lane == start + lax.bitwise_and(to, CAP - 1))
    spread = jnp.where(iota((groups, slots), 0) == source, dot(lines, move), 0.0)
    return jnp.sum(spread, axis=0, keepdims=True)


def reslot(got_ref, out_ref):
    groups = got_ref.shape[0]
    slots = groups * CAP
    width = out_ref.shape[1]
    me = lax.axis_index(ROWS)
    label = slot_labels_of(got_ref, me).astype(jnp.int32)
    cluster = label - 1 - me * GROUP_CLUSTERS
    onehot = ones_where(iota((GROUP_CLUSTERS, slots), 0) == cluster)
    place = cluster * CAP + rank_of(onehot, slots).astype(jnp.int32)
    place = jnp.where(label > 0, place, -1)
    total = GROUP_CLUSTERS * CAP
    step = total // 4
    pieces = width // LANES
    rows = jnp.concatenate(
        [got_ref[:, f * CAP : (f + 1) * CAP, :].reshape(slots, LANES) for f in range(pieces)],
        axis=1,
    )
    for s in range(0, total, step):
        places = jnp.where(iota((step, slots), 0) + s == place, 1.0, 0.0)
        filled = jnp.sum(places, axis=1, keepdims=True) > 0.5
        moved = dot(places.astype(BF16), rows)
        out_ref[s : s + step, LANES:] = moved[:, LANES:].astype(BF16)
        first = moved[:, 0:LANES]
        first = jnp.where((iota(first.shape, 1) == 0) & ~filled, EMPTY, first)
        out_ref[s : s + step, 0:LANES] = first.astype(BF16)


def return_index(labels_ref, rank_ref, got_ref, out_ref):
    groups = got_ref.shape[0]
    docs = labels_ref.shape[1]
    clusters = groups * GROUP_CLUSTERS
    me = lax.axis_index(ROWS)
    at = got_ref.shape[1] - 8
    row = iota((8, LANES), 0)
    before_me = jnp.zeros((8, LANES), F32)
    for g in range(groups):
        before_me = before_me + jnp.where(g < me, got_ref[g, at:, :].astype(F32), 0.0)
    counts = jnp.where(row == groups * CAP // LANES, before_me, 0.0)
    labels = labels_ref[...]
    of_cluster = ones_where(iota((clusters, docs), 0) == labels)
    earlier = jnp.sum(dot(counts.astype(BF16), of_cluster), axis=0, keepdims=True)
    out_ref[...] = labels * CAP + (rank_ref[...] + earlier).astype(jnp.int32)


def best_against(own_ref, other_ref, same):
    block = 256
    out = []
    for j in range(0, own_ref.shape[0], block):
        mine = own_ref[j : j + block, :]
        best = jnp.full((8, block), -1.0, F32)
        for i in range(0, other_ref.shape[0], block):
            theirs = other_ref[i : i + block, :]
            scores = dot_t(theirs, mine)
            keep = theirs[:, 0:1].astype(F32) < 1.5
            if same and i == j:
                keep = keep & (iota((block, block), 0) != iota((block, block), 1))
            scores = jnp.where(keep, scores, -1.0)
            best = jnp.maximum(best, jnp.max(scores.reshape(block // 8, 8, block), axis=0))
        out.append(best)
    return jnp.concatenate(out, axis=1)


def best_own(own_ref, out_ref):
    out_ref[...] = best_against(own_ref, own_ref, True)


def best_more(own_ref, other_ref, so_far_ref, out_ref):
    out_ref[...] = jnp.maximum(best_against(own_ref, other_ref, False), so_far_ref[...])


def three_parts(x):
    high = x.astype(BF16).astype(F32)
    middle = (x - high).astype(BF16).astype(F32)
    return high, middle, x - high - middle


def best_last(own_ref, other_ref, so_far_ref, out_ref):
    total = own_ref.shape[0]
    best = jnp.maximum(best_against(own_ref, other_ref, False), so_far_ref[...])
    best = jnp.max(best, axis=0, keepdims=True)
    pick = ones_where(iota((8, 256), 1) == 0)
    flag = dot_t(pick, own_ref[:, 0:256])[0:1, :]
    width = 2.0 / (BINS - 1)
    centers = -1.0 + iota((BINS, 1), 0).astype(F32) * width
    weights = jnp.maximum(1.0 - jnp.abs(best - centers) / width, 0.0)
    weights = jnp.where(flag < 1.5, weights, 0.0)
    folded = weights[:, 0:LANES]
    for s in range(LANES, total, LANES):
        folded = folded + weights[:, s : s + LANES]
    hist = jnp.sum(folded.T, axis=0, keepdims=True)
    lines = jnp.concatenate([best[:, s : s + LANES] for s in range(0, total, LANES)], axis=0)
    parts = three_parts(lines)
    lane = iota((8, LANES), 1)
    sub = iota((8, LANES), 0)
    quarters = []
    for q in range(4):
        line = jnp.zeros((8, LANES), F32)
        for p in range(3):
            shift = (32 * (p - q)) % LANES
            moved = pltpu.roll(parts[p], shift, 1) if shift else parts[p]
            line = jnp.where(lax.shift_right_logical(lane, 5) == p, moved, line)
        quarters.append(line)
    blocks = []
    for s in range(total // LANES):
        block = jnp.broadcast_to(hist, (8, LANES))
        for q in range(4):
            block = jnp.where(sub == 2 * q + 1, quarters[q][s : s + 1, :], block)
        blocks.append(block)
    block = jnp.concatenate(blocks, axis=0).astype(BF16)
    for at in range(0, out_ref.shape[0], block.shape[0]):
        out_ref[at : at + block.shape[0], :] = block


def pick_results(index_ref, got_ref, best_ref, hist_ref):
    lines = got_ref.shape[0]
    docs = index_ref.shape[1]
    index = index_ref[...]
    line = lax.shift_right_logical(index, 5) * 2 + 1
    depth = lax.bitwise_and(index, 31)
    onehot = ones_where(iota((lines, docs), 0) == line)
    got = got_ref[...]
    picked = dot(got.astype(F32).T.astype(BF16), onehot)
    lane = iota((LANES, docs), 0)
    wanted = (lax.bitwise_and(lane, 31) == depth) & (lane < 96)
    best_ref[...] = jnp.sum(jnp.where(wanted, picked, 0.0), axis=0, keepdims=True)
    even = ones_where(lax.bitwise_and(iota((8, lines), 1), 1) == 0)
    hist = dot(even, got)[0:1, :]
    hist_ref[...] = hist * (1.0 / (lines // 2 * docs))


VMEM = pl.BlockSpec(memory_space=pltpu.VMEM)
ANY = pl.BlockSpec(memory_space=pl.ANY)


def call(kernel, outs, specs, flops, scratch=()):
    many = isinstance(outs, tuple)
    return pl.pallas_call(
        kernel,
        out_shape=outs,
        in_specs=specs,
        out_specs=tuple(VMEM for _ in outs) if many else VMEM,
        scratch_shapes=scratch,
        compiler_params=pltpu.CompilerParams(vmem_limit_bytes=24 * 2**20),
        cost_estimate=pl.CostEstimate(flops=flops, bytes_accessed=4000000, transcendentals=0),
    )


def shape(dims, dtype):
    return jax.ShapeDtypeStruct(dims, dtype)


def exchange(x, axes):
    return lax.all_to_all(x, axes, split_axis=0, concat_axis=0, tiled=True)


def shards(embeddings, document_cluster_index):
    row_count = lax.axis_size(ROWS)
    col_count = lax.axis_size(COLS)
    docs, width = embeddings.shape
    labels = document_cluster_index.reshape(1, docs)
    block = CAP * width // LANES + 8
    sends, rank = call(
        normalise_and_slot,
        (shape((row_count, block, LANES), BF16), shape((1, docs), F32)),
        [ANY, ANY],
        2 * row_count * CAP * docs * width,
        [
            pltpu.VMEM((1, docs), jnp.int32),
            pltpu.VMEM((docs, width), BF16),
            pltpu.SemaphoreType.DMA((2,)),
        ],
    )(labels, embeddings)
    got = exchange(sends, ROWS)
    total = GROUP_CLUSTERS * CAP
    sends = call(reslot, shape((total, width), BF16), [VMEM], 2 * total * row_count * CAP * width)(
        got
    )
    own = exchange(sends.reshape(col_count, total // col_count, width), COLS)
    own, got = lax.optimization_barrier((own.reshape(total, width), got))
    pairs = [(i, i ^ 1) for i in range(col_count)]
    half = total // 2
    other = [lax.ppermute(own[s : s + half], COLS, pairs) for s in (0, half)]
    flops = 2 * total * half * width
    best = call(best_own, shape((8, total), F32), [VMEM], 2 * flops)(own)
    best = call(best_more, shape((8, total), F32), [VMEM] * 3, flops)(own, other[0], best)
    index = call(return_index, shape((1, docs), jnp.int32), [VMEM] * 3, 2**26)(labels, rank, got)
    results = call(best_last, shape((row_count * col_count * 2, LANES), BF16), [VMEM] * 3, flops)(
        own, other[1], best
    )
    results, index = lax.optimization_barrier((results, index))
    results = exchange(results.reshape(row_count * col_count, 2, LANES), ALL)
    results = results.reshape(row_count * col_count * 2, LANES)
    best, hist = call(
        pick_results, (shape((1, docs), F32), shape((1, BINS), F32)), [VMEM, VMEM], 2**26
    )(index, results)
    return (best.reshape(docs), hist.reshape(BINS))


def solution(mesh):
    torus = Mesh(
        mesh.devices.reshape(2, 4, 2, 8, 2), ("rows_0", "rows_1", "cols_0", "cols_1", "cols_2")
    )
    in_specs = (P(ALL, None), P(ALL))
    out_specs = (P(ALL), P())
    return jax.shard_map(
        shards, mesh=torus, in_specs=in_specs, out_specs=out_specs, check_vma=False
    )
```

time: 108 us -> 102 us (0.944)
  blocking collectives: 48.2 us -> 88.7 us
  waiting for transfers between devices: 31.7 us -> 0.01 us
  starting transfers between devices: 15.3 us -> 2.62 us
  Pallas kernels: 10.2 us -> 7.59 us
    all_to_all x1 -> x3, blocking collectives: 48.2 us -> 88.7 us  [exchange(): return lax.all_to_all(x, axes, split_axis=0, concat_axis=0, tiled=True)]
    all_to_all x2 -> x0, waiting for transfers between devices: 30.6 us -> none  [exchange(): return lax.all_to_all(x, axes, split_axis=0, concat_axis=0, tiled=True)]
    all_to_all x2 -> x0, starting transfers between devices: 12.9 us -> none  [exchange(): return lax.all_to_all(x, axes, split_axis=0, concat_axis=0, tiled=True)]
    pallas_call x6 -> x7, Pallas kernels: 10.2 us -> 7.59 us  [the longest x1 1.85 us: shards(): best = call(best_own, shape((8, total), F32), [VMEM], 2 * flops)(own)]
    ppermute x1 -> x2, waiting for transfers between devices: 1.11 us -> 0.01 us  [shards(): other = [lax.ppermute(own[s:s + half], COLS, pairs) for s in (0, half)]]
    ppermute x1 -> x2, starting transfers between devices: 2.43 us -> 2.62 us  [shards(): other = [lax.ppermute(own[s:s + half], COLS, pairs) for s in (0, half)]]
  transfers between devices with their start and end apart: 3 -> 2, of which waited for: 3 -> 0; matrix products, arithmetic and copies ran while one was open for 0% -> 0% of each run, Pallas kernels for 2% -> 3%
where the time goes in v3:
time: 102 us; the launch traced here: 101 us
  blocking collectives  88.7 us (87%)
  Pallas kernels  7.59 us (7%)
  starting transfers between devices  2.62 us (3%)
  local copies, waits for them, and re-layouts  1.78 us (2%)
    all_to_all x3, blocking collectives, exchange(): return lax.all_to_all(x, axes, split_axis=0, concat_axis=0, tiled=True)  88.7 us
    ppermute x2, starting transfers between devices, shards(): other = [lax.ppermute(own[s:s + half], COLS, pairs) for s in (0, half)]  2.62 us
  transfers between devices with their start and end apart: 2, of which 0 were waited for; matrix products, arithmetic and copies ran while one was open for 0% of the time, Pallas kernels for 3%

profile of v3, /device:TPU:1, one launch (start us, length us, event | category | flops | bytes accessed | tf_op | source)
XLA Modules:
  0.0 101.4 jit_solution(10937964567957671407)
XLA Ops:
  0.6 0.0 copy-start
  0.6 0.7 copy-done
  1.3 0.0 copy-start.2
  1.3 1.0 copy-done.2
  2.3 1.1 %shard_map.41 = (bf16[8,392,128]{2,1,0:T(8,128)(2,1)S(1)}, f32[1,256]{1,0:T(1,128)S(1)}) custom-call(s32[1,256]{1,0:T(1,128)S(1)} %bitcast.14, bf16[256,768]{1,0:T(8,128)(2,1)S(1)} %copy-done.2), custom_call_target="tpu_custom_call" | custom-call | flops 201326592 | bytes 4000000 | tf_op jit(solution)/shard_map/pallas_call | solution.py:264
  3.5 21.0 %all_to_all.15.got_ref = bf16[8,392,128]{2,1,0:T(8,128)(2,1)S(1)} all-to-all(bf16[8,392,128]{2,1,0:T(8,128)(2,1)S(1)} %get-tuple-element.10), channel_id=1, replica_groups=mesh['rows_0'=2,'rows_1'=4,'cols_0'=2,'cols_1'=8,'cols_2'=2] {'rows_0','..., dimensions={0} | all-to-all | bytes 1605632 | tf_op jit(solution)/shard_map/all_to_all | solution.py:255
  24.5 1.4 %shard_map.42 = bf16[1024,768]{1,0:T(8,128)(2,1)S(1)} custom-call(bf16[8,392,128]{2,1,0:T(8,128)(2,1)S(1)} %all_to_all.15.got_ref), custom_call_target="tpu_custom_call" | custom-call | flops 805306368 | bytes 4000000 | tf_op jit(solution)/shard_map/pallas_call | solution.py:277
  25.9 49.4 %all_to_all.16 = bf16[32,32,768]{2,1,0:T(8,128)(2,1)S(1)} all-to-all(bf16[32,32,768]{2,1,0:T(8,128)(2,1)S(1)} %bitcast.11), channel_id=1, replica_groups=mesh['rows_0'=2,'rows_1'=4,'cols_0'=2,'cols_1'=8,'cols_2'=2] {'cols_0','..., dimensions={0} | all-to-all | bytes 3145728 | tf_op jit(solution)/shard_map/all_to_all | solution.py:255
  75.3 0.0 copy-start.1
  75.3 0.1 fusion
  75.4 2.5 %collective-permute-start.1 = (bf16[512,768]{1,0:T(8,128)(2,1)S(1)}, bf16[512,768]{1,0:T(8,128)(2,1)S(1)}, u32[]{:S(2)}, u32[]{:S(2)}) collective-permute-start(bf16[512,768]{1,0:T(8,128)(2,1)S(1)} %get-tuple-element.18), channel_id=1, source_target_pairs={{0,1},{1,0},{2,3},{3,2},{4,5},{5,4},{6,7},{7,6},{8,9},{9,8},{10,11... | collective-permute-start | bytes 2359304 | tf_op jit(solution)/shard_map/ppermute | solution.py:284
  77.9 0.1 collective-permute-start
  78.0 0.0 copy-done.1
  78.0 0.2 shard_map.46.index_ref
  78.2 1.8 %shard_map.43.so_far_ref = f32[8,1024]{1,0:T(8,128)S(1)} custom-call(bf16[1024,768]{1,0:T(8,128)(2,1)S(1)} %bitcast.8), custom_call_target="tpu_custom_call" | custom-call | flops 1610612736 | bytes 4000000 | tf_op jit(solution)/shard_map/pallas_call | solution.py:286
  80.1 0.0 collective-permute-done.1.other_ref
  80.1 1.0 %shard_map.44.so_far_ref = f32[8,1024]{1,0:T(8,128)S(1)} custom-call(bf16[1024,768]{1,0:T(8,128)(2,1)S(1)} %bitcast.9, bf16[512,768]{1,0:T(8,128)(2,1)S(1)} %collective-permute-done.1.other_ref, f32[8,1024]{1,0:T(8,128)S(1)} %shard_map.43.so_far_ref), custom_call_target="tpu_custom_call" | custom-call | flops 805306368 | bytes 4000000 | tf_op jit(solution)/shard_map/pallas_call | solution.py:287
  81.1 0.0 collective-permute-done.other_ref
  81.1 1.2 %shard_map.45 = bf16[512,128]{1,0:T(8,128)(2,1)S(1)} custom-call(bf16[1024,768]{1,0:T(8,128)(2,1)S(1)} %bitcast.10, bf16[512,768]{1,0:T(8,128)(2,1)S(1)} %collective-permute-done.other_ref, f32[8,1024]{1,0:T(8,128)S(1)} %shard_map.44.so_far_ref), custom_call_target="tpu_custom_call" | custom-call | flops 805306368 | bytes 4000000 | tf_op jit(solution)/shard_map/pallas_call | solution.py:289
  82.3 18.3 %all_to_all.17 = bf16[256,2,128]{2,1,0:T(2,128)(2,1)S(1)} all-to-all(bf16[256,2,128]{2,1,0:T(2,128)(2,1)S(1)} %bitcast.13), channel_id=1, replica_groups=mesh['rows_0'=2,'rows_1'=4,'cols_0'=2,'cols_1'=8,'cols_2'=2] {'rows_0','..., dimensions={0} | all-to-all | bytes 262144 | tf_op jit(solution)/shard_map/all_to_all | solution.py:255
  100.6 0.8 shard_map.47
Async XLA Ops:
  0.6 0.7 copy-start
  1.3 1.0 copy-start.2
  75.3 2.7 %copy-start.1 = (s32[256]{0:T(256)S(1)}, s32[256]{0:T(256)}, u32[]{:S(2)}) copy-start(s32[256]{0:T(256)} %param.3) | copy-start | bytes 3076
  75.4 4.6 %collective-permute-start.1 = (bf16[512,768]{1,0:T(8,128)(2,1)S(1)}, bf16[512,768]{1,0:T(8,128)(2,1)S(1)}, u32[]{:S(2)}, u32[]{:S(2)}) collective-permute-start(bf16[512,768]{1,0:T(8,128)(2,1)S(1)} %get-tuple-element.18), channel_id=1, source_target_pairs={{0,1},{1,0},{2,3},{3,2},{4,5},{5,4},{6,7},{7,6},{8,9},{9,8},{10,11... | collective-permute-start | bytes 2359304 | tf_op jit(solution)/shard_map/ppermute | solution.py:284
  77.9 3.1 %collective-permute-start = (bf16[512,768]{1,0:T(8,128)(2,1)S(1)}, bf16[512,768]{1,0:T(8,128)(2,1)S(1)}, u32[]{:S(2)}, u32[]{:S(2)}) collective-permute-start(bf16[512,768]{1,0:T(8,128)(2,1)S(1)} %get-tuple-element.19), channel_id=1, source_target_pairs={{0,1},{1,0},{2,3},{3,2},{4,5},{5,4},{6,7},{7,6},{8,9},{9,8},{10,11... | collective-permute-start | bytes 2359304 | tf_op jit(solution)/shard_map/ppermute | solution.py:284

commit v4 on v3

--- a/solution.py
+++ b/solution.py
@@ -11,7 +11,9 @@
 BINS = 128
 ROWS = ("rows_0", "rows_1")
 COLS = ("cols_0", "cols_1", "cols_2")
+CHIPS = ("cols_0", "cols_1")
 ALL = ROWS + COLS
+SAME_CORE = ROWS + CHIPS
 LANES = 128
 EMPTY = 2.0
 F32 = jnp.float32
@@ -170,12 +172,6 @@
     out_ref[...] = jnp.maximum(best_against(own_ref, other_ref, False), so_far_ref[...])
 
 
-def three_parts(x):
-    high = x.astype(BF16).astype(F32)
-    middle = (x - high).astype(BF16).astype(F32)
-    return high, middle, x - high - middle
-
-
 def best_last(own_ref, other_ref, so_far_ref, out_ref):
     total = own_ref.shape[0]
     best = jnp.maximum(best_against(own_ref, other_ref, False), so_far_ref[...])
@@ -190,44 +186,42 @@
     for s in range(LANES, total, LANES):
         folded = folded + weights[:, s : s + LANES]
     hist = jnp.sum(folded.T, axis=0, keepdims=True)
-    lines = jnp.concatenate([best[:, s : s + LANES] for s in range(0, total, LANES)], axis=0)
-    parts = three_parts(lines)
-    lane = iota((8, LANES), 1)
+    high = best.astype(BF16).astype(F32)
+    low = best - high
     sub = iota((8, LANES), 0)
-    quarters = []
-    for q in range(4):
-        line = jnp.zeros((8, LANES), F32)
-        for p in range(3):
-            shift = (32 * (p - q)) % LANES
-            moved = pltpu.roll(parts[p], shift, 1) if shift else parts[p]
-            line = jnp.where(lax.shift_right_logical(lane, 5) == p, moved, line)
-        quarters.append(line)
+    left = iota((1, LANES), 1) < CAP
     blocks = []
-    for s in range(total // LANES):
+    for s in range(0, total, 2 * LANES):
         block = jnp.broadcast_to(hist, (8, LANES))
-        for q in range(4):
-            block = jnp.where(sub == 2 * q + 1, quarters[q][s : s + 1, :], block)
+        for h in range(2):
+            at = s + h * LANES
+            top, rest = high[:, at : at + LANES], low[:, at : at + LANES]
+            first = jnp.where(left, top, pltpu.roll(rest, CAP, 1))
+            second = jnp.where(left, pltpu.roll(top, CAP, 1), rest)
+            block = jnp.where(sub == 4 * h + 1, first, block)
+            block = jnp.where(sub == 4 * h + 3, second, block)
         blocks.append(block)
     block = jnp.concatenate(blocks, axis=0).astype(BF16)
     for at in range(0, out_ref.shape[0], block.shape[0]):
         out_ref[at : at + block.shape[0], :] = block
 
 
-def pick_results(index_ref, got_ref, best_ref, hist_ref):
+def sum_histograms(got_ref, hist_ref):
+    lines = got_ref.shape[0]
+    even = ones_where(lax.bitwise_and(iota((8, lines), 1), 1) == 0)
+    hist_ref[...] = dot(even, got_ref[...])[0:1, :]
+
+
+def pick_results(index_ref, got_ref, best_ref):
     lines = got_ref.shape[0]
     docs = index_ref.shape[1]
     index = index_ref[...]
-    line = lax.shift_right_logical(index, 5) * 2 + 1
-    depth = lax.bitwise_and(index, 31)
+    line = lax.shift_right_logical(index, 6) * 2 + 1
+    rank = lax.bitwise_and(index, CAP - 1)
     onehot = ones_where(iota((lines, docs), 0) == line)
-    got = got_ref[...]
-    picked = dot(got.astype(F32).T.astype(BF16), onehot)
-    lane = iota((LANES, docs), 0)
-    wanted = (lax.bitwise_and(lane, 31) == depth) & (lane < 96)
+    picked = dot(got_ref[...].astype(F32).T.astype(BF16), onehot)
+    wanted = lax.bitwise_and(iota((LANES, docs), 0), CAP - 1) == rank
     best_ref[...] = jnp.sum(jnp.where(wanted, picked, 0.0), axis=0, keepdims=True)
-    even = ones_where(lax.bitwise_and(iota((8, lines), 1), 1) == 0)
-    hist = dot(even, got)[0:1, :]
-    hist_ref[...] = hist * (1.0 / (lines // 2 * docs))
 
 
 VMEM = pl.BlockSpec(memory_space=pltpu.VMEM)
@@ -249,6 +243,10 @@
 
 def shape(dims, dtype):
     return jax.ShapeDtypeStruct(dims, dtype)
+
+
+def in_hbm(x):
+    return pltpu.with_memory_space_constraint(x, pltpu.HBM)
 
 
 def exchange(x, axes):
@@ -271,30 +269,30 @@
             pltpu.VMEM((docs, width), BF16),
             pltpu.SemaphoreType.DMA((2,)),
         ],
-    )(labels, embeddings)
+    )(in_hbm(labels), in_hbm(embeddings))
     got = exchange(sends, ROWS)
     total = GROUP_CLUSTERS * CAP
     sends = call(reslot, shape((total, width), BF16), [VMEM], 2 * total * row_count * CAP * width)(
         got
     )
-    own = exchange(sends.reshape(col_count, total // col_count, width), COLS)
+    own = exchange(sends.reshape(GROUP_CLUSTERS, CAP, width), CHIPS)
     own, got = lax.optimization_barrier((own.reshape(total, width), got))
     pairs = [(i, i ^ 1) for i in range(col_count)]
     half = total // 2
     other = [lax.ppermute(own[s : s + half], COLS, pairs) for s in (0, half)]
     flops = 2 * total * half * width
+    lines = row_count * GROUP_CLUSTERS * 2
     best = call(best_own, shape((8, total), F32), [VMEM], 2 * flops)(own)
     best = call(best_more, shape((8, total), F32), [VMEM] * 3, flops)(own, other[0], best)
     index = call(return_index, shape((1, docs), jnp.int32), [VMEM] * 3, 2**26)(labels, rank, got)
-    results = call(best_last, shape((row_count * col_count * 2, LANES), BF16), [VMEM] * 3, flops)(
+    results = call(best_last, shape((lines, LANES), BF16), [VMEM] * 3, flops)(
         own, other[1], best
     )
     results, index = lax.optimization_barrier((results, index))
-    results = exchange(results.reshape(row_count * col_count, 2, LANES), ALL)
-    results = results.reshape(row_count * col_count * 2, LANES)
-    best, hist = call(
-        pick_results, (shape((1, docs), F32), shape((1, BINS), F32)), [VMEM, VMEM], 2**26
-    )(index, results)
+    results = exchange(results.reshape(lines // 2, 2, LANES), SAME_CORE).reshape(lines, LANES)
+    hist = call(sum_histograms, shape((1, BINS), F32), [VMEM], 2**24)(results)
+    hist = (hist + lax.ppermute(hist, COLS, pairs)) / (docs * row_count * col_count)
+    best = call(pick_results, shape((1, docs), F32), [VMEM, VMEM], 2**26)(index, results)
     return (best.reshape(docs), hist.reshape(BINS))
 
 

time: 102 us -> 98.1 us (0.962)
  blocking collectives: 88.7 us -> 83 us
  starting transfers between devices: 2.62 us -> 5.39 us
  local copies, waits for them, and re-layouts: 1.78 us -> 0.11 us
    all_to_all x3, blocking collectives: 88.7 us -> 83 us  [exchange(): return lax.all_to_all(x, axes, split_axis=0, concat_axis=0, tiled=True)]
    ppermute x0 -> x1, starting transfers between devices: none -> 1.87 us  [shards(): lax.ppermute(hist, COLS, pairs)]
    unnamed x6 -> x2, local copies, waits for them, and re-layouts: 1.67 us -> 0.01 us
    pallas_call x2 -> x3, Pallas kernels: 2.06 us -> 2.13 us  [the longest x1 1.21 us: shards(): call(best_last, shape((lines, LANES), BF16), [VMEM] * 3, flops)]
  transfers between devices with their start and end apart: 2 -> 3, of which waited for: 0 -> 0; matrix products, arithmetic and copies ran while one was open for 0% -> 0% of each run, Pallas kernels for 3% -> 4%
where the time goes in v4:
time: 98.1 us; the launch traced here: 97.9 us
  blocking collectives  83 us (85%)
  Pallas kernels  8.16 us (8%)
  starting transfers between devices  5.39 us (5%)
    all_to_all x3, blocking collectives, exchange(): return lax.all_to_all(x, axes, split_axis=0, concat_axis=0, tiled=True)  83 us
    ppermute x2, starting transfers between devices, shards(): other = [lax.ppermute(own[s:s + half], COLS, pairs) for s in (0, half)]  3.52 us
  transfers between devices with their start and end apart: 3, of which 0 were waited for; matrix products, arithmetic and copies ran while one was open for 0% of the time, Pallas kernels for 4%

profile of v4, /device:TPU:1, one launch (start us, length us, event | category | flops | bytes accessed | tf_op | source)
XLA Modules:
  0.0 97.9 jit_solution(2400011234814143945)
XLA Ops:
  0.6 1.6 %shard_map.41 = (bf16[8,392,128]{2,1,0:T(8,128)(2,1)S(1)}, f32[1,256]{1,0:T(1,128)S(1)}) custom-call(s32[1,256]{1,0:T(1,128)} %bitcast.16, bf16[256,768]{1,0:T(8,128)(2,1)} %embeddings_hbm.1), custom_call_target="tpu_custom_call" | custom-call | flops 201326592 | bytes 4000000 | tf_op jit(solution)/shard_map/pallas_call | solution.py:262
  2.3 21.0 %all_to_all.15.got_ref = bf16[8,392,128]{2,1,0:T(8,128)(2,1)S(1)} all-to-all(bf16[8,392,128]{2,1,0:T(8,128)(2,1)S(1)} %get-tuple-element.8), channel_id=1, replica_groups=mesh['rows_0'=2,'rows_1'=4,'cols_0'=2,'cols_1'=8,'cols_2'=2] {'rows_0','..., dimensions={0} | all-to-all | bytes 1605632 | tf_op jit(solution)/shard_map/all_to_all | solution.py:253
  23.3 1.4 %shard_map.42 = bf16[1024,768]{1,0:T(8,128)(2,1)S(1)} custom-call(bf16[8,392,128]{2,1,0:T(8,128)(2,1)S(1)} %all_to_all.15.got_ref), custom_call_target="tpu_custom_call" | custom-call | flops 805306368 | bytes 4000000 | tf_op jit(solution)/shard_map/pallas_call | solution.py:275
  24.7 43.4 %all_to_all.16 = bf16[16,64,768]{2,1,0:T(8,128)(2,1)S(1)} all-to-all(bf16[16,64,768]{2,1,0:T(8,128)(2,1)S(1)} %bitcast.12), channel_id=1, replica_groups=mesh['rows_0'=2,'rows_1'=4,'cols_0'=2,'cols_1'=8,'cols_2'=2] {'cols_0','..., dimensions={0} | all-to-all | bytes 3145728 | tf_op jit(solution)/shard_map/all_to_all | solution.py:253
  68.1 0.0 copy-start
  68.1 0.1 fusion
  68.2 3.4 %collective-permute-start.1 = (bf16[512,768]{1,0:T(8,128)(2,1)S(1)}, bf16[512,768]{1,0:T(8,128)(2,1)S(1)}, u32[]{:S(2)}, u32[]{:S(2)}) collective-permute-start(bf16[512,768]{1,0:T(8,128)(2,1)S(1)} %get-tuple-element.14), channel_id=1, source_target_pairs={{0,1},{1,0},{2,3},{3,2},{4,5},{5,4},{6,7},{7,6},{8,9},{9,8},{10,11... | collective-permute-start | bytes 2359304 | tf_op jit(solution)/shard_map/ppermute | solution.py:282
  71.6 0.1 collective-permute-start
  71.7 0.0 copy-done
  71.7 0.2 shard_map.46.index_ref
  71.9 1.8 %shard_map.43.so_far_ref = f32[8,1024]{1,0:T(8,128)S(1)} custom-call(bf16[1024,768]{1,0:T(8,128)(2,1)S(1)} %bitcast.9), custom_call_target="tpu_custom_call" | custom-call | flops 1610612736 | bytes 4000000 | tf_op jit(solution)/shard_map/pallas_call | solution.py:285
  73.7 0.0 collective-permute-done.1.other_ref
  73.7 1.0 %shard_map.44.so_far_ref = f32[8,1024]{1,0:T(8,128)S(1)} custom-call(bf16[1024,768]{1,0:T(8,128)(2,1)S(1)} %bitcast.10, bf16[512,768]{1,0:T(8,128)(2,1)S(1)} %collective-permute-done.1.other_ref, f32[8,1024]{1,0:T(8,128)S(1)} %shard_map.43.so_far_ref), custom_call_target="tpu_custom_call" | custom-call | flops 805306368 | bytes 4000000 | tf_op jit(solution)/shard_map/pallas_call | solution.py:286
  74.8 0.0 collective-permute-done.other_ref
  74.8 1.2 %shard_map.45 = bf16[256,128]{1,0:T(8,128)(2,1)S(1)} custom-call(bf16[1024,768]{1,0:T(8,128)(2,1)S(1)} %bitcast.11, bf16[512,768]{1,0:T(8,128)(2,1)S(1)} %collective-permute-done.other_ref, f32[8,1024]{1,0:T(8,128)S(1)} %shard_map.44.so_far_ref), custom_call_target="tpu_custom_call" | custom-call | flops 805306368 | bytes 4000000 | tf_op jit(solution)/shard_map/pallas_call | solution.py:288
  76.0 18.6 %all_to_all.17 = bf16[128,2,128]{2,1,0:T(2,128)(2,1)S(1)} all-to-all(bf16[128,2,128]{2,1,0:T(2,128)(2,1)S(1)} %bitcast.15), channel_id=1, replica_groups=mesh['rows_0'=2,'rows_1'=4,'cols_0'=2,'cols_1'=8,'cols_2'=2] {'rows_0','..., dimensions={0} | all-to-all | bytes 131072 | tf_op jit(solution)/shard_map/all_to_all | solution.py:253
  94.6 0.1 shard_map.48
  94.7 1.9 %collective-permute-start.2 = (f32[1,128]{1,0:T(1,128)S(1)}, f32[1,128]{1,0:T(1,128)S(1)}, u32[]{:S(2)}, u32[]{:S(2)}) collective-permute-start(f32[1,128]{1,0:T(1,128)S(1)} %shard_map.48), channel_id=1, source_target_pairs={{0,1},{1,0},{2,3},{3,2},{4,5},{5,4},{6,7},{7,6},{8,9},{9,8},{10,11... | collective-permute-start | bytes 1544 | tf_op jit(solution)/shard_map/ppermute | solution.py:294
  96.6 0.8 shard_map.47
  97.4 0.0 collective-permute-done.2
  97.4 0.5 multiply_bitcast_fusion
Async XLA Ops:
  68.1 3.6 %copy-start = (s32[256]{0:T(256)S(1)}, s32[256]{0:T(256)}, u32[]{:S(2)}) copy-start(s32[256]{0:T(256)} %param.3) | copy-start | bytes 3076
  68.2 5.5 %collective-permute-start.1 = (bf16[512,768]{1,0:T(8,128)(2,1)S(1)}, bf16[512,768]{1,0:T(8,128)(2,1)S(1)}, u32[]{:S(2)}, u32[]{:S(2)}) collective-permute-start(bf16[512,768]{1,0:T(8,128)(2,1)S(1)} %get-tuple-element.14), channel_id=1, source_target_pairs={{0,1},{1,0},{2,3},{3,2},{4,5},{5,4},{6,7},{7,6},{8,9},{9,8},{10,11... | collective-permute-start | bytes 2359304 | tf_op jit(solution)/shard_map/ppermute | solution.py:282
  71.6 3.1 %collective-permute-start = (bf16[512,768]{1,0:T(8,128)(2,1)S(1)}, bf16[512,768]{1,0:T(8,128)(2,1)S(1)}, u32[]{:S(2)}, u32[]{:S(2)}) collective-permute-start(bf16[512,768]{1,0:T(8,128)(2,1)S(1)} %get-tuple-element.15), channel_id=1, source_target_pairs={{0,1},{1,0},{2,3},{3,2},{4,5},{5,4},{6,7},{7,6},{8,9},{9,8},{10,11... | collective-permute-start | bytes 2359304 | tf_op jit(solution)/shard_map/ppermute | solution.py:282
  94.7 2.7 %collective-permute-start.2 = (f32[1,128]{1,0:T(1,128)S(1)}, f32[1,128]{1,0:T(1,128)S(1)}, u32[]{:S(2)}, u32[]{:S(2)}) collective-permute-start(f32[1,128]{1,0:T(1,128)S(1)} %shard_map.48), channel_id=1, source_target_pairs={{0,1},{1,0},{2,3},{3,2},{4,5},{5,4},{6,7},{7,6},{8,9},{9,8},{10,11... | collective-permute-start | bytes 1544 | tf_op jit(solution)/shard_map/ppermute | solution.py:294

commit v5 on v4

--- a/solution.py
+++ b/solution.py
@@ -15,6 +15,7 @@
 ALL = ROWS + COLS
 SAME_CORE = ROWS + CHIPS
 LANES = 128
+BLOCK = 256
 EMPTY = 2.0
 F32 = jnp.float32
 BF16 = jnp.bfloat16
@@ -146,46 +147,112 @@
     out_ref[...] = labels * CAP + (rank_ref[...] + earlier).astype(jnp.int32)
 
 
-def best_against(own_ref, other_ref, same):
-    block = 256
+def penalties(ref):
+    total, width = ref.shape
+    column = jnp.where(ref[:, 0:1].astype(F32) < 1.5, 0.0, -4.0)
+    pick = ones_where(iota((8, 256), 1) == 0)
+    row = jnp.where(dot_t(pick, ref[:, 0:256])[0:1, :] < 1.5, 0.0, -4.0)
+    return column, row
+
+
+def over_columns(scores):
+    return jnp.max(scores.reshape(BLOCK // 8, 8, BLOCK), axis=0)
+
+
+def over_rows(scores):
+    return jnp.maximum(scores[:, :LANES], scores[:, LANES:])
+
+
+def as_line(columns, rows):
     out = []
-    for j in range(0, own_ref.shape[0], block):
-        mine = own_ref[j : j + block, :]
-        best = jnp.full((8, block), -1.0, F32)
-        for i in range(0, other_ref.shape[0], block):
-            theirs = other_ref[i : i + block, :]
-            scores = dot_t(theirs, mine)
-            keep = theirs[:, 0:1].astype(F32) < 1.5
-            if same and i == j:
-                keep = keep & (iota((block, block), 0) != iota((block, block), 1))
-            scores = jnp.where(keep, scores, -1.0)
-            best = jnp.maximum(best, jnp.max(scores.reshape(block // 8, 8, block), axis=0))
-        out.append(best)
+    for column, row in zip(columns, rows):
+        line = jnp.max(column, axis=0, keepdims=True)
+        if row is not None:
+            turned = [jnp.max(row[h : h + LANES].T, axis=0, keepdims=True) for h in (0, LANES)]
+            line = jnp.maximum(line, jnp.concatenate(turned, axis=1))
+        out.append(line)
     return jnp.concatenate(out, axis=1)
 
 
-def best_own(own_ref, out_ref):
-    out_ref[...] = best_against(own_ref, own_ref, True)
-
-
-def best_more(own_ref, other_ref, so_far_ref, out_ref):
-    out_ref[...] = jnp.maximum(best_against(own_ref, other_ref, False), so_far_ref[...])
-
-
-def best_last(own_ref, other_ref, so_far_ref, out_ref):
-    total = own_ref.shape[0]
-    best = jnp.maximum(best_against(own_ref, other_ref, False), so_far_ref[...])
-    best = jnp.max(best, axis=0, keepdims=True)
-    pick = ones_where(iota((8, 256), 1) == 0)
-    flag = dot_t(pick, own_ref[:, 0:256])[0:1, :]
+def larger(a, b):
+    return b if a is None else jnp.maximum(a, b)
+
+
+def within(ref, penalty, columns, rows):
+    column, row = penalty
+    count = ref.shape[0] // BLOCK
+    for i in range(count):
+        for j in range(i, count):
+            at, to = i * BLOCK, j * BLOCK
+            scores = dot_t(ref[at : at + BLOCK, :], ref[to : to + BLOCK, :])
+            scores = scores + column[at : at + BLOCK] + row[:, to : to + BLOCK]
+            if i == j:
+                other = iota((BLOCK, BLOCK), 0) != iota((BLOCK, BLOCK), 1)
+                scores = jnp.where(other, scores, -4.0)
+            else:
+                rows[i] = larger(rows[i], over_rows(scores))
+            columns[j] = larger(columns[j], over_columns(scores))
+
+
+def between(a_ref, a_penalty, b_ref, b_penalty, rows, columns):
+    for i in range(a_ref.shape[0] // BLOCK):
+        for j in range(b_ref.shape[0] // BLOCK):
+            at, to = i * BLOCK, j * BLOCK
+            scores = dot_t(a_ref[at : at + BLOCK, :], b_ref[to : to + BLOCK, :])
+            scores = scores + a_penalty[0][at : at + BLOCK] + b_penalty[1][:, to : to + BLOCK]
+            rows[i] = larger(rows[i], over_rows(scores))
+            columns[j] = larger(columns[j], over_columns(scores))
+
+
+def nothing(ref):
+    return [None] * (ref.shape[0] // BLOCK)
+
+
+def best_own(own_ref, best_ref):
+    columns, rows = nothing(own_ref), nothing(own_ref)
+    within(own_ref, penalties(own_ref), columns, rows)
+    best_ref[...] = jnp.maximum(as_line(columns, rows), -1.0)
+
+
+def best_more(own_ref, more_ref, so_far_ref, best_ref, best_more_ref):
+    columns, rows, of_own = nothing(more_ref), nothing(more_ref), nothing(own_ref)
+    penalty = penalties(more_ref)
+    between(more_ref, penalty, own_ref, penalties(own_ref), rows, of_own)
+    within(more_ref, penalty, columns, rows)
+    best_more_ref[...] = as_line(columns, rows)
+    best_ref[...] = jnp.maximum(as_line(of_own, nothing(own_ref)), so_far_ref[...])
+
+
+def histogram_parts(best, penalty):
     width = 2.0 / (BINS - 1)
     centers = -1.0 + iota((BINS, 1), 0).astype(F32) * width
     weights = jnp.maximum(1.0 - jnp.abs(best - centers) / width, 0.0)
-    weights = jnp.where(flag < 1.5, weights, 0.0)
+    weights = jnp.where(penalty < 0.0, 0.0, weights)
     folded = weights[:, 0:LANES]
-    for s in range(LANES, total, LANES):
+    for s in range(LANES, best.shape[1], LANES):
         folded = folded + weights[:, s : s + LANES]
-    hist = jnp.sum(folded.T, axis=0, keepdims=True)
+    return folded
+
+
+def best_last(own_ref, more_ref, last_ref, so_far_ref, more_so_far_ref, out_ref):
+    total = own_ref.shape[0]
+    own_penalty, more_penalty = penalties(own_ref), penalties(more_ref)
+    penalty = penalties(last_ref)
+    columns, rows, of_own = nothing(last_ref), nothing(last_ref), nothing(own_ref)
+    of_more = nothing(more_ref)
+    between(more_ref, more_penalty, last_ref, penalty, of_more, columns)
+    between(last_ref, penalty, own_ref, own_penalty, rows, of_own)
+    within(last_ref, penalty, columns, rows)
+    best = jnp.maximum(as_line(of_own, nothing(own_ref)), so_far_ref[...])
+    more_line = [more_so_far_ref[:, s : s + BLOCK] for s in range(0, more_ref.shape[0], BLOCK)]
+    more_best = jnp.maximum(as_line(more_line, of_more), -1.0)
+    last_best = jnp.maximum(as_line(columns, rows), -1.0)
+    mine = histogram_parts(best, own_penalty[1])
+    theirs = histogram_parts(
+        jnp.concatenate([more_best, last_best], axis=1),
+        jnp.concatenate([more_penalty[1], penalty[1]], axis=1),
+    )
+    hist = jnp.sum((mine + theirs).T, axis=0, keepdims=True)
     high = best.astype(BF16).astype(F32)
     low = best - high
     sub = iota((8, LANES), 0)
@@ -206,22 +273,19 @@
         out_ref[at : at + block.shape[0], :] = block
 
 
-def sum_histograms(got_ref, hist_ref):
-    lines = got_ref.shape[0]
-    even = ones_where(lax.bitwise_and(iota((8, lines), 1), 1) == 0)
-    hist_ref[...] = dot(even, got_ref[...])[0:1, :]
-
-
-def pick_results(index_ref, got_ref, best_ref):
+def pick_results(index_ref, got_ref, best_ref, hist_ref):
     lines = got_ref.shape[0]
     docs = index_ref.shape[1]
     index = index_ref[...]
     line = lax.shift_right_logical(index, 6) * 2 + 1
     rank = lax.bitwise_and(index, CAP - 1)
     onehot = ones_where(iota((lines, docs), 0) == line)
-    picked = dot(got_ref[...].astype(F32).T.astype(BF16), onehot)
+    got = got_ref[...]
+    picked = dot(got.astype(F32).T.astype(BF16), onehot)
     wanted = lax.bitwise_and(iota((LANES, docs), 0), CAP - 1) == rank
     best_ref[...] = jnp.sum(jnp.where(wanted, picked, 0.0), axis=0, keepdims=True)
+    even = ones_where(lax.bitwise_and(iota((8, lines), 1), 1) == 0)
+    hist_ref[...] = dot(even, got)[0:1, :] * (1.0 / (lines * docs))
 
 
 VMEM = pl.BlockSpec(memory_space=pltpu.VMEM)
@@ -282,17 +346,18 @@
     other = [lax.ppermute(own[s : s + half], COLS, pairs) for s in (0, half)]
     flops = 2 * total * half * width
     lines = row_count * GROUP_CLUSTERS * 2
-    best = call(best_own, shape((8, total), F32), [VMEM], 2 * flops)(own)
-    best = call(best_more, shape((8, total), F32), [VMEM] * 3, flops)(own, other[0], best)
+    whole, part = shape((1, total), F32), shape((1, half), F32)
+    best = call(best_own, whole, [VMEM], flops)(own)
+    best, more = call(best_more, (whole, part), [VMEM] * 3, flops)(own, other[0], best)
     index = call(return_index, shape((1, docs), jnp.int32), [VMEM] * 3, 2**26)(labels, rank, got)
-    results = call(best_last, shape((lines, LANES), BF16), [VMEM] * 3, flops)(
-        own, other[1], best
+    results = call(best_last, shape((lines, LANES), BF16), [VMEM] * 5, 2 * flops)(
+        own, other[0], other[1], best, more
     )
     results, index = lax.optimization_barrier((results, index))
     results = exchange(results.reshape(lines // 2, 2, LANES), SAME_CORE).reshape(lines, LANES)
-    hist = call(sum_histograms, shape((1, BINS), F32), [VMEM], 2**24)(results)
-    hist = (hist + lax.ppermute(hist, COLS, pairs)) / (docs * row_count * col_count)
-    best = call(pick_results, shape((1, docs), F32), [VMEM, VMEM], 2**26)(index, results)
+    best, hist = call(
+        pick_results, (shape((1, docs), F32), shape((1, BINS), F32)), [VMEM, VMEM], 2**26
+    )(index, results)
     return (best.reshape(docs), hist.reshape(BINS))
 
 

time: 98.1 us -> 97.1 us (0.990)
  starting transfers between devices: 5.39 us -> 3.52 us
  Pallas kernels: 8.16 us -> 9.47 us
    ppermute x1 -> x0, starting transfers between devices: 1.87 us -> none  [shards(): lax.ppermute(hist, COLS, pairs)]
    pallas_call x5 -> x4, Pallas kernels: 4.99 us -> 6.3 us  [the longest x1 2.36 us: shards(): call(best_last, shape((lines, LANES), BF16), [VMEM] * 5, 2 * flops)]
  transfers between devices with their start and end apart: 3 -> 2, of which waited for: 0 -> 1; matrix products, arithmetic and copies ran while one was open for 0% -> 0% of each run, Pallas kernels for 4% -> 3%
where the time goes in v5:
time: 97.1 us; the launch traced here: 96.9 us
  blocking collectives  83 us (85%)
  Pallas kernels  9.47 us (10%)
  starting transfers between devices  3.52 us (4%)
    all_to_all x3, blocking collectives, exchange(): return lax.all_to_all(x, axes, split_axis=0, concat_axis=0, tiled=True)  83 us
    ppermute x2, starting transfers between devices, shards(): other = [lax.ppermute(own[s:s + half], COLS, pairs) for s in (0, half)]  3.52 us
    pallas_call x1, Pallas kernels, shards(): call(best_last, shape((lines, LANES), BF16), [VMEM] * 5, 2 * flops)  2.36 us
  transfers between devices with their start and end apart: 2, of which 1 were waited for; matrix products, arithmetic and copies ran while one was open for 0% of the time, Pallas kernels for 3%

profile of v5, /device:TPU:1, one launch (start us, length us, event | category | flops | bytes accessed | tf_op | source)
XLA Modules:
  0.0 96.9 jit_solution(13052353387843014745)
XLA Ops:
  0.6 1.6 %shard_map.41 = (bf16[8,392,128]{2,1,0:T(8,128)(2,1)S(1)}, f32[1,256]{1,0:T(1,128)S(1)}) custom-call(s32[1,256]{1,0:T(1,128)} %bitcast.14, bf16[256,768]{1,0:T(8,128)(2,1)} %embeddings_hbm.1), custom_call_target="tpu_custom_call" | custom-call | flops 201326592 | bytes 4000000 | tf_op jit(solution)/shard_map/pallas_call | solution.py:326
  2.3 21.0 %all_to_all.15.got_ref = bf16[8,392,128]{2,1,0:T(8,128)(2,1)S(1)} all-to-all(bf16[8,392,128]{2,1,0:T(8,128)(2,1)S(1)} %get-tuple-element.12), channel_id=1, replica_groups=mesh['rows_0'=2,'rows_1'=4,'cols_0'=2,'cols_1'=8,'cols_2'=2] {'rows_0','..., dimensions={0} | all-to-all | bytes 1605632 | tf_op jit(solution)/shard_map/all_to_all | solution.py:317
  23.3 1.4 %shard_map.42 = bf16[1024,768]{1,0:T(8,128)(2,1)S(1)} custom-call(bf16[8,392,128]{2,1,0:T(8,128)(2,1)S(1)} %all_to_all.15.got_ref), custom_call_target="tpu_custom_call" | custom-call | flops 805306368 | bytes 4000000 | tf_op jit(solution)/shard_map/pallas_call | solution.py:339
  24.7 43.4 %all_to_all.16 = bf16[16,64,768]{2,1,0:T(8,128)(2,1)S(1)} all-to-all(bf16[16,64,768]{2,1,0:T(8,128)(2,1)S(1)} %bitcast.11), channel_id=1, replica_groups=mesh['rows_0'=2,'rows_1'=4,'cols_0'=2,'cols_1'=8,'cols_2'=2] {'cols_0','..., dimensions={0} | all-to-all | bytes 3145728 | tf_op jit(solution)/shard_map/all_to_all | solution.py:317
  68.1 0.0 copy-start
  68.1 0.1 fusion
  68.2 3.4 %collective-permute-start = (bf16[512,768]{1,0:T(8,128)(2,1)S(1)}, bf16[512,768]{1,0:T(8,128)(2,1)S(1)}, u32[]{:S(2)}, u32[]{:S(2)}) collective-permute-start(bf16[512,768]{1,0:T(8,128)(2,1)S(1)} %get-tuple-element.23), channel_id=1, source_target_pairs={{0,1},{1,0},{2,3},{3,2},{4,5},{5,4},{6,7},{7,6},{8,9},{9,8},{10,11... | collective-permute-start | bytes 2359304 | tf_op jit(solution)/shard_map/ppermute | solution.py:346
  71.6 0.1 collective-permute-start.1
  71.7 0.0 copy-done
  71.7 0.2 shard_map.46.index_ref
  71.9 1.5 %shard_map.43.so_far_ref = f32[1,1024]{1,0:T(1,128)S(1)} custom-call(bf16[1024,768]{1,0:T(8,128)(2,1)S(1)} %bitcast.8), custom_call_target="tpu_custom_call" | custom-call | flops 805306368 | bytes 4000000 | tf_op jit(solution)/shard_map/pallas_call | solution.py:350
  73.4 0.2 collective-permute-done.more_ref
  73.5 1.7 %shard_map.44 = (f32[1,1024]{1,0:T(1,128)S(1)}, f32[1,512]{1,0:T(1,128)S(1)}) custom-call(bf16[1024,768]{1,0:T(8,128)(2,1)S(1)} %bitcast.9, bf16[512,768]{1,0:T(8,128)(2,1)S(1)} %collective-permute-done.more_ref, f32[1,1024]{1,0:T(1,128)S(1)} %shard_map.43.so_far_ref), custom_call_target="tpu_custom_call" | custom-call | flops 805306368 | bytes 4000000 | tf_op jit(solution)/shard_map/pallas_call | solution.py:351
  75.2 0.0 collective-permute-done.1.last_ref
  75.2 2.4 %shard_map.45 = bf16[256,128]{1,0:T(8,128)(2,1)S(1)} custom-call(bf16[1024,768]{1,0:T(8,128)(2,1)S(1)} %bitcast.10, bf16[512,768]{1,0:T(8,128)(2,1)S(1)} %collective-permute-done.more_ref, bf16[512,768]{1,0:T(8,128)(2,1)S(1)} %collective-permute-done.1.last_ref, f32[1,1024]{1,0:T(1,128)S(1)} %get-tuple-element.14.so_far_ref, ...), custom_call_target="tpu_custom_call" | custom-call | flops 1610612736 | bytes 4000000 | tf_op jit(solution)/shard_map/pallas_call | solution.py:353
  77.6 18.6 %all_to_all.17 = bf16[128,2,128]{2,1,0:T(2,128)(2,1)S(1)} all-to-all(bf16[128,2,128]{2,1,0:T(2,128)(2,1)S(1)} %bitcast.12), channel_id=1, replica_groups=mesh['rows_0'=2,'rows_1'=4,'cols_0'=2,'cols_1'=8,'cols_2'=2] {'rows_0','..., dimensions={0} | all-to-all | bytes 131072 | tf_op jit(solution)/shard_map/all_to_all | solution.py:317
  96.1 0.8 shard_map.47
Async XLA Ops:
  68.1 3.6 %copy-start = (s32[256]{0:T(256)S(1)}, s32[256]{0:T(256)}, u32[]{:S(2)}) copy-start(s32[256]{0:T(256)} %param.3) | copy-start | bytes 3076
  68.2 5.3 %collective-permute-start = (bf16[512,768]{1,0:T(8,128)(2,1)S(1)}, bf16[512,768]{1,0:T(8,128)(2,1)S(1)}, u32[]{:S(2)}, u32[]{:S(2)}) collective-permute-start(bf16[512,768]{1,0:T(8,128)(2,1)S(1)} %get-tuple-element.23), channel_id=1, source_target_pairs={{0,1},{1,0},{2,3},{3,2},{4,5},{5,4},{6,7},{7,6},{8,9},{9,8},{10,11... | collective-permute-start | bytes 2359304 | tf_op jit(solution)/shard_map/ppermute | solution.py:346
  71.6 3.6 %collective-permute-start.1 = (bf16[512,768]{1,0:T(8,128)(2,1)S(1)}, bf16[512,768]{1,0:T(8,128)(2,1)S(1)}, u32[]{:S(2)}, u32[]{:S(2)}) collective-permute-start(bf16[512,768]{1,0:T(8,128)(2,1)S(1)} %get-tuple-element.22), channel_id=1, source_target_pairs={{0,1},{1,0},{2,3},{3,2},{4,5},{5,4},{6,7},{7,6},{8,9},{9,8},{10,11... | collective-permute-start | bytes 2359304 | tf_op jit(solution)/shard_map/ppermute | solution.py:346

commit v6 on v5

--- a/solution.py
+++ b/solution.py
@@ -19,6 +19,10 @@
 EMPTY = 2.0
 F32 = jnp.float32
 BF16 = jnp.bfloat16
+WIRE = jnp.float16
+HIGH_SCALE = 2.0**10
+LOW_SCALE = 2.0**18
+HIST_SCALE = 16.0
 
 
 def iota(shape, dim):
@@ -254,7 +258,9 @@
     )
     hist = jnp.sum((mine + theirs).T, axis=0, keepdims=True)
     high = best.astype(BF16).astype(F32)
-    low = best - high
+    low = (best - high) * LOW_SCALE
+    high = high * HIGH_SCALE
+    hist = hist * HIST_SCALE
     sub = iota((8, LANES), 0)
     left = iota((1, LANES), 1) < CAP
     blocks = []
@@ -268,7 +274,7 @@
             block = jnp.where(sub == 4 * h + 1, first, block)
             block = jnp.where(sub == 4 * h + 3, second, block)
         blocks.append(block)
-    block = jnp.concatenate(blocks, axis=0).astype(BF16)
+    block = jnp.concatenate(blocks, axis=0)
     for at in range(0, out_ref.shape[0], block.shape[0]):
         out_ref[at : at + block.shape[0], :] = block
 
@@ -281,11 +287,19 @@
     rank = lax.bitwise_and(index, CAP - 1)
     onehot = ones_where(iota((lines, docs), 0) == line)
     got = got_ref[...]
-    picked = dot(got.astype(F32).T.astype(BF16), onehot)
-    wanted = lax.bitwise_and(iota((LANES, docs), 0), CAP - 1) == rank
+    turned = got.T
+    high = turned.astype(BF16)
+    low = (turned - high.astype(F32)).astype(BF16)
+    picked = dot(high, onehot) + dot(low, onehot)
+    lane = iota((LANES, docs), 0)
+    picked = picked * jnp.where(lane < CAP, 1.0 / HIGH_SCALE, 1.0 / LOW_SCALE)
+    wanted = lax.bitwise_and(lane, CAP - 1) == rank
     best_ref[...] = jnp.sum(jnp.where(wanted, picked, 0.0), axis=0, keepdims=True)
-    even = ones_where(lax.bitwise_and(iota((8, lines), 1), 1) == 0)
-    hist_ref[...] = dot(even, got)[0:1, :] * (1.0 / (lines * docs))
+    even = lax.bitwise_and(iota((8, LANES), 0), 1) == 0
+    total = jnp.zeros((8, LANES), F32)
+    for s in range(0, lines, 8):
+        total = total + jnp.where(even, got[s : s + 8, :], 0.0)
+    hist_ref[...] = jnp.sum(total, axis=0, keepdims=True) * (1.0 / (HIST_SCALE * lines * docs))
 
 
 VMEM = pl.BlockSpec(memory_space=pltpu.VMEM)
@@ -350,11 +364,12 @@
     best = call(best_own, whole, [VMEM], flops)(own)
     best, more = call(best_more, (whole, part), [VMEM] * 3, flops)(own, other[0], best)
     index = call(return_index, shape((1, docs), jnp.int32), [VMEM] * 3, 2**26)(labels, rank, got)
-    results = call(best_last, shape((lines, LANES), BF16), [VMEM] * 5, 2 * flops)(
+    results = call(best_last, shape((lines, LANES), F32), [VMEM] * 5, 2 * flops)(
         own, other[0], other[1], best, more
     )
     results, index = lax.optimization_barrier((results, index))
-    results = exchange(results.reshape(lines // 2, 2, LANES), SAME_CORE).reshape(lines, LANES)
+    results = exchange(results.astype(WIRE).reshape(lines // 2, 2, LANES), SAME_CORE)
+    results = results.reshape(lines, LANES).astype(F32)
     best, hist = call(
         pick_results, (shape((1, docs), F32), shape((1, BINS), F32)), [VMEM, VMEM], 2**26
     )(index, results)

time: 97.1 us -> 97.2 us (level)
  no operation moved by 1% of the time
where the time goes in v6:
time: 97.2 us; the launch traced here: 97 us
  blocking collectives  83 us (85%)
  Pallas kernels  9.49 us (10%)
  starting transfers between devices  3.52 us (4%)
    all_to_all x3, blocking collectives, exchange(): return lax.all_to_all(x, axes, split_axis=0, concat_axis=0, tiled=True)  83 us
    ppermute x2, starting transfers between devices, shards(): other = [lax.ppermute(own[s:s + half], COLS, pairs) for s in (0, half)]  3.52 us
    pallas_call x1, Pallas kernels, shards(): call(best_last, shape((lines, LANES), F32), [VMEM] * 5, 2 * flops)  2.36 us
  transfers between devices with their start and end apart: 2, of which 1 were waited for; matrix products, arithmetic and copies ran while one was open for 0% of the time, Pallas kernels for 3%

profile of v6, /device:TPU:1, one launch (start us, length us, event | category | flops | bytes accessed | tf_op | source)
XLA Modules:
  0.0 97.0 jit_solution(11470198047350905342)
XLA Ops:
  0.6 1.6 %shard_map.41 = (bf16[8,392,128]{2,1,0:T(8,128)(2,1)S(1)}, f32[1,256]{1,0:T(1,128)S(1)}) custom-call(s32[1,256]{1,0:T(1,128)} %bitcast.13, bf16[256,768]{1,0:T(8,128)(2,1)} %embeddings_hbm.1), custom_call_target="tpu_custom_call" | custom-call | flops 201326592 | bytes 4000000 | tf_op jit(solution)/shard_map/pallas_call | solution.py:340
  2.3 21.0 %all_to_all.15.got_ref = bf16[8,392,128]{2,1,0:T(8,128)(2,1)S(1)} all-to-all(bf16[8,392,128]{2,1,0:T(8,128)(2,1)S(1)} %get-tuple-element.12), channel_id=1, replica_groups=mesh['rows_0'=2,'rows_1'=4,'cols_0'=2,'cols_1'=8,'cols_2'=2] {'rows_0','..., dimensions={0} | all-to-all | bytes 1605632 | tf_op jit(solution)/shard_map/all_to_all | solution.py:331
  23.3 1.4 %shard_map.42 = bf16[1024,768]{1,0:T(8,128)(2,1)S(1)} custom-call(bf16[8,392,128]{2,1,0:T(8,128)(2,1)S(1)} %all_to_all.15.got_ref), custom_call_target="tpu_custom_call" | custom-call | flops 805306368 | bytes 4000000 | tf_op jit(solution)/shard_map/pallas_call | solution.py:353
  24.7 43.4 %all_to_all.16 = bf16[16,64,768]{2,1,0:T(8,128)(2,1)S(1)} all-to-all(bf16[16,64,768]{2,1,0:T(8,128)(2,1)S(1)} %bitcast.12), channel_id=1, replica_groups=mesh['rows_0'=2,'rows_1'=4,'cols_0'=2,'cols_1'=8,'cols_2'=2] {'cols_0','..., dimensions={0} | all-to-all | bytes 3145728 | tf_op jit(solution)/shard_map/all_to_all | solution.py:331
  68.1 0.0 copy-start
  68.1 0.1 fusion
  68.2 3.4 %collective-permute-start = (bf16[512,768]{1,0:T(8,128)(2,1)S(1)}, bf16[512,768]{1,0:T(8,128)(2,1)S(1)}, u32[]{:S(2)}, u32[]{:S(2)}) collective-permute-start(bf16[512,768]{1,0:T(8,128)(2,1)S(1)} %get-tuple-element.23), channel_id=1, source_target_pairs={{0,1},{1,0},{2,3},{3,2},{4,5},{5,4},{6,7},{7,6},{8,9},{9,8},{10,11... | collective-permute-start | bytes 2359304 | tf_op jit(solution)/shard_map/ppermute | solution.py:360
  71.6 0.1 collective-permute-start.1
  71.7 0.0 copy-done
  71.7 0.2 shard_map.46.index_ref
  71.9 1.5 %shard_map.43.so_far_ref = f32[1,1024]{1,0:T(1,128)S(1)} custom-call(bf16[1024,768]{1,0:T(8,128)(2,1)S(1)} %bitcast.9), custom_call_target="tpu_custom_call" | custom-call | flops 805306368 | bytes 4000000 | tf_op jit(solution)/shard_map/pallas_call | solution.py:364
  73.4 0.2 collective-permute-done.more_ref
  73.5 1.7 %shard_map.44 = (f32[1,1024]{1,0:T(1,128)S(1)}, f32[1,512]{1,0:T(1,128)S(1)}) custom-call(bf16[1024,768]{1,0:T(8,128)(2,1)S(1)} %bitcast.10, bf16[512,768]{1,0:T(8,128)(2,1)S(1)} %collective-permute-done.more_ref, f32[1,1024]{1,0:T(1,128)S(1)} %shard_map.43.so_far_ref), custom_call_target="tpu_custom_call" | custom-call | flops 805306368 | bytes 4000000 | tf_op jit(solution)/shard_map/pallas_call | solution.py:365
  75.2 0.0 collective-permute-done.1.last_ref
  75.2 2.4 %shard_map.45 = f32[256,128]{1,0:T(8,128)S(1)} custom-call(bf16[1024,768]{1,0:T(8,128)(2,1)S(1)} %bitcast.11, bf16[512,768]{1,0:T(8,128)(2,1)S(1)} %collective-permute-done.more_ref, bf16[512,768]{1,0:T(8,128)(2,1)S(1)} %collective-permute-done.1.last_ref, f32[1,1024]{1,0:T(1,128)S(1)} %get-tuple-element.14.so_far_ref, ...), custom_call_target="tpu_custom_call" | custom-call | flops 1610612736 | bytes 4000000 | tf_op jit(solution)/shard_map/pallas_call | solution.py:367
  77.6 18.6 %all_to_all.17 = f16[128,2,128]{2,1,0:T(2,128)(2,1)S(1)} all-to-all(f16[128,2,128]{2,1,0:T(2,128)(2,1)S(1)} %bitcast.15), channel_id=1, replica_groups=mesh['rows_0'=2,'rows_1'=4,'cols_0'=2,'cols_1'=8,'cols_2'=2] {'rows_0','..., dimensions={0} | all-to-all | bytes 131072 | tf_op jit(solution)/shard_map/all_to_all | solution.py:331
  96.2 0.8 shard_map.47
  (2 shorter events, 0.0 us)
Async XLA Ops:
  68.1 3.6 %copy-start = (s32[256]{0:T(256)S(1)}, s32[256]{0:T(256)}, u32[]{:S(2)}) copy-start(s32[256]{0:T(256)} %param.3) | copy-start | bytes 3076
  68.2 5.3 %collective-permute-start = (bf16[512,768]{1,0:T(8,128)(2,1)S(1)}, bf16[512,768]{1,0:T(8,128)(2,1)S(1)}, u32[]{:S(2)}, u32[]{:S(2)}) collective-permute-start(bf16[512,768]{1,0:T(8,128)(2,1)S(1)} %get-tuple-element.23), channel_id=1, source_target_pairs={{0,1},{1,0},{2,3},{3,2},{4,5},{5,4},{6,7},{7,6},{8,9},{9,8},{10,11... | collective-permute-start | bytes 2359304 | tf_op jit(solution)/shard_map/ppermute | solution.py:360
  71.6 3.6 %collective-permute-start.1 = (bf16[512,768]{1,0:T(8,128)(2,1)S(1)}, bf16[512,768]{1,0:T(8,128)(2,1)S(1)}, u32[]{:S(2)}, u32[]{:S(2)}) collective-permute-start(bf16[512,768]{1,0:T(8,128)(2,1)S(1)} %get-tuple-element.22), channel_id=1, source_target_pairs={{0,1},{1,0},{2,3},{3,2},{4,5},{5,4},{6,7},{7,6},{8,9},{9,8},{10,11... | collective-permute-start | bytes 2359304 | tf_op jit(solution)/shard_map/ppermute | solution.py:360

commit v7 on v6

--- a/solution.py
+++ b/solution.py
@@ -212,10 +212,34 @@
     return [None] * (ref.shape[0] // BLOCK)
 
 
-def best_own(own_ref, best_ref):
+def best_of(own_ref):
     columns, rows = nothing(own_ref), nothing(own_ref)
     within(own_ref, penalties(own_ref), columns, rows)
-    best_ref[...] = jnp.maximum(as_line(columns, rows), -1.0)
+    return jnp.maximum(as_line(columns, rows), -1.0)
+
+
+def best_own_early(own_ref, best_ref):
+    early = lax.axis_index("cols_2") == 1
+
+    @pl.when(early)
+    def _():
+        best_ref[...] = best_of(own_ref)
+
+    @pl.when(jnp.logical_not(early))
+    def _():
+        best_ref[...] = jnp.full(best_ref.shape, -1.0, F32)
+
+
+def best_own_late(own_ref, early_ref, best_ref):
+    early = lax.axis_index("cols_2") == 1
+
+    @pl.when(early)
+    def _():
+        best_ref[...] = early_ref[...]
+
+    @pl.when(jnp.logical_not(early))
+    def _():
+        best_ref[...] = best_of(own_ref)
 
 
 def best_more(own_ref, more_ref, so_far_ref, best_ref, best_more_ref):
@@ -229,9 +253,8 @@
 
 def histogram_parts(best, penalty):
     width = 2.0 / (BINS - 1)
-    centers = -1.0 + iota((BINS, 1), 0).astype(F32) * width
-    weights = jnp.maximum(1.0 - jnp.abs(best - centers) / width, 0.0)
-    weights = jnp.where(penalty < 0.0, 0.0, weights)
+    at = jnp.where(penalty < 0.0, 2.0 * BINS, (best + 1.0) * (1.0 / width))
+    weights = jnp.maximum(1.0 - jnp.abs(at - iota((BINS, 1), 0).astype(F32)), 0.0)
     folded = weights[:, 0:LANES]
     for s in range(LANES, best.shape[1], LANES):
         folded = folded + weights[:, s : s + LANES]
@@ -355,13 +378,15 @@
     )
     own = exchange(sends.reshape(GROUP_CLUSTERS, CAP, width), CHIPS)
     own, got = lax.optimization_barrier((own.reshape(total, width), got))
+    whole, part = shape((1, total), F32), shape((1, total // 2), F32)
+    flops = 2 * total * total // 2 * width
+    early = call(best_own_early, whole, [VMEM], flops)(own)
+    own, early = lax.optimization_barrier((own, early))
     pairs = [(i, i ^ 1) for i in range(col_count)]
     half = total // 2
     other = [lax.ppermute(own[s : s + half], COLS, pairs) for s in (0, half)]
-    flops = 2 * total * half * width
     lines = row_count * GROUP_CLUSTERS * 2
-    whole, part = shape((1, total), F32), shape((1, half), F32)
-    best = call(best_own, whole, [VMEM], flops)(own)
+    best = call(best_own_late, whole, [VMEM] * 2, flops)(own, early)
     best, more = call(best_more, (whole, part), [VMEM] * 3, flops)(own, other[0], best)
     index = call(return_index, shape((1, docs), jnp.int32), [VMEM] * 3, 2**26)(labels, rank, got)
     results = call(best_last, shape((lines, LANES), F32), [VMEM] * 5, 2 * flops)(

time: 97.2 us -> 97.2 us (level)
  starting transfers between devices: 3.52 us -> 2.01 us
  waiting for transfers between devices: 0.16 us -> 1.64 us
    ppermute x2, starting transfers between devices: 3.52 us -> 2.01 us  [shards(): other = [lax.ppermute(own[s:s + half], COLS, pairs) for s in (0, half)]]
    ppermute x2, waiting for transfers between devices: 0.16 us -> 1.64 us  [shards(): other = [lax.ppermute(own[s:s + half], COLS, pairs) for s in (0, half)]]
  transfers between devices with their start and end apart: 2 -> 2, of which waited for: 1 -> 1; matrix products, arithmetic and copies ran while one was open for 0% -> 0% of each run, Pallas kernels for 3% -> 2%
where the time goes in v7:
time: 97.2 us; the launch traced here: 97 us
  blocking collectives  83.1 us (85%)
  Pallas kernels  9.48 us (10%)
  starting transfers between devices  2.01 us (2%)
  waiting for transfers between devices  1.64 us (2%)
    all_to_all x3, blocking collectives, exchange(): return lax.all_to_all(x, axes, split_axis=0, concat_axis=0, tiled=True)  83.1 us
    pallas_call x1, Pallas kernels, shards(): call(best_last, shape((lines, LANES), F32), [VMEM] * 5, 2 * flops)  2.35 us
    ppermute x2, starting transfers between devices, shards(): other = [lax.ppermute(own[s:s + half], COLS, pairs) for s in (0, half)]  2.01 us
  transfers between devices with their start and end apart: 2, of which 1 were waited for; matrix products, arithmetic and copies ran while one was open for 0% of the time, Pallas kernels for 2%

profile of v7, /device:TPU:1, one launch (start us, length us, event | category | flops | bytes accessed | tf_op | source)
XLA Modules:
  0.0 97.0 jit_solution(510057361156358196)
XLA Ops:
  0.6 1.6 %shard_map.41 = (bf16[8,392,128]{2,1,0:T(8,128)(2,1)S(1)}, f32[1,256]{1,0:T(1,128)S(1)}) custom-call(s32[1,256]{1,0:T(1,128)} %bitcast.14, bf16[256,768]{1,0:T(8,128)(2,1)} %embeddings_hbm.1), custom_call_target="tpu_custom_call" | custom-call | flops 201326592 | bytes 4000000 | tf_op jit(solution)/shard_map/pallas_call | solution.py:363
  2.3 21.0 %all_to_all.15.got_ref = bf16[8,392,128]{2,1,0:T(8,128)(2,1)S(1)} all-to-all(bf16[8,392,128]{2,1,0:T(8,128)(2,1)S(1)} %get-tuple-element.14), channel_id=1, replica_groups=mesh['rows_0'=2,'rows_1'=4,'cols_0'=2,'cols_1'=8,'cols_2'=2] {'rows_0','..., dimensions={0} | all-to-all | bytes 1605632 | tf_op jit(solution)/shard_map/all_to_all | solution.py:354
  23.3 1.4 %shard_map.42 = bf16[1024,768]{1,0:T(8,128)(2,1)S(1)} custom-call(bf16[8,392,128]{2,1,0:T(8,128)(2,1)S(1)} %all_to_all.15.got_ref), custom_call_target="tpu_custom_call" | custom-call | flops 805306368 | bytes 4000000 | tf_op jit(solution)/shard_map/pallas_call | solution.py:376
  24.7 43.4 %all_to_all.16 = bf16[16,64,768]{2,1,0:T(8,128)(2,1)S(1)} all-to-all(bf16[16,64,768]{2,1,0:T(8,128)(2,1)S(1)} %bitcast.13), channel_id=1, replica_groups=mesh['rows_0'=2,'rows_1'=4,'cols_0'=2,'cols_1'=8,'cols_2'=2] {'cols_0','..., dimensions={0} | all-to-all | bytes 3145728 | tf_op jit(solution)/shard_map/all_to_all | solution.py:354
  68.1 1.5 %shard_map.43.early_ref = f32[1,1024]{1,0:T(1,128)S(1)} custom-call(bf16[1024,768]{1,0:T(8,128)(2,1)S(1)} %bitcast.8), custom_call_target="tpu_custom_call" | custom-call | flops 805306368 | bytes 4000000 | tf_op jit(solution)/shard_map/pallas_call | solution.py:383
  69.6 0.0 copy-start
  69.6 0.1 fusion
  69.7 1.9 %collective-permute-start = (bf16[512,768]{1,0:T(8,128)(2,1)S(1)}, bf16[512,768]{1,0:T(8,128)(2,1)S(1)}, u32[]{:S(2)}, u32[]{:S(2)}) collective-permute-start(bf16[512,768]{1,0:T(8,128)(2,1)S(1)} %get-tuple-element.27), channel_id=1, source_target_pairs={{0,1},{1,0},{2,3},{3,2},{4,5},{5,4},{6,7},{7,6},{8,9},{9,8},{10,11... | collective-permute-start | bytes 2359304 | tf_op jit(solution)/shard_map/ppermute | solution.py:387
  71.6 0.1 collective-permute-start.1
  71.7 0.0 copy-done
  71.7 0.2 shard_map.47.index_ref
  71.9 1.6 %collective-permute-done.more_ref = bf16[512,768]{1,0:T(8,128)(2,1)S(1)} collective-permute-done((bf16[512,768]{1,0:T(8,128)(2,1)S(1)}, bf16[512,768]{1,0:T(8,128)(2,1)S(1)}, u32[]{:S(2)}, u32[]{:S(2)}) %collective-permute-start) | collective-permute-done | bytes 786464 | tf_op jit(solution)/shard_map/ppermute | solution.py:387
  73.5 1.7 %shard_map.45 = (f32[1,1024]{1,0:T(1,128)S(1)}, f32[1,512]{1,0:T(1,128)S(1)}) custom-call(bf16[1024,768]{1,0:T(8,128)(2,1)S(1)} %bitcast.11, bf16[512,768]{1,0:T(8,128)(2,1)S(1)} %collective-permute-done.more_ref, f32[1,1024]{1,0:T(1,128)S(1)} %shard_map.44.so_far_ref), custom_call_target="tpu_custom_call" | custom-call | flops 805306368 | bytes 4000000 | tf_op jit(solution)/shard_map/pallas_call | solution.py:390
  75.2 0.0 collective-permute-done.1.last_ref
  75.2 2.3 %shard_map.46 = f32[256,128]{1,0:T(8,128)S(1)} custom-call(bf16[1024,768]{1,0:T(8,128)(2,1)S(1)} %bitcast.12, bf16[512,768]{1,0:T(8,128)(2,1)S(1)} %collective-permute-done.more_ref, bf16[512,768]{1,0:T(8,128)(2,1)S(1)} %collective-permute-done.1.last_ref, f32[1,1024]{1,0:T(1,128)S(1)} %get-tuple-element.18.so_far_ref, ...), custom_call_target="tpu_custom_call" | custom-call | flops 1610612736 | bytes 4000000 | tf_op jit(solution)/shard_map/pallas_call | solution.py:392
  77.6 18.6 %all_to_all.17 = f16[128,2,128]{2,1,0:T(2,128)(2,1)S(1)} all-to-all(f16[128,2,128]{2,1,0:T(2,128)(2,1)S(1)} %bitcast.16), channel_id=1, replica_groups=mesh['rows_0'=2,'rows_1'=4,'cols_0'=2,'cols_1'=8,'cols_2'=2] {'rows_0','..., dimensions={0} | all-to-all | bytes 131072 | tf_op jit(solution)/shard_map/all_to_all | solution.py:354
  96.2 0.8 shard_map.48
  (3 shorter events, 0.0 us)
Async XLA Ops:
  69.6 2.1 %copy-start = (s32[256]{0:T(256)S(1)}, s32[256]{0:T(256)}, u32[]{:S(2)}) copy-start(s32[256]{0:T(256)} %param.3) | copy-start | bytes 3076
  69.7 3.8 %collective-permute-start = (bf16[512,768]{1,0:T(8,128)(2,1)S(1)}, bf16[512,768]{1,0:T(8,128)(2,1)S(1)}, u32[]{:S(2)}, u32[]{:S(2)}) collective-permute-start(bf16[512,768]{1,0:T(8,128)(2,1)S(1)} %get-tuple-element.27), channel_id=1, source_target_pairs={{0,1},{1,0},{2,3},{3,2},{4,5},{5,4},{6,7},{7,6},{8,9},{9,8},{10,11... | collective-permute-start | bytes 2359304 | tf_op jit(solution)/shard_map/ppermute | solution.py:387
  71.6 3.6 %collective-permute-start.1 = (bf16[512,768]{1,0:T(8,128)(2,1)S(1)}, bf16[512,768]{1,0:T(8,128)(2,1)S(1)}, u32[]{:S(2)}, u32[]{:S(2)}) collective-permute-start(bf16[512,768]{1,0:T(8,128)(2,1)S(1)} %get-tuple-element.26), channel_id=1, source_target_pairs={{0,1},{1,0},{2,3},{3,2},{4,5},{5,4},{6,7},{7,6},{8,9},{9,8},{10,11... | collective-permute-start | bytes 2359304 | tf_op jit(solution)/shard_map/ppermute | solution.py:387

commit v8 on v7

--- a/solution.py
+++ b/solution.py
@@ -5,6 +5,7 @@
 from jax.experimental.pallas import tpu as pltpu
 from jax.sharding import Mesh
 from jax.sharding import PartitionSpec as P
+
 
 CAP = 64
 GROUP_CLUSTERS = 16
@@ -152,7 +153,6 @@
 
 
 def penalties(ref):
-    total, width = ref.shape
     column = jnp.where(ref[:, 0:1].astype(F32) < 1.5, 0.0, -4.0)
     pick = ones_where(iota((8, 256), 1) == 0)
     row = jnp.where(dot_t(pick, ref[:, 0:256])[0:1, :] < 1.5, 0.0, -4.0)
@@ -302,14 +302,22 @@
         out_ref[at : at + block.shape[0], :] = block
 
 
-def pick_results(index_ref, got_ref, best_ref, hist_ref):
+def pick_results(index_ref, got_ref, best_hbm, hist_hbm, best_ref, hist_ref, sems):
     lines = got_ref.shape[0]
     docs = index_ref.shape[1]
+    got = got_ref[...]
+    even = lax.bitwise_and(iota((8, LANES), 0), 1) == 0
+    total = jnp.zeros((8, LANES), F32)
+    for s in range(0, lines, 8):
+        total = total + jnp.where(even, got[s : s + 8, :], 0.0)
+    total = jnp.sum(total, axis=0, keepdims=True)
+    hist_ref[...] = total * (1.0 / (HIST_SCALE * lines * docs))
+    hist_copy = pltpu.make_async_copy(hist_ref, hist_hbm, sems.at[0])
+    hist_copy.start()
     index = index_ref[...]
     line = lax.shift_right_logical(index, 6) * 2 + 1
     rank = lax.bitwise_and(index, CAP - 1)
     onehot = ones_where(iota((lines, docs), 0) == line)
-    got = got_ref[...]
     turned = got.T
     high = turned.astype(BF16)
     low = (turned - high.astype(F32)).astype(BF16)
@@ -318,24 +326,23 @@
     picked = picked * jnp.where(lane < CAP, 1.0 / HIGH_SCALE, 1.0 / LOW_SCALE)
     wanted = lax.bitwise_and(lane, CAP - 1) == rank
     best_ref[...] = jnp.sum(jnp.where(wanted, picked, 0.0), axis=0, keepdims=True)
-    even = lax.bitwise_and(iota((8, LANES), 0), 1) == 0
-    total = jnp.zeros((8, LANES), F32)
-    for s in range(0, lines, 8):
-        total = total + jnp.where(even, got[s : s + 8, :], 0.0)
-    hist_ref[...] = jnp.sum(total, axis=0, keepdims=True) * (1.0 / (HIST_SCALE * lines * docs))
+    best_copy = pltpu.make_async_copy(best_ref, best_hbm, sems.at[1])
+    best_copy.start()
+    hist_copy.wait()
+    best_copy.wait()
 
 
 VMEM = pl.BlockSpec(memory_space=pltpu.VMEM)
 ANY = pl.BlockSpec(memory_space=pl.ANY)
 
 
-def call(kernel, outs, specs, flops, scratch=()):
+def call(kernel, outs, specs, flops, scratch=(), place=VMEM):
     many = isinstance(outs, tuple)
     return pl.pallas_call(
         kernel,
         out_shape=outs,
         in_specs=specs,
-        out_specs=tuple(VMEM for _ in outs) if many else VMEM,
+        out_specs=tuple(place for _ in outs) if many else place,
         scratch_shapes=scratch,
         compiler_params=pltpu.CompilerParams(vmem_limit_bytes=24 * 2**20),
         cost_estimate=pl.CostEstimate(flops=flops, bytes_accessed=4000000, transcendentals=0),
@@ -378,26 +385,26 @@
     )
     own = exchange(sends.reshape(GROUP_CLUSTERS, CAP, width), CHIPS)
     own, got = lax.optimization_barrier((own.reshape(total, width), got))
-    whole, part = shape((1, total), F32), shape((1, total // 2), F32)
+    whole, part = shape((1, total), F32), shape((1, BLOCK), F32)
     flops = 2 * total * total // 2 * width
     early = call(best_own_early, whole, [VMEM], flops)(own)
     own, early = lax.optimization_barrier((own, early))
     pairs = [(i, i ^ 1) for i in range(col_count)]
-    half = total // 2
-    other = [lax.ppermute(own[s : s + half], COLS, pairs) for s in (0, half)]
+    first = lax.ppermute(own[:BLOCK], COLS, pairs)
+    rest = lax.ppermute(own[BLOCK:], COLS, pairs)
     lines = row_count * GROUP_CLUSTERS * 2
     best = call(best_own_late, whole, [VMEM] * 2, flops)(own, early)
-    best, more = call(best_more, (whole, part), [VMEM] * 3, flops)(own, other[0], best)
+    best, more = call(best_more, (whole, part), [VMEM] * 3, flops)(own, first, best)
     index = call(return_index, shape((1, docs), jnp.int32), [VMEM] * 3, 2**26)(labels, rank, got)
     results = call(best_last, shape((lines, LANES), F32), [VMEM] * 5, 2 * flops)(
-        own, other[0], other[1], best, more
+        own, first, rest, best, more
     )
     results, index = lax.optimization_barrier((results, index))
     results = exchange(results.astype(WIRE).reshape(lines // 2, 2, LANES), SAME_CORE)
     results = results.reshape(lines, LANES).astype(F32)
-    best, hist = call(
-        pick_results, (shape((1, docs), F32), shape((1, BINS), F32)), [VMEM, VMEM], 2**26
-    )(index, results)
+    outs = (shape((1, docs), F32), shape((1, BINS), F32))
+    scratch = [pltpu.VMEM((1, docs), F32), pltpu.VMEM((1, BINS), F32), pltpu.SemaphoreType.DMA((2,))]
+    best, hist = call(pick_results, outs, [VMEM, VMEM], 2**26, scratch, ANY)(index, results)
     return (best.reshape(docs), hist.reshape(BINS))
 
 

time: 97.2 us -> 98.4 us (1.012)
  waiting for transfers between devices: 1.64 us -> 2.72 us
    ppermute x2, waiting for transfers between devices: 1.64 us -> 2.72 us  [the longest x1 2.72 us: shards(): first = lax.ppermute(own[:BLOCK], COLS, pairs)]
  transfers between devices with their start and end apart: 2 -> 2, of which waited for: 1 -> 1; matrix products, arithmetic and copies ran while one was open for 0% -> 0% of each run, Pallas kernels for 2% -> 1%
where the time goes in v8:
time: 98.4 us; the launch traced here: 98.1 us
  blocking collectives  83.1 us (84%)
  Pallas kernels  9.51 us (10%)
  waiting for transfers between devices  2.72 us (3%)
  starting transfers between devices  2.01 us (2%)
    all_to_all x3, blocking collectives, exchange(): return lax.all_to_all(x, axes, split_axis=0, concat_axis=0, tiled=True)  83.1 us
    pallas_call x1, Pallas kernels, shards(): call(best_last, shape((lines, LANES), F32), [VMEM] * 5, 2 * flops)  3.04 us
    ppermute x1, waiting for transfers between devices, shards(): first = lax.ppermute(own[:BLOCK], COLS, pairs)  2.72 us
  transfers between devices with their start and end apart: 2, of which 1 were waited for; matrix products, arithmetic and copies ran while one was open for 0% of the time, Pallas kernels for 1%

profile of v8, /device:TPU:1, one launch (start us, length us, event | category | flops | bytes accessed | tf_op | source)
XLA Modules:
  0.0 98.1 jit_solution(11158112690983032858)
XLA Ops:
  0.6 1.6 %shard_map.41 = (bf16[8,392,128]{2,1,0:T(8,128)(2,1)S(1)}, f32[1,256]{1,0:T(1,128)S(1)}) custom-call(s32[1,256]{1,0:T(1,128)} %bitcast.15, bf16[256,768]{1,0:T(8,128)(2,1)} %embeddings_hbm.1), custom_call_target="tpu_custom_call" | custom-call | flops 201326592 | bytes 4000000 | tf_op jit(solution)/shard_map/pallas_call | solution.py:370
  2.3 21.0 %all_to_all.15.got_ref = bf16[8,392,128]{2,1,0:T(8,128)(2,1)S(1)} all-to-all(bf16[8,392,128]{2,1,0:T(8,128)(2,1)S(1)} %get-tuple-element.14), channel_id=1, replica_groups=mesh['rows_0'=2,'rows_1'=4,'cols_0'=2,'cols_1'=8,'cols_2'=2] {'rows_0','..., dimensions={0} | all-to-all | bytes 1605632 | tf_op jit(solution)/shard_map/all_to_all | solution.py:361
  23.3 1.4 %shard_map.42 = bf16[1024,768]{1,0:T(8,128)(2,1)S(1)} custom-call(bf16[8,392,128]{2,1,0:T(8,128)(2,1)S(1)} %all_to_all.15.got_ref), custom_call_target="tpu_custom_call" | custom-call | flops 805306368 | bytes 4000000 | tf_op jit(solution)/shard_map/pallas_call | solution.py:383
  24.7 43.4 %all_to_all.16 = bf16[16,64,768]{2,1,0:T(8,128)(2,1)S(1)} all-to-all(bf16[16,64,768]{2,1,0:T(8,128)(2,1)S(1)} %bitcast.14), channel_id=1, replica_groups=mesh['rows_0'=2,'rows_1'=4,'cols_0'=2,'cols_1'=8,'cols_2'=2] {'cols_0','..., dimensions={0} | all-to-all | bytes 3145728 | tf_op jit(solution)/shard_map/all_to_all | solution.py:361
  68.1 1.5 %shard_map.43.early_ref = f32[1,1024]{1,0:T(1,128)S(1)} custom-call(bf16[1024,768]{1,0:T(8,128)(2,1)S(1)} %bitcast.8), custom_call_target="tpu_custom_call" | custom-call | flops 805306368 | bytes 4000000 | tf_op jit(solution)/shard_map/pallas_call | solution.py:390
  69.6 0.0 copy-start
  69.6 0.1 slice.7
  69.7 1.9 %collective-permute-start.1 = (bf16[768,768]{1,0:T(8,128)(2,1)S(1)}, bf16[768,768]{1,0:T(8,128)(2,1)S(1)}, u32[]{:S(2)}, u32[]{:S(2)}) collective-permute-start(bf16[768,768]{1,0:T(8,128)(2,1)S(1)} %slice.7), channel_id=1, source_target_pairs={{0,1},{1,0},{2,3},{3,2},{4,5},{5,4},{6,7},{7,6},{8,9},{9,8},{10,11... | collective-permute-start | bytes 3538952 | tf_op jit(solution)/shard_map/ppermute | solution.py:394
  71.6 0.1 collective-permute-start
  71.7 0.0 copy-done
  71.7 0.2 shard_map.47.index_ref
  71.9 2.7 %collective-permute-done.more_ref = bf16[256,768]{1,0:T(8,128)(2,1)S(1)} collective-permute-done((bf16[256,768]{1,0:T(8,128)(2,1)S(1)}, bf16[256,768]{1,0:T(8,128)(2,1)S(1)}, u32[]{:S(2)}, u32[]{:S(2)}) %collective-permute-start) | collective-permute-done | bytes 393248 | tf_op jit(solution)/shard_map/ppermute | solution.py:393
  74.6 1.0 shard_map.45
  75.6 0.0 collective-permute-done.1.last_ref
  75.6 3.0 %shard_map.46 = f32[256,128]{1,0:T(8,128)S(1)} custom-call(bf16[1024,768]{1,0:T(8,128)(2,1)S(1)} %bitcast.13, bf16[256,768]{1,0:T(8,128)(2,1)S(1)} %collective-permute-done.more_ref, bf16[768,768]{1,0:T(8,128)(2,1)S(1)} %collective-permute-done.1.last_ref, f32[1,1024]{1,0:T(1,128)S(1)} %get-tuple-element.18.so_far_ref, ...), custom_call_target="tpu_custom_call" | custom-call | flops 1610612736 | bytes 4000000 | tf_op jit(solution)/shard_map/pallas_call | solution.py:399
  78.7 18.6 %all_to_all.17 = f16[128,2,128]{2,1,0:T(2,128)(2,1)S(1)} all-to-all(f16[128,2,128]{2,1,0:T(2,128)(2,1)S(1)} %bitcast.17), channel_id=1, replica_groups=mesh['rows_0'=2,'rows_1'=4,'cols_0'=2,'cols_1'=8,'cols_2'=2] {'rows_0','..., dimensions={0} | all-to-all | bytes 131072 | tf_op jit(solution)/shard_map/all_to_all | solution.py:361
  97.3 0.8 shard_map.48
  (4 shorter events, 0.1 us)
Async XLA Ops:
  69.6 2.1 %copy-start = (s32[256]{0:T(256)S(1)}, s32[256]{0:T(256)}, u32[]{:S(2)}) copy-start(s32[256]{0:T(256)} %param.3) | copy-start | bytes 3076
  69.7 5.9 %collective-permute-start.1 = (bf16[768,768]{1,0:T(8,128)(2,1)S(1)}, bf16[768,768]{1,0:T(8,128)(2,1)S(1)}, u32[]{:S(2)}, u32[]{:S(2)}) collective-permute-start(bf16[768,768]{1,0:T(8,128)(2,1)S(1)} %slice.7), channel_id=1, source_target_pairs={{0,1},{1,0},{2,3},{3,2},{4,5},{5,4},{6,7},{7,6},{8,9},{9,8},{10,11... | collective-permute-start | bytes 3538952 | tf_op jit(solution)/shard_map/ppermute | solution.py:394
  71.6 3.0 %collective-permute-start = (bf16[256,768]{1,0:T(8,128)(2,1)S(1)}, bf16[256,768]{1,0:T(8,128)(2,1)S(1)}, u32[]{:S(2)}, u32[]{:S(2)}) collective-permute-start(bf16[256,768]{1,0:T(8,128)(2,1)S(1)} %slice.6), channel_id=1, source_target_pairs={{0,1},{1,0},{2,3},{3,2},{4,5},{5,4},{6,7},{7,6},{8,9},{9,8},{10,11... | collective-permute-start | bytes 1179656 | tf_op jit(solution)/shard_map/ppermute | solution.py:393

commit v9 on v6

--- a/solution.py
+++ b/solution.py
@@ -9,10 +9,10 @@
 CAP = 64
 GROUP_CLUSTERS = 16
 BINS = 128
-ROWS = ("rows_0", "rows_1")
+ROWS = ("rows_1", "rows_0")
 COLS = ("cols_0", "cols_1", "cols_2")
 CHIPS = ("cols_0", "cols_1")
-ALL = ROWS + COLS
+ALL = ("rows_0", "rows_1") + COLS
 SAME_CORE = ROWS + CHIPS
 LANES = 128
 BLOCK = 256
@@ -117,6 +117,7 @@
     onehot = ones_where(iota((GROUP_CLUSTERS, slots), 0) == cluster)
     place = cluster * CAP + rank_of(onehot, slots).astype(jnp.int32)
     place = jnp.where(label > 0, place, -1)
+    counts = jnp.sum(onehot.astype(F32), axis=1, keepdims=True).astype(jnp.int32)
     total = GROUP_CLUSTERS * CAP
     step = total // 4
     pieces = width // LANES
@@ -124,14 +125,17 @@
         [got_ref[:, f * CAP : (f + 1) * CAP, :].reshape(slots, LANES) for f in range(pieces)],
         axis=1,
     )
+    lane, rank = iota((CAP, LANES), 1), iota((CAP, LANES), 0)
+    marks = []
+    for c in range(GROUP_CLUSTERS):
+        empty = (rank >= counts[c : c + 1, :]) & (lane == 0)
+        marks.append(jnp.where(empty, EMPTY, 0.0))
     for s in range(0, total, step):
-        places = jnp.where(iota((step, slots), 0) + s == place, 1.0, 0.0)
-        filled = jnp.sum(places, axis=1, keepdims=True) > 0.5
-        moved = dot(places.astype(BF16), rows)
+        places = ones_where(iota((step, slots), 0) + s == place)
+        moved = dot(places, rows)
         out_ref[s : s + step, LANES:] = moved[:, LANES:].astype(BF16)
-        first = moved[:, 0:LANES]
-        first = jnp.where((iota(first.shape, 1) == 0) & ~filled, EMPTY, first)
-        out_ref[s : s + step, 0:LANES] = first.astype(BF16)
+        mark = jnp.concatenate(marks[s // CAP : (s + step) // CAP], axis=0)
+        out_ref[s : s + step, 0:LANES] = (moved[:, 0:LANES] + mark).astype(BF16)
 
 
 def return_index(labels_ref, rank_ref, got_ref, out_ref):
@@ -151,9 +155,12 @@
     out_ref[...] = labels * CAP + (rank_ref[...] + earlier).astype(jnp.int32)
 
 
+def column_of(ref):
+    return jnp.where(ref[:, 0:1].astype(F32) < 1.5, 0.0, -4.0)
+
+
 def penalties(ref):
-    total, width = ref.shape
-    column = jnp.where(ref[:, 0:1].astype(F32) < 1.5, 0.0, -4.0)
+    column = column_of(ref)
     pick = ones_where(iota((8, 256), 1) == 0)
     row = jnp.where(dot_t(pick, ref[:, 0:256])[0:1, :] < 1.5, 0.0, -4.0)
     return column, row
@@ -212,18 +219,21 @@
     return [None] * (ref.shape[0] // BLOCK)
 
 
-def best_own(own_ref, best_ref):
+def best_own(own_ref, best_ref, penalty_ref):
     columns, rows = nothing(own_ref), nothing(own_ref)
-    within(own_ref, penalties(own_ref), columns, rows)
+    penalty = penalties(own_ref)
+    within(own_ref, penalty, columns, rows)
     best_ref[...] = jnp.maximum(as_line(columns, rows), -1.0)
-
-
-def best_more(own_ref, more_ref, so_far_ref, best_ref, best_more_ref):
+    penalty_ref[...] = penalty[1]
+
+
+def best_more(own_ref, more_ref, so_far_ref, own_row_ref, best_ref, columns_ref, rows_ref):
     columns, rows, of_own = nothing(more_ref), nothing(more_ref), nothing(own_ref)
     penalty = penalties(more_ref)
-    between(more_ref, penalty, own_ref, penalties(own_ref), rows, of_own)
+    between(more_ref, penalty, own_ref, (None, own_row_ref[...]), rows, of_own)
     within(more_ref, penalty, columns, rows)
-    best_more_ref[...] = as_line(columns, rows)
+    columns_ref[...] = jnp.concatenate(columns, axis=1)
+    rows_ref[...] = jnp.concatenate(rows, axis=0)
     best_ref[...] = jnp.maximum(as_line(of_own, nothing(own_ref)), so_far_ref[...])
 
 
@@ -238,17 +248,20 @@
     return folded
 
 
-def best_last(own_ref, more_ref, last_ref, so_far_ref, more_so_far_ref, out_ref):
+def best_last(
+    own_ref, more_ref, last_ref, so_far_ref, own_row_ref, more_columns_ref, more_rows_ref, out_ref
+):
     total = own_ref.shape[0]
-    own_penalty, more_penalty = penalties(own_ref), penalties(more_ref)
+    own_penalty, more_penalty = (None, own_row_ref[...]), penalties(more_ref)
     penalty = penalties(last_ref)
     columns, rows, of_own = nothing(last_ref), nothing(last_ref), nothing(own_ref)
-    of_more = nothing(more_ref)
+    starts = range(0, more_ref.shape[0], BLOCK)
+    of_more = [more_rows_ref[s : s + BLOCK, :] for s in starts]
     between(more_ref, more_penalty, last_ref, penalty, of_more, columns)
     between(last_ref, penalty, own_ref, own_penalty, rows, of_own)
     within(last_ref, penalty, columns, rows)
     best = jnp.maximum(as_line(of_own, nothing(own_ref)), so_far_ref[...])
-    more_line = [more_so_far_ref[:, s : s + BLOCK] for s in range(0, more_ref.shape[0], BLOCK)]
+    more_line = [more_columns_ref[:, s : s + BLOCK] for s in starts]
     more_best = jnp.maximum(as_line(more_line, of_more), -1.0)
     last_best = jnp.maximum(as_line(columns, rows), -1.0)
     mine = histogram_parts(best, own_penalty[1])
@@ -360,12 +373,15 @@
     other = [lax.ppermute(own[s : s + half], COLS, pairs) for s in (0, half)]
     flops = 2 * total * half * width
     lines = row_count * GROUP_CLUSTERS * 2
-    whole, part = shape((1, total), F32), shape((1, half), F32)
-    best = call(best_own, whole, [VMEM], flops)(own)
-    best, more = call(best_more, (whole, part), [VMEM] * 3, flops)(own, other[0], best)
+    whole = shape((1, total), F32)
+    best, own_row = call(best_own, (whole, whole), [VMEM], flops)(own)
+    parts = (whole, shape((8, half), F32), shape((half, LANES), F32))
+    best, more_columns, more_rows = call(best_more, parts, [VMEM] * 4, flops)(
+        own, other[0], best, own_row
+    )
     index = call(return_index, shape((1, docs), jnp.int32), [VMEM] * 3, 2**26)(labels, rank, got)
-    results = call(best_last, shape((lines, LANES), F32), [VMEM] * 5, 2 * flops)(
-        own, other[0], other[1], best, more
+    results = call(best_last, shape((lines, LANES), F32), [VMEM] * 7, 2 * flops)(
+        own, other[0], other[1], best, own_row, more_columns, more_rows
     )
     results, index = lax.optimization_barrier((results, index))
     results = exchange(results.astype(WIRE).reshape(lines // 2, 2, LANES), SAME_CORE)

time: 97.2 us -> 96.4 us (level)
  no operation moved by 1% of the time
where the time goes in v9:
time: 96.4 us; the launch traced here: 96.2 us
  blocking collectives  82.9 us (86%)
  Pallas kernels  9.03 us (9%)
  starting transfers between devices  3.32 us (3%)
    all_to_all x3, blocking collectives, exchange(): return lax.all_to_all(x, axes, split_axis=0, concat_axis=0, tiled=True)  82.9 us
    ppermute x2, starting transfers between devices, shards(): other = [lax.ppermute(own[s:s + half], COLS, pairs) for s in (0, half)]  3.32 us
    pallas_call x1, Pallas kernels, shards(): call(best_last, shape((lines, LANES), F32), [VMEM] * 7, 2 * flops)  2.22 us
  transfers between devices with their start and end apart: 2, of which 1 were waited for; matrix products, arithmetic and copies ran while one was open for 0% of the time, Pallas kernels for 3%

profile of v9, /device:TPU:1, one launch (start us, length us, event | category | flops | bytes accessed | tf_op | source)
XLA Modules:
  0.0 96.2 jit_solution(1091987780205471161)
XLA Ops:
  0.6 1.6 %shard_map.41 = (bf16[8,392,128]{2,1,0:T(8,128)(2,1)S(1)}, f32[1,256]{1,0:T(1,128)S(1)}) custom-call(s32[1,256]{1,0:T(1,128)} %bitcast.13, bf16[256,768]{1,0:T(8,128)(2,1)} %embeddings_hbm.1), custom_call_target="tpu_custom_call" | custom-call | flops 201326592 | bytes 4000000 | tf_op jit(solution)/shard_map/pallas_call | solution.py:353
  2.3 21.2 %all_to_all.15.got_ref = bf16[8,392,128]{2,1,0:T(8,128)(2,1)S(1)} all-to-all(bf16[8,392,128]{2,1,0:T(8,128)(2,1)S(1)} %get-tuple-element.15), channel_id=1, replica_groups=mesh['rows_0'=2,'rows_1'=4,'cols_0'=2,'cols_1'=8,'cols_2'=2] {'rows_1','..., dimensions={0} | all-to-all | bytes 1605632 | tf_op jit(solution)/shard_map/all_to_all | solution.py:344
  23.5 1.3 %shard_map.42 = bf16[1024,768]{1,0:T(8,128)(2,1)S(1)} custom-call(bf16[8,392,128]{2,1,0:T(8,128)(2,1)S(1)} %all_to_all.15.got_ref), custom_call_target="tpu_custom_call" | custom-call | flops 805306368 | bytes 4000000 | tf_op jit(solution)/shard_map/pallas_call | solution.py:366
  24.7 43.6 %all_to_all.16 = bf16[16,64,768]{2,1,0:T(8,128)(2,1)S(1)} all-to-all(bf16[16,64,768]{2,1,0:T(8,128)(2,1)S(1)} %bitcast.12), channel_id=1, replica_groups=mesh['rows_0'=2,'rows_1'=4,'cols_0'=2,'cols_1'=8,'cols_2'=2] {'cols_0','..., dimensions={0} | all-to-all | bytes 3145728 | tf_op jit(solution)/shard_map/all_to_all | solution.py:344
  68.3 0.0 copy-start
  68.3 0.1 fusion
  68.4 3.2 %collective-permute-start = (bf16[512,768]{1,0:T(8,128)(2,1)S(1)}, bf16[512,768]{1,0:T(8,128)(2,1)S(1)}, u32[]{:S(2)}, u32[]{:S(2)}) collective-permute-start(bf16[512,768]{1,0:T(8,128)(2,1)S(1)} %get-tuple-element.29), channel_id=1, source_target_pairs={{0,1},{1,0},{2,3},{3,2},{4,5},{5,4},{6,7},{7,6},{8,9},{9,8},{10,11... | collective-permute-start | bytes 2359304 | tf_op jit(solution)/shard_map/ppermute | solution.py:373
  71.7 0.1 collective-permute-start.1
  71.8 0.0 copy-done
  71.8 0.2 shard_map.46.index_ref
  71.9 1.5 %shard_map.43 = (f32[1,1024]{1,0:T(1,128)S(1)}, f32[1,1024]{1,0:T(1,128)S(1)}) custom-call(bf16[1024,768]{1,0:T(8,128)(2,1)S(1)} %bitcast.9), custom_call_target="tpu_custom_call" | custom-call | flops 805306368 | bytes 4000000 | tf_op jit(solution)/shard_map/pallas_call | solution.py:377
  73.4 0.2 collective-permute-done.more_ref
  73.6 1.5 %shard_map.44 = (f32[1,1024]{1,0:T(1,128)S(1)}, f32[8,512]{1,0:T(8,128)S(1)}, f32[512,128]{1,0:T(8,128)S(1)}) custom-call(bf16[1024,768]{1,0:T(8,128)(2,1)S(1)} %bitcast.10, bf16[512,768]{1,0:T(8,128)(2,1)S(1)} %collective-permute-done.more_ref, f32[1,1024]{1,0:T(1,128)S(1)} %get-tuple-element.17.so_far_ref, f32[1,1024]{1,0:T(1,128)S(1)} %get-tuple-element.18.own_row_ref), custom_call_target="tpu_custom_call" | custom-call | flops 805306368 | bytes 4000000 | tf_op jit(solution)/shard_map/pallas_call | solution.py:379
  75.0 0.0 collective-permute-done.1.last_ref
  75.0 2.2 %shard_map.45 = f32[256,128]{1,0:T(8,128)S(1)} custom-call(bf16[1024,768]{1,0:T(8,128)(2,1)S(1)} %bitcast.11, bf16[512,768]{1,0:T(8,128)(2,1)S(1)} %collective-permute-done.more_ref, bf16[512,768]{1,0:T(8,128)(2,1)S(1)} %collective-permute-done.1.last_ref, f32[1,1024]{1,0:T(1,128)S(1)} %get-tuple-element.19.so_far_ref, ...), custom_call_target="tpu_custom_call" | custom-call | flops 1610612736 | bytes 4000000 | tf_op jit(solution)/shard_map/pallas_call | solution.py:383
  77.3 18.1 %all_to_all.17 = f16[128,2,128]{2,1,0:T(2,128)(2,1)S(1)} all-to-all(f16[128,2,128]{2,1,0:T(2,128)(2,1)S(1)} %bitcast.15), channel_id=1, replica_groups=mesh['rows_0'=2,'rows_1'=4,'cols_0'=2,'cols_1'=8,'cols_2'=2] {'rows_1','..., dimensions={0} | all-to-all | bytes 131072 | tf_op jit(solution)/shard_map/all_to_all | solution.py:344
  95.4 0.8 shard_map.47
  (2 shorter events, 0.0 us)
Async XLA Ops:
  68.3 3.4 %copy-start = (s32[256]{0:T(256)S(1)}, s32[256]{0:T(256)}, u32[]{:S(2)}) copy-start(s32[256]{0:T(256)} %param.3) | copy-start | bytes 3076
  68.4 5.1 %collective-permute-start = (bf16[512,768]{1,0:T(8,128)(2,1)S(1)}, bf16[512,768]{1,0:T(8,128)(2,1)S(1)}, u32[]{:S(2)}, u32[]{:S(2)}) collective-permute-start(bf16[512,768]{1,0:T(8,128)(2,1)S(1)} %get-tuple-element.29), channel_id=1, source_target_pairs={{0,1},{1,0},{2,3},{3,2},{4,5},{5,4},{6,7},{7,6},{8,9},{9,8},{10,11... | collective-permute-start | bytes 2359304 | tf_op jit(solution)/shard_map/ppermute | solution.py:373
  71.7 3.4 %collective-permute-start.1 = (bf16[512,768]{1,0:T(8,128)(2,1)S(1)}, bf16[512,768]{1,0:T(8,128)(2,1)S(1)}, u32[]{:S(2)}, u32[]{:S(2)}) collective-permute-start(bf16[512,768]{1,0:T(8,128)(2,1)S(1)} %get-tuple-element.28), channel_id=1, source_target_pairs={{0,1},{1,0},{2,3},{3,2},{4,5},{5,4},{6,7},{7,6},{8,9},{9,8},{10,11... | collective-permute-start | bytes 2359304 | tf_op jit(solution)/shard_map/ppermute | solution.py:373

commit v10 on v9

--- a/solution.py
+++ b/solution.py
@@ -219,22 +219,20 @@
     return [None] * (ref.shape[0] // BLOCK)
 
 
-def best_own(own_ref, best_ref, penalty_ref):
+def best_own(own_ref, found_ref):
     columns, rows = nothing(own_ref), nothing(own_ref)
     penalty = penalties(own_ref)
     within(own_ref, penalty, columns, rows)
-    best_ref[...] = jnp.maximum(as_line(columns, rows), -1.0)
-    penalty_ref[...] = penalty[1]
-
-
-def best_more(own_ref, more_ref, so_far_ref, own_row_ref, best_ref, columns_ref, rows_ref):
-    columns, rows, of_own = nothing(more_ref), nothing(more_ref), nothing(own_ref)
-    penalty = penalties(more_ref)
-    between(more_ref, penalty, own_ref, (None, own_row_ref[...]), rows, of_own)
-    within(more_ref, penalty, columns, rows)
-    columns_ref[...] = jnp.concatenate(columns, axis=1)
+    found_ref[0:1, :] = jnp.maximum(as_line(columns, rows), -1.0)
+    found_ref[1:2, :] = penalty[1]
+
+
+def best_more(own_ref, more_ref, found_ref, best_ref, rows_ref):
+    rows, of_own = nothing(more_ref), nothing(own_ref)
+    penalty = (column_of(more_ref), None)
+    between(more_ref, penalty, own_ref, (None, found_ref[1:2, :]), rows, of_own)
     rows_ref[...] = jnp.concatenate(rows, axis=0)
-    best_ref[...] = jnp.maximum(as_line(of_own, nothing(own_ref)), so_far_ref[...])
+    best_ref[...] = jnp.maximum(as_line(of_own, nothing(own_ref)), found_ref[0:1, :])
 
 
 def histogram_parts(best, penalty):
@@ -249,26 +247,20 @@
 
 
 def best_last(
-    own_ref, more_ref, last_ref, so_far_ref, own_row_ref, more_columns_ref, more_rows_ref, out_ref
+    own_ref, last_ref, so_far_ref, found_ref, more_rows_ref, theirs_ref, out_ref
 ):
     total = own_ref.shape[0]
-    own_penalty, more_penalty = (None, own_row_ref[...]), penalties(more_ref)
-    penalty = penalties(last_ref)
-    columns, rows, of_own = nothing(last_ref), nothing(last_ref), nothing(own_ref)
-    starts = range(0, more_ref.shape[0], BLOCK)
-    of_more = [more_rows_ref[s : s + BLOCK, :] for s in starts]
-    between(more_ref, more_penalty, last_ref, penalty, of_more, columns)
-    between(last_ref, penalty, own_ref, own_penalty, rows, of_own)
-    within(last_ref, penalty, columns, rows)
+    own_penalty = (None, found_ref[1:2, :])
+    rows, of_own = nothing(last_ref), nothing(own_ref)
+    starts = range(0, more_rows_ref.shape[0], BLOCK)
+    more_rows = [more_rows_ref[s : s + BLOCK, :] for s in starts]
+    between(last_ref, (column_of(last_ref), None), own_ref, own_penalty, rows, of_own)
     best = jnp.maximum(as_line(of_own, nothing(own_ref)), so_far_ref[...])
-    more_line = [more_columns_ref[:, s : s + BLOCK] for s in starts]
-    more_best = jnp.maximum(as_line(more_line, of_more), -1.0)
-    last_best = jnp.maximum(as_line(columns, rows), -1.0)
+    rows = more_rows + rows
+    their_line = [theirs_ref[0:1, s : s + BLOCK] for s in range(0, total, BLOCK)]
+    their_best = as_line(their_line, rows)
     mine = histogram_parts(best, own_penalty[1])
-    theirs = histogram_parts(
-        jnp.concatenate([more_best, last_best], axis=1),
-        jnp.concatenate([more_penalty[1], penalty[1]], axis=1),
-    )
+    theirs = histogram_parts(their_best, theirs_ref[1:2, :])
     hist = jnp.sum((mine + theirs).T, axis=0, keepdims=True)
     high = best.astype(BF16).astype(F32)
     low = (best - high) * LOW_SCALE
@@ -373,15 +365,13 @@
     other = [lax.ppermute(own[s : s + half], COLS, pairs) for s in (0, half)]
     flops = 2 * total * half * width
     lines = row_count * GROUP_CLUSTERS * 2
-    whole = shape((1, total), F32)
-    best, own_row = call(best_own, (whole, whole), [VMEM], flops)(own)
-    parts = (whole, shape((8, half), F32), shape((half, LANES), F32))
-    best, more_columns, more_rows = call(best_more, parts, [VMEM] * 4, flops)(
-        own, other[0], best, own_row
-    )
+    found = call(best_own, shape((2, total), F32), [VMEM], flops)(own)
+    theirs = lax.ppermute(found, COLS, pairs)
+    parts = (shape((1, total), F32), shape((half, LANES), F32))
+    best, more_rows = call(best_more, parts, [VMEM] * 3, flops)(own, other[0], found)
     index = call(return_index, shape((1, docs), jnp.int32), [VMEM] * 3, 2**26)(labels, rank, got)
-    results = call(best_last, shape((lines, LANES), F32), [VMEM] * 7, 2 * flops)(
-        own, other[0], other[1], best, own_row, more_columns, more_rows
+    results = call(best_last, shape((lines, LANES), F32), [VMEM] * 6, flops)(
+        own, other[1], best, found, more_rows, theirs
     )
     results, index = lax.optimization_barrier((results, index))
     results = exchange(results.astype(WIRE).reshape(lines // 2, 2, LANES), SAME_CORE)

time: 96.4 us -> 95.5 us (level)
  Pallas kernels: 9.03 us -> 7.69 us
    pallas_call x3, Pallas kernels: 5.17 us -> 3.83 us  [the longest x1 1.48 us: shards(): found = call(best_own, shape((2, total), F32), [VMEM], flops)(own)]
  transfers between devices with their start and end apart: 2 -> 3, of which waited for: 1 -> 0; matrix products, arithmetic and copies ran while one was open for 0% -> 0% of each run, Pallas kernels for 3% -> 3%
where the time goes in v10:
time: 95.5 us; the launch traced here: 95.3 us
  blocking collectives  82.9 us (87%)
  Pallas kernels  7.69 us (8%)
  starting transfers between devices  3.82 us (4%)
    all_to_all x3, blocking collectives, exchange(): return lax.all_to_all(x, axes, split_axis=0, concat_axis=0, tiled=True)  82.9 us
    ppermute x2, starting transfers between devices, shards(): other = [lax.ppermute(own[s:s + half], COLS, pairs) for s in (0, half)]  3.32 us
  transfers between devices with their start and end apart: 3, of which 0 were waited for; matrix products, arithmetic and copies ran while one was open for 0% of the time, Pallas kernels for 3%

profile of v10, /device:TPU:1, one launch (start us, length us, event | category | flops | bytes accessed | tf_op | source)
XLA Modules:
  0.0 95.3 jit_solution(10959232179778461203)
XLA Ops:
  0.6 1.6 %shard_map.41 = (bf16[8,392,128]{2,1,0:T(8,128)(2,1)S(1)}, f32[1,256]{1,0:T(1,128)S(1)}) custom-call(s32[1,256]{1,0:T(1,128)} %bitcast.13, bf16[256,768]{1,0:T(8,128)(2,1)} %embeddings_hbm.1), custom_call_target="tpu_custom_call" | custom-call | flops 201326592 | bytes 4000000 | tf_op jit(solution)/shard_map/pallas_call | solution.py:345
  2.3 21.2 %all_to_all.15.got_ref = bf16[8,392,128]{2,1,0:T(8,128)(2,1)S(1)} all-to-all(bf16[8,392,128]{2,1,0:T(8,128)(2,1)S(1)} %get-tuple-element.12), channel_id=1, replica_groups=mesh['rows_0'=2,'rows_1'=4,'cols_0'=2,'cols_1'=8,'cols_2'=2] {'rows_1','..., dimensions={0} | all-to-all | bytes 1605632 | tf_op jit(solution)/shard_map/all_to_all | solution.py:336
  23.5 1.3 %shard_map.42 = bf16[1024,768]{1,0:T(8,128)(2,1)S(1)} custom-call(bf16[8,392,128]{2,1,0:T(8,128)(2,1)S(1)} %all_to_all.15.got_ref), custom_call_target="tpu_custom_call" | custom-call | flops 805306368 | bytes 4000000 | tf_op jit(solution)/shard_map/pallas_call | solution.py:358
  24.7 43.6 %all_to_all.16 = bf16[16,64,768]{2,1,0:T(8,128)(2,1)S(1)} all-to-all(bf16[16,64,768]{2,1,0:T(8,128)(2,1)S(1)} %bitcast.12), channel_id=1, replica_groups=mesh['rows_0'=2,'rows_1'=4,'cols_0'=2,'cols_1'=8,'cols_2'=2] {'cols_0','..., dimensions={0} | all-to-all | bytes 3145728 | tf_op jit(solution)/shard_map/all_to_all | solution.py:336
  68.3 0.1 fusion
  68.4 0.0 copy-start
  68.5 3.2 %collective-permute-start.1 = (bf16[512,768]{1,0:T(8,128)(2,1)S(1)}, bf16[512,768]{1,0:T(8,128)(2,1)S(1)}, u32[]{:S(2)}, u32[]{:S(2)}) collective-permute-start(bf16[512,768]{1,0:T(8,128)(2,1)S(1)} %get-tuple-element.22), channel_id=1, source_target_pairs={{0,1},{1,0},{2,3},{3,2},{4,5},{5,4},{6,7},{7,6},{8,9},{9,8},{10,11... | collective-permute-start | bytes 2359304 | tf_op jit(solution)/shard_map/ppermute | solution.py:365
  71.7 0.1 collective-permute-start
  71.8 1.5 %shard_map.43.found_ref = f32[2,1024]{1,0:T(2,128)S(1)} custom-call(bf16[1024,768]{1,0:T(8,128)(2,1)S(1)} %bitcast.9), custom_call_target="tpu_custom_call" | custom-call | flops 805306368 | bytes 4000000 | tf_op jit(solution)/shard_map/pallas_call | solution.py:368
  73.3 0.5 collective-permute-start.2
  73.8 0.0 copy-done
  73.8 0.2 shard_map.46.index_ref
  73.9 0.0 collective-permute-done.1.more_ref
  73.9 1.0 %shard_map.44 = (f32[1,1024]{1,0:T(1,128)S(1)}, f32[512,128]{1,0:T(8,128)S(1)}) custom-call(bf16[1024,768]{1,0:T(8,128)(2,1)S(1)} %bitcast.10, bf16[512,768]{1,0:T(8,128)(2,1)S(1)} %collective-permute-done.1.more_ref, f32[2,1024]{1,0:T(2,128)S(1)} %shard_map.43.found_ref), custom_call_target="tpu_custom_call" | custom-call | flops 805306368 | bytes 4000000 | tf_op jit(solution)/shard_map/pallas_call | solution.py:371
  75.0 0.0 collective-permute-done.2.theirs_ref
  75.0 0.0 collective-permute-done.last_ref
  75.0 1.3 %shard_map.45 = f32[256,128]{1,0:T(8,128)S(1)} custom-call(bf16[1024,768]{1,0:T(8,128)(2,1)S(1)} %bitcast.11, bf16[512,768]{1,0:T(8,128)(2,1)S(1)} %collective-permute-done.last_ref, f32[1,1024]{1,0:T(1,128)S(1)} %get-tuple-element.14.so_far_ref, f32[2,1024]{1,0:T(2,128)S(1)} %shard_map.43.found_ref, f32[512,128]{1,0:T(8,128)S(1)} %get-tuple-element.15.more_rows_ref, ...), custom_call_target="tpu_custom_call" | custom-call | flops 805306368 | bytes 4000000 | tf_op jit(solution)/shard_map/pallas_call | solution.py:373
  76.3 18.1 %all_to_all.17 = f16[128,2,128]{2,1,0:T(2,128)(2,1)S(1)} all-to-all(f16[128,2,128]{2,1,0:T(2,128)(2,1)S(1)} %bitcast.15), channel_id=1, replica_groups=mesh['rows_0'=2,'rows_1'=4,'cols_0'=2,'cols_1'=8,'cols_2'=2] {'rows_1','..., dimensions={0} | all-to-all | bytes 131072 | tf_op jit(solution)/shard_map/all_to_all | solution.py:336
  94.4 0.8 shard_map.47
  (2 shorter events, 0.0 us)
Async XLA Ops:
  68.4 5.3 %copy-start = (s32[256]{0:T(256)S(1)}, s32[256]{0:T(256)}, u32[]{:S(2)}) copy-start(s32[256]{0:T(256)} %param.3) | copy-start | bytes 3076
  68.5 5.5 %collective-permute-start.1 = (bf16[512,768]{1,0:T(8,128)(2,1)S(1)}, bf16[512,768]{1,0:T(8,128)(2,1)S(1)}, u32[]{:S(2)}, u32[]{:S(2)}) collective-permute-start(bf16[512,768]{1,0:T(8,128)(2,1)S(1)} %get-tuple-element.22), channel_id=1, source_target_pairs={{0,1},{1,0},{2,3},{3,2},{4,5},{5,4},{6,7},{7,6},{8,9},{9,8},{10,11... | collective-permute-start | bytes 2359304 | tf_op jit(solution)/shard_map/ppermute | solution.py:365
  71.7 3.3 %collective-permute-start = (bf16[512,768]{1,0:T(8,128)(2,1)S(1)}, bf16[512,768]{1,0:T(8,128)(2,1)S(1)}, u32[]{:S(2)}, u32[]{:S(2)}) collective-permute-start(bf16[512,768]{1,0:T(8,128)(2,1)S(1)} %get-tuple-element.23), channel_id=1, source_target_pairs={{0,1},{1,0},{2,3},{3,2},{4,5},{5,4},{6,7},{7,6},{8,9},{9,8},{10,11... | collective-permute-start | bytes 2359304 | tf_op jit(solution)/shard_map/ppermute | solution.py:365
  73.3 1.7 %collective-permute-start.2 = (f32[2,1024]{1,0:T(2,128)S(1)}, f32[2,1024]{1,0:T(2,128)S(1)}, u32[]{:S(2)}, u32[]{:S(2)}) collective-permute-start(f32[2,1024]{1,0:T(2,128)S(1)} %shard_map.43.found_ref), channel_id=1, source_target_pairs={{0,1},{1,0},{2,3},{3,2},{4,5},{5,4},{6,7},{7,6},{8,9},{9,8},{10,11... | collective-permute-start | bytes 24584 | tf_op jit(solution)/shard_map/ppermute | solution.py:369

commit v11 on v10

--- a/solution.py
+++ b/solution.py
@@ -225,6 +225,31 @@
     within(own_ref, penalty, columns, rows)
     found_ref[0:1, :] = jnp.maximum(as_line(columns, rows), -1.0)
     found_ref[1:2, :] = penalty[1]
+
+
+def best_own_early(own_ref, found_ref):
+    early = lax.axis_index("cols_2") == 1
+
+    @pl.when(early)
+    def _():
+        best_own(own_ref, found_ref)
+
+    @pl.when(jnp.logical_not(early))
+    def _():
+        found_ref[...] = jnp.full(found_ref.shape, -1.0, F32)
+
+
+def best_own_late(own_ref, early_ref, labels_ref, rank_ref, got_ref, found_ref, index_ref):
+    early = lax.axis_index("cols_2") == 1
+    return_index(labels_ref, rank_ref, got_ref, index_ref)
+
+    @pl.when(early)
+    def _():
+        found_ref[...] = early_ref[...]
+
+    @pl.when(jnp.logical_not(early))
+    def _():
+        best_own(own_ref, found_ref)
 
 
 def best_more(own_ref, more_ref, found_ref, best_ref, rows_ref):
@@ -360,20 +385,21 @@
     )
     own = exchange(sends.reshape(GROUP_CLUSTERS, CAP, width), CHIPS)
     own, got = lax.optimization_barrier((own.reshape(total, width), got))
+    flops = 2 * total * total // 2 * width
+    early = call(best_own_early, shape((2, total), F32), [VMEM], flops)(own)
+    own, early = lax.optimization_barrier((own, early))
     pairs = [(i, i ^ 1) for i in range(col_count)]
     half = total // 2
     other = [lax.ppermute(own[s : s + half], COLS, pairs) for s in (0, half)]
-    flops = 2 * total * half * width
     lines = row_count * GROUP_CLUSTERS * 2
-    found = call(best_own, shape((2, total), F32), [VMEM], flops)(own)
+    outs = (shape((2, total), F32), shape((1, docs), jnp.int32))
+    found, index = call(best_own_late, outs, [VMEM] * 5, flops)(own, early, labels, rank, got)
     theirs = lax.ppermute(found, COLS, pairs)
     parts = (shape((1, total), F32), shape((half, LANES), F32))
     best, more_rows = call(best_more, parts, [VMEM] * 3, flops)(own, other[0], found)
-    index = call(return_index, shape((1, docs), jnp.int32), [VMEM] * 3, 2**26)(labels, rank, got)
     results = call(best_last, shape((lines, LANES), F32), [VMEM] * 6, flops)(
         own, other[1], best, found, more_rows, theirs
     )
-    results, index = lax.optimization_barrier((results, index))
     results = exchange(results.astype(WIRE).reshape(lines // 2, 2, LANES), SAME_CORE)
     results = results.reshape(lines, LANES).astype(F32)
     best, hist = call(

time: 95.5 us -> 95.5 us (level)
    ppermute x2, starting transfers between devices: 3.32 us -> 1.82 us  [shards(): other = [lax.ppermute(own[s:s + half], COLS, pairs) for s in (0, half)]]
    ppermute x1, starting transfers between devices: 0.5 us -> 1.97 us  [shards(): theirs = lax.ppermute(found, COLS, pairs)]
  transfers between devices with their start and end apart: 3 -> 3, of which waited for: 0 -> 0; matrix products, arithmetic and copies ran while one was open for 0% -> 0% of each run, Pallas kernels for 3% -> 1%
where the time goes in v11:
time: 95.5 us; the launch traced here: 95.3 us
  blocking collectives  82.9 us (87%)
  Pallas kernels  7.7 us (8%)
  starting transfers between devices  3.8 us (4%)
    all_to_all x3, blocking collectives, exchange(): return lax.all_to_all(x, axes, split_axis=0, concat_axis=0, tiled=True)  82.9 us
    ppermute x1, starting transfers between devices, shards(): theirs = lax.ppermute(found, COLS, pairs)  1.97 us
  transfers between devices with their start and end apart: 3, of which 0 were waited for; matrix products, arithmetic and copies ran while one was open for 0% of the time, Pallas kernels for 1%

profile of v11, /device:TPU:1, one launch (start us, length us, event | category | flops | bytes accessed | tf_op | source)
XLA Modules:
  0.0 95.3 jit_solution(5243446015753128029)
XLA Ops:
  0.6 1.6 %shard_map.41 = (bf16[8,392,128]{2,1,0:T(8,128)(2,1)S(1)}, f32[1,256]{1,0:T(1,128)S(1)}) custom-call(s32[1,256]{1,0:T(1,128)} %bitcast.14, bf16[256,768]{1,0:T(8,128)(2,1)} %embeddings_hbm.1), custom_call_target="tpu_custom_call" | custom-call | flops 201326592 | bytes 4000000 | tf_op jit(solution)/shard_map/pallas_call | solution.py:370
  2.3 21.2 %all_to_all.15.got_ref = bf16[8,392,128]{2,1,0:T(8,128)(2,1)S(1)} all-to-all(bf16[8,392,128]{2,1,0:T(8,128)(2,1)S(1)} %get-tuple-element.14), channel_id=1, replica_groups=mesh['rows_0'=2,'rows_1'=4,'cols_0'=2,'cols_1'=8,'cols_2'=2] {'rows_1','..., dimensions={0} | all-to-all | bytes 1605632 | tf_op jit(solution)/shard_map/all_to_all | solution.py:361
  23.5 1.3 %shard_map.42 = bf16[1024,768]{1,0:T(8,128)(2,1)S(1)} custom-call(bf16[8,392,128]{2,1,0:T(8,128)(2,1)S(1)} %all_to_all.15.got_ref), custom_call_target="tpu_custom_call" | custom-call | flops 805306368 | bytes 4000000 | tf_op jit(solution)/shard_map/pallas_call | solution.py:383
  24.7 43.6 %all_to_all.16 = bf16[16,64,768]{2,1,0:T(8,128)(2,1)S(1)} all-to-all(bf16[16,64,768]{2,1,0:T(8,128)(2,1)S(1)} %bitcast.13), channel_id=1, replica_groups=mesh['rows_0'=2,'rows_1'=4,'cols_0'=2,'cols_1'=8,'cols_2'=2] {'cols_0','..., dimensions={0} | all-to-all | bytes 3145728 | tf_op jit(solution)/shard_map/all_to_all | solution.py:361
  68.3 1.5 %shard_map.43.early_ref = f32[2,1024]{1,0:T(2,128)S(1)} custom-call(bf16[1024,768]{1,0:T(8,128)(2,1)S(1)} %bitcast.8), custom_call_target="tpu_custom_call" | custom-call | flops 805306368 | bytes 4000000 | tf_op jit(solution)/shard_map/pallas_call | solution.py:389
  69.8 0.0 copy-start
  69.8 0.1 fusion
  69.9 1.7 %collective-permute-start.1 = (bf16[512,768]{1,0:T(8,128)(2,1)S(1)}, bf16[512,768]{1,0:T(8,128)(2,1)S(1)}, u32[]{:S(2)}, u32[]{:S(2)}) collective-permute-start(bf16[512,768]{1,0:T(8,128)(2,1)S(1)} %get-tuple-element.26), channel_id=1, source_target_pairs={{0,1},{1,0},{2,3},{3,2},{4,5},{5,4},{6,7},{7,6},{8,9},{9,8},{10,11... | collective-permute-start | bytes 2359304 | tf_op jit(solution)/shard_map/ppermute | solution.py:393
  71.7 0.1 collective-permute-start
  71.8 0.0 copy-done
  71.8 0.2 shard_map.44
  71.9 2.0 %collective-permute-start.2 = (f32[2,1024]{1,0:T(2,128)S(1)}, f32[2,1024]{1,0:T(2,128)S(1)}, u32[]{:S(2)}, u32[]{:S(2)}) collective-permute-start(f32[2,1024]{1,0:T(2,128)S(1)} %get-tuple-element.21.found_ref), channel_id=1, source_target_pairs={{0,1},{1,0},{2,3},{3,2},{4,5},{5,4},{6,7},{7,6},{8,9},{9,8},{10,11... | collective-permute-start | bytes 24584 | tf_op jit(solution)/shard_map/ppermute | solution.py:397
  73.9 0.0 collective-permute-done.1.more_ref
  73.9 1.0 %shard_map.45 = (f32[1,1024]{1,0:T(1,128)S(1)}, f32[512,128]{1,0:T(8,128)S(1)}) custom-call(bf16[1024,768]{1,0:T(8,128)(2,1)S(1)} %bitcast.11, bf16[512,768]{1,0:T(8,128)(2,1)S(1)} %collective-permute-done.1.more_ref, f32[2,1024]{1,0:T(2,128)S(1)} %get-tuple-element.21.found_ref), custom_call_target="tpu_custom_call" | custom-call | flops 805306368 | bytes 4000000 | tf_op jit(solution)/shard_map/pallas_call | solution.py:399
  75.0 0.0 collective-permute-done.2.theirs_ref
  75.0 0.0 collective-permute-done.last_ref
  75.0 1.3 %shard_map.46 = f32[256,128]{1,0:T(8,128)S(1)} custom-call(bf16[1024,768]{1,0:T(8,128)(2,1)S(1)} %bitcast.12, bf16[512,768]{1,0:T(8,128)(2,1)S(1)} %collective-permute-done.last_ref, f32[1,1024]{1,0:T(1,128)S(1)} %get-tuple-element.22.so_far_ref, f32[2,1024]{1,0:T(2,128)S(1)} %get-tuple-element.21.found_ref, f32[512,128]{1,0:T(8,128)S(1)} %get-tuple-element.23.more_rows_ref, ...), custom_call_target="tpu_custom_call" | custom-call | flops 805306368 | bytes 4000000 | tf_op jit(solution)/shard_map/pallas_call | solution.py:400
  76.3 18.1 %all_to_all.17 = f16[128,2,128]{2,1,0:T(2,128)(2,1)S(1)} all-to-all(f16[128,2,128]{2,1,0:T(2,128)(2,1)S(1)} %bitcast.16), channel_id=1, replica_groups=mesh['rows_0'=2,'rows_1'=4,'cols_0'=2,'cols_1'=8,'cols_2'=2] {'rows_1','..., dimensions={0} | all-to-all | bytes 131072 | tf_op jit(solution)/shard_map/all_to_all | solution.py:361
  94.4 0.8 shard_map.47
  (2 shorter events, 0.0 us)
Async XLA Ops:
  69.8 1.9 %copy-start = (s32[256]{0:T(256)S(1)}, s32[256]{0:T(256)}, u32[]{:S(2)}) copy-start(s32[256]{0:T(256)} %param.3) | copy-start | bytes 3076
  69.9 4.0 %collective-permute-start.1 = (bf16[512,768]{1,0:T(8,128)(2,1)S(1)}, bf16[512,768]{1,0:T(8,128)(2,1)S(1)}, u32[]{:S(2)}, u32[]{:S(2)}) collective-permute-start(bf16[512,768]{1,0:T(8,128)(2,1)S(1)} %get-tuple-element.26), channel_id=1, source_target_pairs={{0,1},{1,0},{2,3},{3,2},{4,5},{5,4},{6,7},{7,6},{8,9},{9,8},{10,11... | collective-permute-start | bytes 2359304 | tf_op jit(solution)/shard_map/ppermute | solution.py:393
  71.7 3.3 %collective-permute-start = (bf16[512,768]{1,0:T(8,128)(2,1)S(1)}, bf16[512,768]{1,0:T(8,128)(2,1)S(1)}, u32[]{:S(2)}, u32[]{:S(2)}) collective-permute-start(bf16[512,768]{1,0:T(8,128)(2,1)S(1)} %get-tuple-element.27), channel_id=1, source_target_pairs={{0,1},{1,0},{2,3},{3,2},{4,5},{5,4},{6,7},{7,6},{8,9},{9,8},{10,11... | collective-permute-start | bytes 2359304 | tf_op jit(solution)/shard_map/ppermute | solution.py:393
  71.9 3.0 %collective-permute-start.2 = (f32[2,1024]{1,0:T(2,128)S(1)}, f32[2,1024]{1,0:T(2,128)S(1)}, u32[]{:S(2)}, u32[]{:S(2)}) collective-permute-start(f32[2,1024]{1,0:T(2,128)S(1)} %get-tuple-element.21.found_ref), channel_id=1, source_target_pairs={{0,1},{1,0},{2,3},{3,2},{4,5},{5,4},{6,7},{7,6},{8,9},{9,8},{10,11... | collective-permute-start | bytes 24584 | tf_op jit(solution)/shard_map/ppermute | solution.py:397

commit v12 on v10

--- a/solution.py
+++ b/solution.py
@@ -219,20 +219,25 @@
     return [None] * (ref.shape[0] // BLOCK)
 
 
-def best_own(own_ref, found_ref):
+def best_own(own_ref, labels_ref, rank_ref, got_ref, found_ref, index_ref):
+    return_index(labels_ref, rank_ref, got_ref, index_ref)
     columns, rows = nothing(own_ref), nothing(own_ref)
     penalty = penalties(own_ref)
     within(own_ref, penalty, columns, rows)
-    found_ref[0:1, :] = jnp.maximum(as_line(columns, rows), -1.0)
-    found_ref[1:2, :] = penalty[1]
+    best = jnp.maximum(as_line(columns, rows), -1.0)
+    found_ref[...] = jnp.where(penalty[1] < 0.0, -8.0, best)
+
+
+def penalty_of(found):
+    return jnp.where(found < -4.0, -4.0, 0.0)
 
 
 def best_more(own_ref, more_ref, found_ref, best_ref, rows_ref):
     rows, of_own = nothing(more_ref), nothing(own_ref)
     penalty = (column_of(more_ref), None)
-    between(more_ref, penalty, own_ref, (None, found_ref[1:2, :]), rows, of_own)
+    between(more_ref, penalty, own_ref, (None, penalty_of(found_ref[...])), rows, of_own)
     rows_ref[...] = jnp.concatenate(rows, axis=0)
-    best_ref[...] = jnp.maximum(as_line(of_own, nothing(own_ref)), found_ref[0:1, :])
+    best_ref[...] = jnp.maximum(as_line(of_own, nothing(own_ref)), found_ref[...])
 
 
 def histogram_parts(best, penalty):
@@ -250,17 +255,17 @@
     own_ref, last_ref, so_far_ref, found_ref, more_rows_ref, theirs_ref, out_ref
 ):
     total = own_ref.shape[0]
-    own_penalty = (None, found_ref[1:2, :])
+    own_penalty = (None, penalty_of(found_ref[...]))
     rows, of_own = nothing(last_ref), nothing(own_ref)
     starts = range(0, more_rows_ref.shape[0], BLOCK)
     more_rows = [more_rows_ref[s : s + BLOCK, :] for s in starts]
     between(last_ref, (column_of(last_ref), None), own_ref, own_penalty, rows, of_own)
     best = jnp.maximum(as_line(of_own, nothing(own_ref)), so_far_ref[...])
     rows = more_rows + rows
-    their_line = [theirs_ref[0:1, s : s + BLOCK] for s in range(0, total, BLOCK)]
+    their_line = [theirs_ref[:, s : s + BLOCK] for s in range(0, total, BLOCK)]
     their_best = as_line(their_line, rows)
     mine = histogram_parts(best, own_penalty[1])
-    theirs = histogram_parts(their_best, theirs_ref[1:2, :])
+    theirs = histogram_parts(their_best, penalty_of(theirs_ref[...]))
     hist = jnp.sum((mine + theirs).T, axis=0, keepdims=True)
     high = best.astype(BF16).astype(F32)
     low = (best - high) * LOW_SCALE
@@ -365,15 +370,14 @@
     other = [lax.ppermute(own[s : s + half], COLS, pairs) for s in (0, half)]
     flops = 2 * total * half * width
     lines = row_count * GROUP_CLUSTERS * 2
-    found = call(best_own, shape((2, total), F32), [VMEM], flops)(own)
+    outs = (shape((1, total), F32), shape((1, docs), jnp.int32))
+    found, index = call(best_own, outs, [VMEM] * 4, flops)(own, labels, rank, got)
     theirs = lax.ppermute(found, COLS, pairs)
     parts = (shape((1, total), F32), shape((half, LANES), F32))
     best, more_rows = call(best_more, parts, [VMEM] * 3, flops)(own, other[0], found)
-    index = call(return_index, shape((1, docs), jnp.int32), [VMEM] * 3, 2**26)(labels, rank, got)
     results = call(best_last, shape((lines, LANES), F32), [VMEM] * 6, flops)(
         own, other[1], best, found, more_rows, theirs
     )
-    results, index = lax.optimization_barrier((results, index))
     results = exchange(results.astype(WIRE).reshape(lines // 2, 2, LANES), SAME_CORE)
     results = results.reshape(lines, LANES).astype(F32)
     best, hist = call(

time: 95.5 us -> 95.3 us (level)
  no operation moved by 1% of the time
where the time goes in v12:
time: 95.3 us; the launch traced here: 95.1 us
  blocking collectives  82.9 us (87%)
  Pallas kernels  7.53 us (8%)
  starting transfers between devices  3.82 us (4%)
    all_to_all x3, blocking collectives, exchange(): return lax.all_to_all(x, axes, split_axis=0, concat_axis=0, tiled=True)  82.9 us
    ppermute x2, starting transfers between devices, shards(): other = [lax.ppermute(own[s:s + half], COLS, pairs) for s in (0, half)]  3.32 us
  transfers between devices with their start and end apart: 3, of which 0 were waited for; matrix products, arithmetic and copies ran while one was open for 0% of the time, Pallas kernels for 3%

profile of v12, /device:TPU:1, one launch (start us, length us, event | category | flops | bytes accessed | tf_op | source)
XLA Modules:
  0.0 95.1 jit_solution(16585321490801939890)
XLA Ops:
  0.6 1.6 %shard_map.41 = (bf16[8,392,128]{2,1,0:T(8,128)(2,1)S(1)}, f32[1,256]{1,0:T(1,128)S(1)}) custom-call(s32[1,256]{1,0:T(1,128)} %bitcast.13, bf16[256,768]{1,0:T(8,128)(2,1)} %embeddings_hbm.1), custom_call_target="tpu_custom_call" | custom-call | flops 201326592 | bytes 4000000 | tf_op jit(solution)/shard_map/pallas_call | solution.py:350
  2.3 21.2 %all_to_all.15.got_ref = bf16[8,392,128]{2,1,0:T(8,128)(2,1)S(1)} all-to-all(bf16[8,392,128]{2,1,0:T(8,128)(2,1)S(1)} %get-tuple-element.12), channel_id=1, replica_groups=mesh['rows_0'=2,'rows_1'=4,'cols_0'=2,'cols_1'=8,'cols_2'=2] {'rows_1','..., dimensions={0} | all-to-all | bytes 1605632 | tf_op jit(solution)/shard_map/all_to_all | solution.py:341
  23.5 1.3 %shard_map.42 = bf16[1024,768]{1,0:T(8,128)(2,1)S(1)} custom-call(bf16[8,392,128]{2,1,0:T(8,128)(2,1)S(1)} %all_to_all.15.got_ref), custom_call_target="tpu_custom_call" | custom-call | flops 805306368 | bytes 4000000 | tf_op jit(solution)/shard_map/pallas_call | solution.py:363
  24.7 43.6 %all_to_all.16 = bf16[16,64,768]{2,1,0:T(8,128)(2,1)S(1)} all-to-all(bf16[16,64,768]{2,1,0:T(8,128)(2,1)S(1)} %bitcast.12), channel_id=1, replica_groups=mesh['rows_0'=2,'rows_1'=4,'cols_0'=2,'cols_1'=8,'cols_2'=2] {'cols_0','..., dimensions={0} | all-to-all | bytes 3145728 | tf_op jit(solution)/shard_map/all_to_all | solution.py:341
  68.3 0.0 copy-start
  68.3 0.1 fusion
  68.4 3.2 %collective-permute-start.1 = (bf16[512,768]{1,0:T(8,128)(2,1)S(1)}, bf16[512,768]{1,0:T(8,128)(2,1)S(1)}, u32[]{:S(2)}, u32[]{:S(2)}) collective-permute-start(bf16[512,768]{1,0:T(8,128)(2,1)S(1)} %get-tuple-element.22), channel_id=1, source_target_pairs={{0,1},{1,0},{2,3},{3,2},{4,5},{5,4},{6,7},{7,6},{8,9},{9,8},{10,11... | collective-permute-start | bytes 2359304 | tf_op jit(solution)/shard_map/ppermute | solution.py:370
  71.7 0.1 collective-permute-start
  71.8 0.0 copy-done
  71.8 1.5 %shard_map.43 = (f32[1,1024]{1,0:T(1,128)S(1)}, s32[1,256]{1,0:T(1,128)S(1)}) custom-call(bf16[1024,768]{1,0:T(8,128)(2,1)S(1)} %bitcast.9, s32[1,256]{1,0:T(1,128)S(1)} %bitcast.14, f32[1,256]{1,0:T(1,128)S(1)} %get-tuple-element.14.rank_ref, bf16[8,392,128]{2,1,0:T(8,128)(2,1)S(1)} %all_to_all.15.got_ref), custom_call_target="tpu_custom_call" | custom-call | flops 805306368 | bytes 4000000 | tf_op jit(solution)/shard_map/pallas_call | solution.py:374
  73.2 0.5 collective-permute-start.2
  73.7 0.0 collective-permute-done.1.more_ref
  73.7 1.0 %shard_map.44 = (f32[1,1024]{1,0:T(1,128)S(1)}, f32[512,128]{1,0:T(8,128)S(1)}) custom-call(bf16[1024,768]{1,0:T(8,128)(2,1)S(1)} %bitcast.10, bf16[512,768]{1,0:T(8,128)(2,1)S(1)} %collective-permute-done.1.more_ref, f32[1,1024]{1,0:T(1,128)S(1)} %get-tuple-element.17.found_ref), custom_call_target="tpu_custom_call" | custom-call | flops 805306368 | bytes 4000000 | tf_op jit(solution)/shard_map/pallas_call | solution.py:377
  74.8 0.0 collective-permute-done.2.theirs_ref
  74.8 0.0 collective-permute-done.last_ref
  74.8 1.3 %shard_map.45 = f32[256,128]{1,0:T(8,128)S(1)} custom-call(bf16[1024,768]{1,0:T(8,128)(2,1)S(1)} %bitcast.11, bf16[512,768]{1,0:T(8,128)(2,1)S(1)} %collective-permute-done.last_ref, f32[1,1024]{1,0:T(1,128)S(1)} %get-tuple-element.18.so_far_ref, f32[1,1024]{1,0:T(1,128)S(1)} %get-tuple-element.17.found_ref, f32[512,128]{1,0:T(8,128)S(1)} %get-tuple-element.19.more_rows_ref, ...), custom_call_target="tpu_custom_call" | custom-call | flops 805306368 | bytes 4000000 | tf_op jit(solution)/shard_map/pallas_call | solution.py:378
  76.1 18.1 %all_to_all.17 = f16[128,2,128]{2,1,0:T(2,128)(2,1)S(1)} all-to-all(f16[128,2,128]{2,1,0:T(2,128)(2,1)S(1)} %bitcast.15), channel_id=1, replica_groups=mesh['rows_0'=2,'rows_1'=4,'cols_0'=2,'cols_1'=8,'cols_2'=2] {'rows_1','..., dimensions={0} | all-to-all | bytes 131072 | tf_op jit(solution)/shard_map/all_to_all | solution.py:341
  94.3 0.8 shard_map.46
  (2 shorter events, 0.0 us)
Async XLA Ops:
  68.3 3.4 %copy-start = (s32[256]{0:T(256)S(1)}, s32[256]{0:T(256)}, u32[]{:S(2)}) copy-start(s32[256]{0:T(256)} %param.3) | copy-start | bytes 3076
  68.4 5.3 %collective-permute-start.1 = (bf16[512,768]{1,0:T(8,128)(2,1)S(1)}, bf16[512,768]{1,0:T(8,128)(2,1)S(1)}, u32[]{:S(2)}, u32[]{:S(2)}) collective-permute-start(bf16[512,768]{1,0:T(8,128)(2,1)S(1)} %get-tuple-element.22), channel_id=1, source_target_pairs={{0,1},{1,0},{2,3},{3,2},{4,5},{5,4},{6,7},{7,6},{8,9},{9,8},{10,11... | collective-permute-start | bytes 2359304 | tf_op jit(solution)/shard_map/ppermute | solution.py:370
  71.7 3.1 %collective-permute-start = (bf16[512,768]{1,0:T(8,128)(2,1)S(1)}, bf16[512,768]{1,0:T(8,128)(2,1)S(1)}, u32[]{:S(2)}, u32[]{:S(2)}) collective-permute-start(bf16[512,768]{1,0:T(8,128)(2,1)S(1)} %get-tuple-element.23), channel_id=1, source_target_pairs={{0,1},{1,0},{2,3},{3,2},{4,5},{5,4},{6,7},{7,6},{8,9},{9,8},{10,11... | collective-permute-start | bytes 2359304 | tf_op jit(solution)/shard_map/ppermute | solution.py:370
  73.2 1.5 %collective-permute-start.2 = (f32[1,1024]{1,0:T(1,128)S(1)}, f32[1,1024]{1,0:T(1,128)S(1)}, u32[]{:S(2)}, u32[]{:S(2)}) collective-permute-start(f32[1,1024]{1,0:T(1,128)S(1)} %get-tuple-element.17.found_ref), channel_id=1, source_target_pairs={{0,1},{1,0},{2,3},{3,2},{4,5},{5,4},{6,7},{7,6},{8,9},{9,8},{10,11... | collective-permute-start | bytes 12296 | tf_op jit(solution)/shard_map/ppermute | solution.py:375

commit v13 on v10

--- a/solution.py
+++ b/solution.py
@@ -16,6 +16,7 @@
 SAME_CORE = ROWS + CHIPS
 LANES = 128
 BLOCK = 256
+PIECES = 4
 EMPTY = 2.0
 F32 = jnp.float32
 BF16 = jnp.bfloat16
@@ -52,9 +53,15 @@
 
 def normalise_and_slot(labels_hbm, embeddings_hbm, out_ref, rank_ref, labels_ref, embeddings_ref, sems):
     labels_copy = pltpu.make_async_copy(labels_hbm, labels_ref, sems.at[0])
-    embeddings_copy = pltpu.make_async_copy(embeddings_hbm, embeddings_ref, sems.at[1])
+    step = embeddings_ref.shape[0] // PIECES
+    pieces_of = [pl.ds(p * step, step) for p in range(PIECES)]
+    embeddings_copies = [
+        pltpu.make_async_copy(embeddings_hbm.at[at], embeddings_ref.at[at], sems.at[1 + p])
+        for p, at in enumerate(pieces_of)
+    ]
     labels_copy.start()
-    embeddings_copy.start()
+    for copy in embeddings_copies:
+        copy.start()
     docs, width = embeddings_ref.shape
     groups = out_ref.shape[0]
     clusters = groups * GROUP_CLUSTERS
@@ -74,10 +81,13 @@
         meta = jnp.where(row == s, slot_labels[:, s * LANES : (s + 1) * LANES], meta)
     meta = meta.astype(BF16)
     rank_ref[...] = rank_of(of_cluster, docs)
-    embeddings_copy.wait()
-    values = embeddings_ref[...].astype(F32)
-    total = jnp.sum(values * values, axis=1, keepdims=True)
-    normed = (values * lax.rsqrt(total + 1e-06)).astype(BF16)
+    normed = []
+    for copy, at in zip(embeddings_copies, pieces_of):
+        copy.wait()
+        values = embeddings_ref[at, :].astype(F32)
+        total = jnp.sum(values * values, axis=1, keepdims=True)
+        normed.append((values * lax.rsqrt(total + 1e-06)).astype(BF16))
+    normed = jnp.concatenate(normed, axis=0)
     rows = dot(places, normed).astype(BF16)
     pieces = width // LANES
     for g in range(groups):
@@ -350,7 +360,7 @@
         [
             pltpu.VMEM((1, docs), jnp.int32),
             pltpu.VMEM((docs, width), BF16),
-            pltpu.SemaphoreType.DMA((2,)),
+            pltpu.SemaphoreType.DMA((1 + PIECES,)),
         ],
     )(in_hbm(labels), in_hbm(embeddings))
     got = exchange(sends, ROWS)

time: 95.5 us -> 95.8 us (level)
  no operation moved by 1% of the time
where the time goes in v13:
time: 95.8 us; the launch traced here: 95.6 us
  blocking collectives  82.9 us (87%)
  Pallas kernels  7.99 us (8%)
  starting transfers between devices  3.8 us (4%)
    all_to_all x3, blocking collectives, exchange(): return lax.all_to_all(x, axes, split_axis=0, concat_axis=0, tiled=True)  82.9 us
    ppermute x2, starting transfers between devices, shards(): other = [lax.ppermute(own[s:s + half], COLS, pairs) for s in (0, half)]  3.31 us
    pallas_call x1, Pallas kernels, shards(): call(normalise_and_slot, (shape((row_count, block, LANES), BF16), shape((...  1.94 us
  transfers between devices with their start and end apart: 3, of which 0 were waited for; matrix products, arithmetic and copies ran while one was open for 0% of the time, Pallas kernels for 3%

profile of v13, /device:TPU:1, one launch (start us, length us, event | category | flops | bytes accessed | tf_op | source)
XLA Modules:
  0.0 95.6 jit_solution(8010829289584578070)
XLA Ops:
  0.6 1.9 %shard_map.41 = (bf16[8,392,128]{2,1,0:T(8,128)(2,1)S(1)}, f32[1,256]{1,0:T(1,128)S(1)}) custom-call(s32[1,256]{1,0:T(1,128)} %bitcast.13, bf16[256,768]{1,0:T(8,128)(2,1)} %embeddings_hbm.1), custom_call_target="tpu_custom_call" | custom-call | flops 201326592 | bytes 4000000 | tf_op jit(solution)/shard_map/pallas_call | solution.py:355
  2.6 21.2 %all_to_all.15.got_ref = bf16[8,392,128]{2,1,0:T(8,128)(2,1)S(1)} all-to-all(bf16[8,392,128]{2,1,0:T(8,128)(2,1)S(1)} %get-tuple-element.12), channel_id=1, replica_groups=mesh['rows_0'=2,'rows_1'=4,'cols_0'=2,'cols_1'=8,'cols_2'=2] {'rows_1','..., dimensions={0} | all-to-all | bytes 1605632 | tf_op jit(solution)/shard_map/all_to_all | solution.py:346
  23.8 1.3 %shard_map.42 = bf16[1024,768]{1,0:T(8,128)(2,1)S(1)} custom-call(bf16[8,392,128]{2,1,0:T(8,128)(2,1)S(1)} %all_to_all.15.got_ref), custom_call_target="tpu_custom_call" | custom-call | flops 805306368 | bytes 4000000 | tf_op jit(solution)/shard_map/pallas_call | solution.py:368
  25.0 43.6 %all_to_all.16 = bf16[16,64,768]{2,1,0:T(8,128)(2,1)S(1)} all-to-all(bf16[16,64,768]{2,1,0:T(8,128)(2,1)S(1)} %bitcast.12), channel_id=1, replica_groups=mesh['rows_0'=2,'rows_1'=4,'cols_0'=2,'cols_1'=8,'cols_2'=2] {'cols_0','..., dimensions={0} | all-to-all | bytes 3145728 | tf_op jit(solution)/shard_map/all_to_all | solution.py:346
  68.6 0.1 fusion
  68.7 0.0 copy-start
  68.8 3.2 %collective-permute-start.1 = (bf16[512,768]{1,0:T(8,128)(2,1)S(1)}, bf16[512,768]{1,0:T(8,128)(2,1)S(1)}, u32[]{:S(2)}, u32[]{:S(2)}) collective-permute-start(bf16[512,768]{1,0:T(8,128)(2,1)S(1)} %get-tuple-element.22), channel_id=1, source_target_pairs={{0,1},{1,0},{2,3},{3,2},{4,5},{5,4},{6,7},{7,6},{8,9},{9,8},{10,11... | collective-permute-start | bytes 2359304 | tf_op jit(solution)/shard_map/ppermute | solution.py:375
  72.0 0.1 collective-permute-start
  72.1 1.5 %shard_map.43.found_ref = f32[2,1024]{1,0:T(2,128)S(1)} custom-call(bf16[1024,768]{1,0:T(8,128)(2,1)S(1)} %bitcast.9), custom_call_target="tpu_custom_call" | custom-call | flops 805306368 | bytes 4000000 | tf_op jit(solution)/shard_map/pallas_call | solution.py:378
  73.6 0.5 collective-permute-start.2
  74.0 0.0 copy-done
  74.0 0.2 shard_map.46.index_ref
  74.2 0.0 collective-permute-done.1.more_ref
  74.2 1.0 %shard_map.44 = (f32[1,1024]{1,0:T(1,128)S(1)}, f32[512,128]{1,0:T(8,128)S(1)}) custom-call(bf16[1024,768]{1,0:T(8,128)(2,1)S(1)} %bitcast.10, bf16[512,768]{1,0:T(8,128)(2,1)S(1)} %collective-permute-done.1.more_ref, f32[2,1024]{1,0:T(2,128)S(1)} %shard_map.43.found_ref), custom_call_target="tpu_custom_call" | custom-call | flops 805306368 | bytes 4000000 | tf_op jit(solution)/shard_map/pallas_call | solution.py:381
  75.3 0.0 collective-permute-done.2.theirs_ref
  75.3 0.0 collective-permute-done.last_ref
  75.3 1.3 %shard_map.45 = f32[256,128]{1,0:T(8,128)S(1)} custom-call(bf16[1024,768]{1,0:T(8,128)(2,1)S(1)} %bitcast.11, bf16[512,768]{1,0:T(8,128)(2,1)S(1)} %collective-permute-done.last_ref, f32[1,1024]{1,0:T(1,128)S(1)} %get-tuple-element.14.so_far_ref, f32[2,1024]{1,0:T(2,128)S(1)} %shard_map.43.found_ref, f32[512,128]{1,0:T(8,128)S(1)} %get-tuple-element.15.more_rows_ref, ...), custom_call_target="tpu_custom_call" | custom-call | flops 805306368 | bytes 4000000 | tf_op jit(solution)/shard_map/pallas_call | solution.py:383
  76.6 18.1 %all_to_all.17 = f16[128,2,128]{2,1,0:T(2,128)(2,1)S(1)} all-to-all(f16[128,2,128]{2,1,0:T(2,128)(2,1)S(1)} %bitcast.15), channel_id=1, replica_groups=mesh['rows_0'=2,'rows_1'=4,'cols_0'=2,'cols_1'=8,'cols_2'=2] {'rows_1','..., dimensions={0} | all-to-all | bytes 131072 | tf_op jit(solution)/shard_map/all_to_all | solution.py:346
  94.7 0.8 shard_map.47
  (2 shorter events, 0.0 us)
Async XLA Ops:
  68.7 5.3 %copy-start = (s32[256]{0:T(256)S(1)}, s32[256]{0:T(256)}, u32[]{:S(2)}) copy-start(s32[256]{0:T(256)} %param.3) | copy-start | bytes 3076
  68.8 5.4 %collective-permute-start.1 = (bf16[512,768]{1,0:T(8,128)(2,1)S(1)}, bf16[512,768]{1,0:T(8,128)(2,1)S(1)}, u32[]{:S(2)}, u32[]{:S(2)}) collective-permute-start(bf16[512,768]{1,0:T(8,128)(2,1)S(1)} %get-tuple-element.22), channel_id=1, source_target_pairs={{0,1},{1,0},{2,3},{3,2},{4,5},{5,4},{6,7},{7,6},{8,9},{9,8},{10,11... | collective-permute-start | bytes 2359304 | tf_op jit(solution)/shard_map/ppermute | solution.py:375
  72.0 3.3 %collective-permute-start = (bf16[512,768]{1,0:T(8,128)(2,1)S(1)}, bf16[512,768]{1,0:T(8,128)(2,1)S(1)}, u32[]{:S(2)}, u32[]{:S(2)}) collective-permute-start(bf16[512,768]{1,0:T(8,128)(2,1)S(1)} %get-tuple-element.23), channel_id=1, source_target_pairs={{0,1},{1,0},{2,3},{3,2},{4,5},{5,4},{6,7},{7,6},{8,9},{9,8},{10,11... | collective-permute-start | bytes 2359304 | tf_op jit(solution)/shard_map/ppermute | solution.py:375
  73.6 1.7 %collective-permute-start.2 = (f32[2,1024]{1,0:T(2,128)S(1)}, f32[2,1024]{1,0:T(2,128)S(1)}, u32[]{:S(2)}, u32[]{:S(2)}) collective-permute-start(f32[2,1024]{1,0:T(2,128)S(1)} %shard_map.43.found_ref), channel_id=1, source_target_pairs={{0,1},{1,0},{2,3},{3,2},{4,5},{5,4},{6,7},{7,6},{8,9},{9,8},{10,11... | collective-permute-start | bytes 24584 | tf_op jit(solution)/shard_map/ppermute | solution.py:379

commit v14 on v10

--- a/solution.py
+++ b/solution.py
@@ -64,6 +64,10 @@
     onehot = ones_where(iota((groups, docs), 0) == group)
     slot = group * CAP + rank_of(onehot, docs).astype(jnp.int32)
     places = ones_where(iota((groups * CAP, docs), 0) == slot)
+    embeddings_copy.wait()
+    values = embeddings_ref[...].astype(F32)
+    total = jnp.sum(values * values, axis=1, keepdims=True)
+    normed = (values * lax.rsqrt(total + 1e-06)).astype(BF16)
     shifted = jnp.broadcast_to((labels + 1).astype(F32), (8, docs)).astype(BF16)
     slot_labels = dot_t(shifted, places)
     of_cluster = ones_where(iota((clusters, docs), 0) == labels)
@@ -74,10 +78,6 @@
         meta = jnp.where(row == s, slot_labels[:, s * LANES : (s + 1) * LANES], meta)
     meta = meta.astype(BF16)
     rank_ref[...] = rank_of(of_cluster, docs)
-    embeddings_copy.wait()
-    values = embeddings_ref[...].astype(F32)
-    total = jnp.sum(values * values, axis=1, keepdims=True)
-    normed = (values * lax.rsqrt(total + 1e-06)).astype(BF16)
     rows = dot(places, normed).astype(BF16)
     pieces = width // LANES
     for g in range(groups):

time: 95.5 us -> 95.4 us (level)
  no operation moved by 1% of the time
where the time goes in v14:
time: 95.4 us; the launch traced here: 95.2 us
  blocking collectives  82.9 us (87%)
  Pallas kernels  7.63 us (8%)
  starting transfers between devices  3.82 us (4%)
    all_to_all x3, blocking collectives, exchange(): return lax.all_to_all(x, axes, split_axis=0, concat_axis=0, tiled=True)  82.9 us
    ppermute x2, starting transfers between devices, shards(): other = [lax.ppermute(own[s:s + half], COLS, pairs) for s in (0, half)]  3.32 us
  transfers between devices with their start and end apart: 3, of which 0 were waited for; matrix products, arithmetic and copies ran while one was open for 0% of the time, Pallas kernels for 3%

profile of v14, /device:TPU:1, one launch (start us, length us, event | category | flops | bytes accessed | tf_op | source)
XLA Modules:
  0.0 95.2 jit_solution(7537792504623176326)
XLA Ops:
  0.6 1.6 %shard_map.41 = (bf16[8,392,128]{2,1,0:T(8,128)(2,1)S(1)}, f32[1,256]{1,0:T(1,128)S(1)}) custom-call(s32[1,256]{1,0:T(1,128)} %bitcast.13, bf16[256,768]{1,0:T(8,128)(2,1)} %embeddings_hbm.1), custom_call_target="tpu_custom_call" | custom-call | flops 201326592 | bytes 4000000 | tf_op jit(solution)/shard_map/pallas_call | solution.py:345
  2.2 21.2 %all_to_all.15.got_ref = bf16[8,392,128]{2,1,0:T(8,128)(2,1)S(1)} all-to-all(bf16[8,392,128]{2,1,0:T(8,128)(2,1)S(1)} %get-tuple-element.12), channel_id=1, replica_groups=mesh['rows_0'=2,'rows_1'=4,'cols_0'=2,'cols_1'=8,'cols_2'=2] {'rows_1','..., dimensions={0} | all-to-all | bytes 1605632 | tf_op jit(solution)/shard_map/all_to_all | solution.py:336
  23.4 1.3 %shard_map.42 = bf16[1024,768]{1,0:T(8,128)(2,1)S(1)} custom-call(bf16[8,392,128]{2,1,0:T(8,128)(2,1)S(1)} %all_to_all.15.got_ref), custom_call_target="tpu_custom_call" | custom-call | flops 805306368 | bytes 4000000 | tf_op jit(solution)/shard_map/pallas_call | solution.py:358
  24.7 43.6 %all_to_all.16 = bf16[16,64,768]{2,1,0:T(8,128)(2,1)S(1)} all-to-all(bf16[16,64,768]{2,1,0:T(8,128)(2,1)S(1)} %bitcast.12), channel_id=1, replica_groups=mesh['rows_0'=2,'rows_1'=4,'cols_0'=2,'cols_1'=8,'cols_2'=2] {'cols_0','..., dimensions={0} | all-to-all | bytes 3145728 | tf_op jit(solution)/shard_map/all_to_all | solution.py:336
  68.3 0.1 fusion
  68.4 0.0 copy-start
  68.4 3.2 %collective-permute-start.1 = (bf16[512,768]{1,0:T(8,128)(2,1)S(1)}, bf16[512,768]{1,0:T(8,128)(2,1)S(1)}, u32[]{:S(2)}, u32[]{:S(2)}) collective-permute-start(bf16[512,768]{1,0:T(8,128)(2,1)S(1)} %get-tuple-element.22), channel_id=1, source_target_pairs={{0,1},{1,0},{2,3},{3,2},{4,5},{5,4},{6,7},{7,6},{8,9},{9,8},{10,11... | collective-permute-start | bytes 2359304 | tf_op jit(solution)/shard_map/ppermute | solution.py:365
  71.6 0.1 collective-permute-start
  71.7 1.5 %shard_map.43.found_ref = f32[2,1024]{1,0:T(2,128)S(1)} custom-call(bf16[1024,768]{1,0:T(8,128)(2,1)S(1)} %bitcast.9), custom_call_target="tpu_custom_call" | custom-call | flops 805306368 | bytes 4000000 | tf_op jit(solution)/shard_map/pallas_call | solution.py:368
  73.2 0.5 collective-permute-start.2
  73.7 0.0 copy-done
  73.7 0.2 shard_map.46.index_ref
  73.8 0.0 collective-permute-done.1.more_ref
  73.8 1.0 %shard_map.44 = (f32[1,1024]{1,0:T(1,128)S(1)}, f32[512,128]{1,0:T(8,128)S(1)}) custom-call(bf16[1024,768]{1,0:T(8,128)(2,1)S(1)} %bitcast.10, bf16[512,768]{1,0:T(8,128)(2,1)S(1)} %collective-permute-done.1.more_ref, f32[2,1024]{1,0:T(2,128)S(1)} %shard_map.43.found_ref), custom_call_target="tpu_custom_call" | custom-call | flops 805306368 | bytes 4000000 | tf_op jit(solution)/shard_map/pallas_call | solution.py:371
  74.9 0.0 collective-permute-done.2.theirs_ref
  74.9 0.0 collective-permute-done.last_ref
  74.9 1.3 %shard_map.45 = f32[256,128]{1,0:T(8,128)S(1)} custom-call(bf16[1024,768]{1,0:T(8,128)(2,1)S(1)} %bitcast.11, bf16[512,768]{1,0:T(8,128)(2,1)S(1)} %collective-permute-done.last_ref, f32[1,1024]{1,0:T(1,128)S(1)} %get-tuple-element.14.so_far_ref, f32[2,1024]{1,0:T(2,128)S(1)} %shard_map.43.found_ref, f32[512,128]{1,0:T(8,128)S(1)} %get-tuple-element.15.more_rows_ref, ...), custom_call_target="tpu_custom_call" | custom-call | flops 805306368 | bytes 4000000 | tf_op jit(solution)/shard_map/pallas_call | solution.py:373
  76.3 18.1 %all_to_all.17 = f16[128,2,128]{2,1,0:T(2,128)(2,1)S(1)} all-to-all(f16[128,2,128]{2,1,0:T(2,128)(2,1)S(1)} %bitcast.15), channel_id=1, replica_groups=mesh['rows_0'=2,'rows_1'=4,'cols_0'=2,'cols_1'=8,'cols_2'=2] {'rows_1','..., dimensions={0} | all-to-all | bytes 131072 | tf_op jit(solution)/shard_map/all_to_all | solution.py:336
  94.4 0.8 shard_map.47
  (2 shorter events, 0.0 us)
Async XLA Ops:
  68.4 5.3 %copy-start = (s32[256]{0:T(256)S(1)}, s32[256]{0:T(256)}, u32[]{:S(2)}) copy-start(s32[256]{0:T(256)} %param.3) | copy-start | bytes 3076
  68.4 5.5 %collective-permute-start.1 = (bf16[512,768]{1,0:T(8,128)(2,1)S(1)}, bf16[512,768]{1,0:T(8,128)(2,1)S(1)}, u32[]{:S(2)}, u32[]{:S(2)}) collective-permute-start(bf16[512,768]{1,0:T(8,128)(2,1)S(1)} %get-tuple-element.22), channel_id=1, source_target_pairs={{0,1},{1,0},{2,3},{3,2},{4,5},{5,4},{6,7},{7,6},{8,9},{9,8},{10,11... | collective-permute-start | bytes 2359304 | tf_op jit(solution)/shard_map/ppermute | solution.py:365
  71.6 3.3 %collective-permute-start = (bf16[512,768]{1,0:T(8,128)(2,1)S(1)}, bf16[512,768]{1,0:T(8,128)(2,1)S(1)}, u32[]{:S(2)}, u32[]{:S(2)}) collective-permute-start(bf16[512,768]{1,0:T(8,128)(2,1)S(1)} %get-tuple-element.23), channel_id=1, source_target_pairs={{0,1},{1,0},{2,3},{3,2},{4,5},{5,4},{6,7},{7,6},{8,9},{9,8},{10,11... | collective-permute-start | bytes 2359304 | tf_op jit(solution)/shard_map/ppermute | solution.py:365
  73.2 1.7 %collective-permute-start.2 = (f32[2,1024]{1,0:T(2,128)S(1)}, f32[2,1024]{1,0:T(2,128)S(1)}, u32[]{:S(2)}, u32[]{:S(2)}) collective-permute-start(f32[2,1024]{1,0:T(2,128)S(1)} %shard_map.43.found_ref), channel_id=1, source_target_pairs={{0,1},{1,0},{2,3},{3,2},{4,5},{5,4},{6,7},{7,6},{8,9},{9,8},{10,11... | collective-permute-start | bytes 24584 | tf_op jit(solution)/shard_map/ppermute | solution.py:369

commit v15 on v12

--- a/solution.py
+++ b/solution.py
@@ -64,6 +64,10 @@
     onehot = ones_where(iota((groups, docs), 0) == group)
     slot = group * CAP + rank_of(onehot, docs).astype(jnp.int32)
     places = ones_where(iota((groups * CAP, docs), 0) == slot)
+    embeddings_copy.wait()
+    values = embeddings_ref[...].astype(F32)
+    total = jnp.sum(values * values, axis=1, keepdims=True)
+    normed = (values * lax.rsqrt(total + 1e-06)).astype(BF16)
     shifted = jnp.broadcast_to((labels + 1).astype(F32), (8, docs)).astype(BF16)
     slot_labels = dot_t(shifted, places)
     of_cluster = ones_where(iota((clusters, docs), 0) == labels)
@@ -74,10 +78,6 @@
         meta = jnp.where(row == s, slot_labels[:, s * LANES : (s + 1) * LANES], meta)
     meta = meta.astype(BF16)
     rank_ref[...] = rank_of(of_cluster, docs)
-    embeddings_copy.wait()
-    values = embeddings_ref[...].astype(F32)
-    total = jnp.sum(values * values, axis=1, keepdims=True)
-    normed = (values * lax.rsqrt(total + 1e-06)).astype(BF16)
     rows = dot(places, normed).astype(BF16)
     pieces = width // LANES
     for g in range(groups):

time: 95.3 us -> 95.2 us (level)
  no operation moved by 1% of the time
where the time goes in v15:
time: 95.2 us; the launch traced here: 95 us
  blocking collectives  82.9 us (87%)
  Pallas kernels  7.47 us (8%)
  starting transfers between devices  3.82 us (4%)
    all_to_all x3, blocking collectives, exchange(): return lax.all_to_all(x, axes, split_axis=0, concat_axis=0, tiled=True)  82.9 us
    ppermute x2, starting transfers between devices, shards(): other = [lax.ppermute(own[s:s + half], COLS, pairs) for s in (0, half)]  3.32 us
  transfers between devices with their start and end apart: 3, of which 0 were waited for; matrix products, arithmetic and copies ran while one was open for 0% of the time, Pallas kernels for 3%

profile of v15, /device:TPU:1, one launch (start us, length us, event | category | flops | bytes accessed | tf_op | source)
XLA Modules:
  0.0 95.0 jit_solution(14185676596875611235)
XLA Ops:
  0.6 1.6 %shard_map.41 = (bf16[8,392,128]{2,1,0:T(8,128)(2,1)S(1)}, f32[1,256]{1,0:T(1,128)S(1)}) custom-call(s32[1,256]{1,0:T(1,128)} %bitcast.13, bf16[256,768]{1,0:T(8,128)(2,1)} %embeddings_hbm.1), custom_call_target="tpu_custom_call" | custom-call | flops 201326592 | bytes 4000000 | tf_op jit(solution)/shard_map/pallas_call | solution.py:350
  2.2 21.2 %all_to_all.15.got_ref = bf16[8,392,128]{2,1,0:T(8,128)(2,1)S(1)} all-to-all(bf16[8,392,128]{2,1,0:T(8,128)(2,1)S(1)} %get-tuple-element.12), channel_id=1, replica_groups=mesh['rows_0'=2,'rows_1'=4,'cols_0'=2,'cols_1'=8,'cols_2'=2] {'rows_1','..., dimensions={0} | all-to-all | bytes 1605632 | tf_op jit(solution)/shard_map/all_to_all | solution.py:341
  23.4 1.3 %shard_map.42 = bf16[1024,768]{1,0:T(8,128)(2,1)S(1)} custom-call(bf16[8,392,128]{2,1,0:T(8,128)(2,1)S(1)} %all_to_all.15.got_ref), custom_call_target="tpu_custom_call" | custom-call | flops 805306368 | bytes 4000000 | tf_op jit(solution)/shard_map/pallas_call | solution.py:363
  24.7 43.6 %all_to_all.16 = bf16[16,64,768]{2,1,0:T(8,128)(2,1)S(1)} all-to-all(bf16[16,64,768]{2,1,0:T(8,128)(2,1)S(1)} %bitcast.12), channel_id=1, replica_groups=mesh['rows_0'=2,'rows_1'=4,'cols_0'=2,'cols_1'=8,'cols_2'=2] {'cols_0','..., dimensions={0} | all-to-all | bytes 3145728 | tf_op jit(solution)/shard_map/all_to_all | solution.py:341
  68.3 0.0 copy-start
  68.3 0.1 fusion
  68.4 3.2 %collective-permute-start.1 = (bf16[512,768]{1,0:T(8,128)(2,1)S(1)}, bf16[512,768]{1,0:T(8,128)(2,1)S(1)}, u32[]{:S(2)}, u32[]{:S(2)}) collective-permute-start(bf16[512,768]{1,0:T(8,128)(2,1)S(1)} %get-tuple-element.22), channel_id=1, source_target_pairs={{0,1},{1,0},{2,3},{3,2},{4,5},{5,4},{6,7},{7,6},{8,9},{9,8},{10,11... | collective-permute-start | bytes 2359304 | tf_op jit(solution)/shard_map/ppermute | solution.py:370
  71.6 0.1 collective-permute-start
  71.7 0.0 copy-done
  71.7 1.5 %shard_map.43 = (f32[1,1024]{1,0:T(1,128)S(1)}, s32[1,256]{1,0:T(1,128)S(1)}) custom-call(bf16[1024,768]{1,0:T(8,128)(2,1)S(1)} %bitcast.9, s32[1,256]{1,0:T(1,128)S(1)} %bitcast.14, f32[1,256]{1,0:T(1,128)S(1)} %get-tuple-element.14.rank_ref, bf16[8,392,128]{2,1,0:T(8,128)(2,1)S(1)} %all_to_all.15.got_ref), custom_call_target="tpu_custom_call" | custom-call | flops 805306368 | bytes 4000000 | tf_op jit(solution)/shard_map/pallas_call | solution.py:374
  73.2 0.5 collective-permute-start.2
  73.7 0.0 collective-permute-done.1.more_ref
  73.7 1.0 %shard_map.44 = (f32[1,1024]{1,0:T(1,128)S(1)}, f32[512,128]{1,0:T(8,128)S(1)}) custom-call(bf16[1024,768]{1,0:T(8,128)(2,1)S(1)} %bitcast.10, bf16[512,768]{1,0:T(8,128)(2,1)S(1)} %collective-permute-done.1.more_ref, f32[1,1024]{1,0:T(1,128)S(1)} %get-tuple-element.17.found_ref), custom_call_target="tpu_custom_call" | custom-call | flops 805306368 | bytes 4000000 | tf_op jit(solution)/shard_map/pallas_call | solution.py:377
  74.7 0.0 collective-permute-done.2.theirs_ref
  74.7 0.0 collective-permute-done.last_ref
  74.7 1.3 %shard_map.45 = f32[256,128]{1,0:T(8,128)S(1)} custom-call(bf16[1024,768]{1,0:T(8,128)(2,1)S(1)} %bitcast.11, bf16[512,768]{1,0:T(8,128)(2,1)S(1)} %collective-permute-done.last_ref, f32[1,1024]{1,0:T(1,128)S(1)} %get-tuple-element.18.so_far_ref, f32[1,1024]{1,0:T(1,128)S(1)} %get-tuple-element.17.found_ref, f32[512,128]{1,0:T(8,128)S(1)} %get-tuple-element.19.more_rows_ref, ...), custom_call_target="tpu_custom_call" | custom-call | flops 805306368 | bytes 4000000 | tf_op jit(solution)/shard_map/pallas_call | solution.py:378
  76.1 18.1 %all_to_all.17 = f16[128,2,128]{2,1,0:T(2,128)(2,1)S(1)} all-to-all(f16[128,2,128]{2,1,0:T(2,128)(2,1)S(1)} %bitcast.15), channel_id=1, replica_groups=mesh['rows_0'=2,'rows_1'=4,'cols_0'=2,'cols_1'=8,'cols_2'=2] {'rows_1','..., dimensions={0} | all-to-all | bytes 131072 | tf_op jit(solution)/shard_map/all_to_all | solution.py:341
  94.2 0.8 shard_map.46
  (2 shorter events, 0.0 us)
Async XLA Ops:
  68.3 3.4 %copy-start = (s32[256]{0:T(256)S(1)}, s32[256]{0:T(256)}, u32[]{:S(2)}) copy-start(s32[256]{0:T(256)} %param.3) | copy-start | bytes 3076
  68.4 5.3 %collective-permute-start.1 = (bf16[512,768]{1,0:T(8,128)(2,1)S(1)}, bf16[512,768]{1,0:T(8,128)(2,1)S(1)}, u32[]{:S(2)}, u32[]{:S(2)}) collective-permute-start(bf16[512,768]{1,0:T(8,128)(2,1)S(1)} %get-tuple-element.22), channel_id=1, source_target_pairs={{0,1},{1,0},{2,3},{3,2},{4,5},{5,4},{6,7},{7,6},{8,9},{9,8},{10,11... | collective-permute-start | bytes 2359304 | tf_op jit(solution)/shard_map/ppermute | solution.py:370
  71.6 3.1 %collective-permute-start = (bf16[512,768]{1,0:T(8,128)(2,1)S(1)}, bf16[512,768]{1,0:T(8,128)(2,1)S(1)}, u32[]{:S(2)}, u32[]{:S(2)}) collective-permute-start(bf16[512,768]{1,0:T(8,128)(2,1)S(1)} %get-tuple-element.23), channel_id=1, source_target_pairs={{0,1},{1,0},{2,3},{3,2},{4,5},{5,4},{6,7},{7,6},{8,9},{9,8},{10,11... | collective-permute-start | bytes 2359304 | tf_op jit(solution)/shard_map/ppermute | solution.py:370
  73.2 1.5 %collective-permute-start.2 = (f32[1,1024]{1,0:T(1,128)S(1)}, f32[1,1024]{1,0:T(1,128)S(1)}, u32[]{:S(2)}, u32[]{:S(2)}) collective-permute-start(f32[1,1024]{1,0:T(1,128)S(1)} %get-tuple-element.17.found_ref), channel_id=1, source_target_pairs={{0,1},{1,0},{2,3},{3,2},{4,5},{5,4},{6,7},{7,6},{8,9},{9,8},{10,11... | collective-permute-start | bytes 12296 | tf_op jit(solution)/shard_map/ppermute | solution.py:375
